TPU v7x, 128 devices: a whole 4x4x4 slice. The times are simulated.
128 devices in a mesh: gx: 32 (over y, z, core), gy: 4 (over x).
Axes of the slice: x: 4, y: 4, z: 4, core: 2. Of those that a mesh axis runs over, the one named last changes fastest.
Arguments:
- velocity: bfloat16 [3, 64, 16, 16, 512], P(None, 'gx', 'gy'), may hold values from -6 to 6
- part_pos: float32 [16384, 3, 128], P(('gx', 'gy')), may hold values from -1 to 1
- part_vel: float32 [16384, 3, 128], P(('gx', 'gy')), may hold values from -6 to 6
- part_coef: float32 [16384, 2, 128], P(('gx', 'gy')), may hold values from 0.3 to 3
- counts: int32 [16384], P(('gx', 'gy')), may hold values from 1 to 128
- dest: int32 [16384], P(('gx', 'gy')), may hold values from 0 to 3, as said below
- elem: int32 [16384], P(('gx', 'gy')), may hold values from 0 to 127, as said below
Outputs:
- drag: float32 [16384, 3, 128], P(('gx', 'gy'))
- source: float32 [3, 64, 16, 16, 512], P(None, 'gx', 'gy')
Inputs may be any that keep to these rules, and one draw needn't show every extreme that they name: `dest`: every device sends exactly 32 blocks to each gy index. `elem`: on every owning device, each of its 128 elements receives exactly one block.
All inputs are finite; a program needn't handle non-finite values.
Results may differ from a plain program's by a relative error of at most 0.0003.
Values sent between devices are 32-bit elements; how exact they have to be, the bound alone decides.
No kernel may reach another device: no remote copies, remote signals or barrier semaphores. Data moves between devices by JAX's collectives and lax.ppermute only.
A program may use at most 128 MiB of HBM per device.

v0:
```python
import jax
import jax.numpy as jnp
import numpy as np
from jax import lax
from jax.experimental import pallas as pl
from jax.experimental.pallas import tpu as pltpu
from jax.sharding import PartitionSpec as P

GLL = (
    -1.0,
    -0.8717401485096066,
    -0.5917001814331423,
    -0.2092992179024789,
    0.2092992179024789,
    0.5917001814331423,
    0.8717401485096066,
    1.0,
)
SHARPNESS = 8.0
INTERPRET = False
F32 = jnp.float32
BF16 = jnp.bfloat16
VMEM = pltpu.VMEM
SMEM = pltpu.SMEM
N_GY = 4
SHARE = 32
ROWS = 264
PAIRED = (0, 2, 4, 6, 1, 3, 5, 7)


def node_table():
    q = np.array(GLL, np.float64)
    rows = []
    for order in (tuple(range(8)), PAIRED):
        for t in range(7):
            rows.append([q[[m for m in range(8) if m != i][t]] for i in order])
        rows.append([1.0 / np.prod([q[i] - q[m] for m in range(8) if m != i]) for i in order])
    rows.append([q[i] for i in range(8)])
    for shift in (-2.0, 0.0, 2.0):
        rows.append([q[i] + shift for i in PAIRED])
    table = np.array(rows, np.float32).reshape(-1, 1)
    return np.ascontiguousarray(np.broadcast_to(table, (table.shape[0], 128)))


NODE_ROWS = 8 * 20


def whole(space=VMEM):
    return pl.BlockSpec(memory_space=space)


def call(kernel, out_shape, out_specs, in_specs, scratch=()):
    return pl.pallas_call(
        kernel,
        out_shape=out_shape,
        in_specs=in_specs,
        out_specs=out_specs,
        scratch_shapes=scratch,
        interpret=INTERPRET,
    )


def lanes(shape=(1, 128)):
    return lax.broadcasted_iota(jnp.int32, shape, len(shape) - 1)


def pack_kernel(dest, counts, elem, pos, vel, coef, send, slot):
    lane = lanes()
    ids = lax.broadcasted_iota(jnp.int32, (8, 128), 0) * 128 + lanes((8, 128))

    def one(b, state):
        taken, labels = state
        d = dest[b]
        r = (taken >> (8 * d)) & 255
        slot[b] = d * 96 + r
        base = d * ROWS + r
        send[pl.ds(base, 3, stride=32), :] = pos[pl.ds(b, 3, stride=128), :]
        send[pl.ds(base + 96, 3, stride=32), :] = vel[pl.ds(b, 3, stride=128), :]
        rate = coef[pl.ds(2 * b, 1), :]
        send[pl.ds(base + 192, 1), :] = jnp.where(lane < counts[b], rate, 0.0)
        send[pl.ds(base + 224, 1), :] = coef[pl.ds(2 * b + 1, 1), :]
        labels = jnp.where(ids == d * 128 + r, elem[b], labels)
        return (taken + (1 << (8 * d)), labels)

    _, labels = lax.fori_loop(0, 128, one, (jnp.int32(0), jnp.zeros((8, 128), jnp.int32)), unroll=8)
    labels = labels.astype(F32)
    for d in range(N_GY):
        send[d * ROWS + 256 : d * ROWS + 264, :] = jnp.broadcast_to(labels[d : d + 1, :], (8, 128))


def split_two(x):
    high = x.astype(BF16)
    low = (x - high.astype(F32)).astype(BF16)
    return high, low


def lagrange(x, nodes, first):
    out = nodes[8 * (first + 7) : 8 * (first + 8), :]
    for t in range(7):
        out = out * (x - nodes[8 * (first + t) : 8 * (first + t + 1), :])
    return out


def gauss(x, nodes, row):
    d = nodes[8 * row : 8 * row + 8, :] - x
    return jnp.exp(d * d * (-SHARPNESS))


def outer(a, b):
    return jnp.concatenate([a[j : j + 1, :] * b for j in range(8)], axis=0)


def main_kernel(
    recv, vel, nodes, drag, inside, ghost_lo, ghost_hi, field, fluid, parts, lab_v, lab_s, sem
):
    low_half = lanes((1, 128)) < 64
    for s in range(N_GY):
        lab_v[s : s + 1, :] = recv[s * ROWS + 256 : s * ROWS + 257, :].astype(jnp.int32)
    copy = pltpu.make_async_copy(lab_v, lab_s, sem)
    copy.start()

    def spread_field(xy, _):
        for c in range(3):
            for h in range(4):
                t = vel[c * 8 + xy, :, 128 * h : 128 * h + 128].astype(F32)
                turned = pltpu.roll(t, 64, 1)
                at = xy * 384 + (c * 8 + h) * 16
                field[pl.ds(at, 16), :] = jnp.where(low_half, t, turned)
                field[pl.ds(at + 64, 16), :] = jnp.where(low_half, turned, t)
        return 0

    lax.fori_loop(0, 8, spread_field, 0)
    copy.wait()

    def interpolate(n, _):
        s = n // SHARE
        r = n % SHARE
        e = lab_s[s, r]
        xy = e // 16
        z = e % 16
        base = s * ROWS + r
        basis_r = lagrange(recv[pl.ds(base, 1), :], nodes, 8)
        basis_s = lagrange(recv[pl.ds(base + 32, 1), :], nodes, 0)
        basis_t = lagrange(recv[pl.ds(base + 64, 1), :], nodes, 0)
        high, low = split_two(outer(basis_s, basis_t))
        nodal = field[pl.ds(xy * 384 + z, 24, stride=16), :].astype(BF16)
        part = jnp.dot(nodal, jnp.concatenate([high, low], axis=0), preferred_element_type=F32)
        for c in range(3):
            fluid[pl.ds(s * 96 + c * 32 + r, 1), :] = jnp.sum(
                part[8 * c : 8 * c + 8, :] * basis_r, axis=0, keepdims=True
            )
        return 0

    lax.fori_loop(0, 128, interpolate, 0, unroll=8)

    for s in range(N_GY):
        w = [
            fluid[s * 96 + 32 * c : s * 96 + 32 * c + 32, :]
            - recv[s * ROWS + 96 + 32 * c : s * ROWS + 128 + 32 * c, :]
            for c in range(3)
        ]
        rate = recv[s * ROWS + 192 : s * ROWS + 224, :]
        scale = recv[s * ROWS + 224 : s * ROWS + 256, :]
        square = (w[0] * w[0] + w[1] * w[1] + w[2] * w[2]) * (scale * scale)
        power = jnp.where(square > 0.0, jnp.exp(0.3435 * jnp.log(square)), 0.0)
        factor = rate * (1.0 + 0.15 * power)
        for c in range(3):
            drag[s * 96 + 32 * c : s * 96 + 32 * c + 32, :] = factor * w[c]

    def project(n, _):
        s = n // SHARE
        r = n % SHARE
        e = lab_s[s, r]
        xy = e // 16
        z = e % 16
        base = s * ROWS + r
        x = recv[pl.ds(base, 1), :]
        weights = [gauss(x, nodes, 17 + k) for k in range(3)]
        planes = outer(
            gauss(recv[pl.ds(base + 32, 1), :], nodes, 16),
            gauss(recv[pl.ds(base + 64, 1), :], nodes, 16),
        )
        planes = jnp.concatenate(split_two(planes), axis=0)
        rows = []
        for c in range(3):
            force = -drag[pl.ds(s * 96 + c * 32 + r, 1), :]
            rows += [wr * force for wr in weights]
        rows = jnp.concatenate(split_two(jnp.concatenate(rows, axis=0)), axis=0)
        both = lax.dot_general(
            rows, planes, (((1,), (1,)), ((), ())), preferred_element_type=F32
        )
        both = both[:72, :] + both[72:, :]
        both = both + pltpu.roll(both, 64, 1)
        for k in range(9):
            t = both[8 * k : 8 * k + 8, :]
            t = jnp.where(low_half, t, pltpu.roll(t, 4, 0))
            parts[pl.ds(xy * 576 + k * 64 + z, 4, stride=16), :] = t[0:4, :]
        return 0

    lax.fori_loop(0, 128, project, 0, unroll=4)

    def part(x, y, c, k, h):
        return parts[pl.ds((x * 4 + y) * 576 + (c * 3 + k) * 64 + h * 16, 16), :]

    def gather_parts(y, _):
        for c in range(3):
            lower = []
            upper = []
            for h in range(4):
                lo = part(0, y, c, 1, h) + part(1, y, c, 0, h)
                hi = part(1, y, c, 1, h) + part(0, y, c, 2, h)
                inside[c * 8 + y, :, 128 * h : 128 * h + 128] = lo
                inside[c * 8 + 4 + y, :, 128 * h : 128 * h + 128] = hi
                lower.append(lo)
                upper.append(hi)
            for h in range(4):
                lo = part(0, y, c, 0, h)
                hi = part(1, y, c, 2, h)
                if h == 3:
                    lo = lo + jnp.where(low_half, 0.0, pltpu.roll(lower[0], 64, 1))
                if h == 0:
                    hi = hi + jnp.where(low_half, pltpu.roll(upper[3], 64, 1), 0.0)
                ghost_lo[c * 4 + y, :, 128 * h : 128 * h + 128] = lo
                ghost_hi[c * 4 + y, :, 128 * h : 128 * h + 128] = hi
        return 0

    lax.fori_loop(0, 4, gather_parts, 0)


def first_pass_kernel(ends, inside, sent_lo, sent_hi, got_lo, got_hi, field, face_lo, face_hi):
    low_half = lanes((1, 128)) < 64
    spot = (lanes((1, 128)) % 64) // 8
    has_before = ends[0] > 0
    has_after = ends[1] > 0

    def cut(ref, at, h):
        return ref[at, :, 128 * h : 128 * h + 128]

    for c in range(3):
        packed = [jnp.zeros((16, 128), F32), jnp.zeros((16, 128), F32)]
        for y in range(4):
            lower = [cut(inside, c * 8 + y, h) + cut(got_lo, c * 4 + y, h) for h in range(4)]
            upper = [cut(inside, c * 8 + 4 + y, h) + cut(got_hi, c * 4 + y, h) for h in range(4)]
            first = cut(got_lo, c * 4 + y, 0) + pltpu.roll(cut(sent_lo, c * 4 + y, 3), 64, 1)
            last = cut(got_hi, c * 4 + y, 3) + pltpu.roll(cut(sent_hi, c * 4 + y, 0), 64, 1)
            low3, up0 = lower[3], upper[0]
            lower[0] = jnp.where(low_half & has_before, first, lower[0])
            upper[3] = jnp.where(low_half | jnp.logical_not(has_after), upper[3], last)
            lower[3] = jnp.where(low_half, low3, low3 + pltpu.roll(up0, 64, 1))
            upper[0] = jnp.where(low_half, up0 + pltpu.roll(low3, 64, 1), up0)
            for x, layer in ((0, lower), (1, upper)):
                for h in range(4):
                    field[c * 8 + x * 4 + y, :, 128 * h : 128 * h + 128] = layer[h]
                    k = x * 4 + h
                    if y == 0:
                        moved = pltpu.roll(layer[h], 8 * k, 1) if k else layer[h]
                        packed[0] = jnp.where(spot == k, moved, packed[0])
                    if y == 3:
                        by = (8 * k - 56) % 128
                        moved = pltpu.roll(layer[h], by, 1) if by else layer[h]
                        packed[1] = jnp.where(spot == k, moved, packed[1])
        face_lo[16 * c : 16 * c + 16, :] = packed[0]
        face_hi[16 * c : 16 * c + 16, :] = packed[1]


def last_pass_kernel(field, got_lo, got_hi, ret, slot, out, drag):
    lane = lanes((1, 128))
    bottom = (lane % 64) < 8
    top = (lane % 64) >= 56
    z = lax.broadcasted_iota(jnp.int32, (16, 128), 0)
    lane16 = lanes((16, 128))
    up_here = (lane16 % 8 == 7) & (z < 15)
    down_here = (lane16 % 8 == 0) & (z > 0)

    def one_comp(c, _):
        lo_pack = got_lo[pl.ds(16 * c, 16), :]
        hi_pack = got_hi[pl.ds(16 * c, 16), :]
        for x in range(2):
            for h in range(4):
                k = x * 4 + h
                f = [field[c * 8 + x * 4 + y, :, 128 * h : 128 * h + 128] for y in range(4)]
                down = lo_pack if k == 0 else pltpu.roll(lo_pack, (128 - 8 * k) % 128, 1)
                up = hi_pack if k == 7 else pltpu.roll(hi_pack, 56 - 8 * k, 1)
                for y in range(4):
                    above = up if y == 3 else pltpu.roll(f[y + 1], 56, 1)
                    below = down if y == 0 else pltpu.roll(f[y - 1], 72, 1)
                    g = f[y] + jnp.where(top, above, jnp.where(bottom, below, 0.0))
                    above = pltpu.roll(pltpu.roll(g, 7, 1), 15, 0)
                    below = pltpu.roll(pltpu.roll(g, 121, 1), 1, 0)
                    g = g + jnp.where(up_here, above, jnp.where(down_here, below, 0.0))
                    out[c * 8 + x * 4 + y, :, 128 * h : 128 * h + 128] = g
        return 0

    lax.fori_loop(0, 3, one_comp, 0)

    def unpack(b, _):
        drag[pl.ds(b, 3, stride=128), :] = ret[pl.ds(slot[b], 3, stride=32), :]
        return 0

    lax.fori_loop(0, 128, unpack, 0, unroll=8)


def shifted(shard, axis, by):
    count = lax.axis_size(axis)
    pairs = [(i, i + by) for i in range(count) if 0 <= i + by < count]
    return lax.ppermute(shard, axis, pairs)


def sds(*shape, dtype=F32):
    return jax.ShapeDtypeStruct(shape, dtype)


def body(velocity, part_pos, part_vel, part_coef, counts, dest, elem):
    pos = part_pos.transpose(1, 0, 2).reshape(384, 128)
    vel = part_vel.transpose(1, 0, 2).reshape(384, 128)
    coef = part_coef.reshape(256, 128)
    nodes = jnp.asarray(node_table())
    send, slot = call(
        pack_kernel,
        (sds(N_GY * ROWS, 128), sds(128, dtype=jnp.int32)),
        (whole(), whole(SMEM)),
        [whole(SMEM)] * 3 + [whole()] * 3,
    )(dest, counts, elem, pos, vel, coef)
    recv = lax.all_to_all(
        send.reshape(N_GY, ROWS, 128), "gy", split_axis=0, concat_axis=0, tiled=True
    ).reshape(N_GY * ROWS, 128)
    drag_e, inside, ghost_lo, ghost_hi = call(
        main_kernel,
        (sds(384, 128), sds(24, 16, 512), sds(12, 16, 512), sds(12, 16, 512)),
        (whole(),) * 4,
        [whole()] * 3,
        (
            VMEM((8 * 384, 128), F32),
            VMEM((384, 128), F32),
            VMEM((8 * 576, 128), F32),
            VMEM((8, 128), jnp.int32),
            SMEM((8, 128), jnp.int32),
            pltpu.SemaphoreType.DMA,
        ),
    )(recv, velocity.reshape(24, 16, 512), nodes)
    got_hi = shifted(ghost_lo, "gx", -1)
    got_lo = shifted(ghost_hi, "gx", 1)
    ret = lax.all_to_all(
        drag_e.reshape(N_GY, 96, 128), "gy", split_axis=0, concat_axis=0, tiled=True
    ).reshape(384, 128)
    at = lax.axis_index("gx")
    ends = jnp.stack([at, lax.axis_size("gx") - 1 - at]).astype(jnp.int32)
    field, face_lo, face_hi = call(
        first_pass_kernel,
        (sds(24, 16, 512), sds(48, 128), sds(48, 128)),
        (whole(),) * 3,
        [whole(SMEM)] + [whole()] * 5,
    )(ends, inside, ghost_lo, ghost_hi, got_lo, got_hi)
    face_after = shifted(face_lo, "gy", -1)
    face_before = shifted(face_hi, "gy", 1)
    out, drag = call(
        last_pass_kernel,
        (sds(24, 16, 512), sds(384, 128)),
        (whole(), whole()),
        [whole()] * 4 + [whole(SMEM)],
    )(field, face_before, face_after, ret, slot)
    return (
        drag.reshape(3, 128, 128).transpose(1, 0, 2),
        out.reshape(velocity.shape),
    )


def solution(mesh):
    in_specs = (
        P(None, "gx", "gy", None, None),
        P(("gx", "gy"), None, None),
        P(("gx", "gy"), None, None),
        P(("gx", "gy"), None, None),
        P(("gx", "gy")),
        P(("gx", "gy")),
        P(("gx", "gy")),
    )
    out_specs = (P(("gx", "gy"), None, None), P(None, "gx", "gy", None, None))
    return jax.shard_map(body, mesh=mesh, in_specs=in_specs, out_specs=out_specs, check_vma=False)
```

profile of v0, /device:TPU:24, one launch (start us, length us, event | category | flops | bytes accessed | tf_op | source)
XLA Modules:
  0.0 71.1 jit_solution(12484006820069844247)
XLA Ops:
  0.6 3.0 %shard_map.95 = (f32[1056,128]{1,0:T(8,128)}, s32[128]{0:T(128)}) custom-call(s32[128]{0:T(128)} %dest.1, s32[128]{0:T(128)} %counts.1, s32[128]{0:T(128)} %elem.1, f32[384,128]{1,0:T(8,128)} %bitcast.22, f32[384,128]{1,0:T(8,128)} %bitcast.23, f32[256,128]{1,0:T(8,128)} %bitcast.25), custom_call_target="tpu_custom_call" | custom-call | tf_op jit(solution)/shard_map/pallas_call | solution.py:318
  3.6 14.2 %all_to_all.10 = f32[4,264,128]{2,1,0:T(8,128)} all-to-all(f32[4,264,128]{2,1,0:T(8,128)} %bitcast.20), channel_id=1, replica_groups=mesh['gx'=32,'gy'=4] {'gy'}, dimensions={0} | all-to-all | bytes 1081344 | tf_op jit(solution)/shard_map/all_to_all | solution.py:324
  17.8 18.4 %shard_map.96 = (f32[384,128]{1,0:T(8,128)}, f32[24,16,512]{2,1,0:T(8,128)}, f32[12,16,512]{2,1,0:T(8,128)}, f32[12,16,512]{2,1,0:T(8,128)}) custom-call(f32[1056,128]{1,0:T(8,128)} %bitcast.18, bf16[24,16,512]{2,1,0:T(8,128)(2,1)} %bitcast.21, f32[160,128]{1,0:T(8,128)} %constant.10.clone.nodes), custom_call_target="tpu_custom_call" | custom-call | tf_op jit(solution)/shard_map/pallas_call | solution.py:327
  36.2 4.2 %collective-permute-start.1 = (f32[12,16,512]{2,1,0:T(8,128)}, f32[12,16,512]{2,1,0:T(8,128)S(1)}, u32[]{:S(2)}, u32[]{:S(2)}) collective-permute-start(f32[12,16,512]{2,1,0:T(8,128)} %get-tuple-element.15.sent_lo), channel_id=1, source_target_pairs={{4,0},{8,4},{12,8},{16,12},{20,16},{24,20},{28,24},{32,28},{36,32}... | collective-permute-start | bytes 1179656 | tf_op jit(solution)/shard_map/ppermute | solution.py:306
  40.5 1.9 %collective-permute-start = (f32[12,16,512]{2,1,0:T(8,128)}, f32[12,16,512]{2,1,0:T(8,128)S(1)}, u32[]{:S(2)}, u32[]{:S(2)}) collective-permute-start(f32[12,16,512]{2,1,0:T(8,128)} %get-tuple-element.16.sent_hi), channel_id=1, source_target_pairs={{0,4},{4,8},{8,12},{12,16},{16,20},{20,24},{24,28},{28,32},{32,36}... | collective-permute-start | bytes 1179656 | tf_op jit(solution)/shard_map/ppermute | solution.py:306
  42.4 3.4 %all-to-all-start.1 = ((f32[4,96,128]{2,1,0:T(8,128)}), f32[4,96,128]{2,1,0:T(8,128)S(1)}, u32[]{:S(2)}, u32[]{:S(2)}) async-start(f32[4,96,128]{2,1,0:T(8,128)} %bitcast.24), calls=%async_computation.1 | async-start | bytes 393216 | tf_op jit(solution)/shard_map/all_to_all | solution.py:343
  45.8 0.7 pad_add_fusion.ends
  46.4 0.0 collective-permute-done.1.got_hi
  46.4 0.0 copy-start.1
  46.4 5.4 %collective-permute-done.got_lo = f32[12,16,512]{2,1,0:T(8,128)S(1)} collective-permute-done((f32[12,16,512]{2,1,0:T(8,128)}, f32[12,16,512]{2,1,0:T(8,128)S(1)}, u32[]{:S(2)}, u32[]{:S(2)}) %collective-permute-start) | collective-permute-done | bytes 393248 | tf_op jit(solution)/shard_map/ppermute | solution.py:306
  51.9 0.0 copy-start.2
  51.9 0.0 copy-done.1
  51.9 0.7 %copy-done.2 = f32[12,16,512]{2,1,0:T(8,128)} copy-done((f32[12,16,512]{2,1,0:T(8,128)}, f32[12,16,512]{2,1,0:T(8,128)S(1)}, u32[]{:S(2)}) %copy-start.2) | copy-done | bytes 393240
  52.6 2.9 %shard_map.97 = (f32[24,16,512]{2,1,0:T(8,128)}, f32[48,128]{1,0:T(8,128)}, f32[48,128]{1,0:T(8,128)}) custom-call(s32[2]{0:T(128)} %pad_add_fusion.ends, f32[24,16,512]{2,1,0:T(8,128)} %get-tuple-element.14.inside, f32[12,16,512]{2,1,0:T(8,128)} %get-tuple-element.15.sent_lo, f32[12,16,512]{2,1,0:T(8,128)} %get-tuple-element.16.sent_hi, ...), custom_call_target="tpu_custom_call" | custom-call | tf_op jit(solution)/shard_map/pallas_call | solution.py:348
  55.5 2.5 %collective-permute-start.2 = (f32[48,128]{1,0:T(8,128)}, f32[48,128]{1,0:T(8,128)S(1)}, u32[]{:S(2)}, u32[]{:S(2)}) collective-permute-start(f32[48,128]{1,0:T(8,128)} %get-tuple-element.18), channel_id=1, source_target_pairs={{0,1},{1,2},{2,3},{4,5},{5,6},{6,7},{8,9},{9,10},{10,11},{12,13},{... | collective-permute-start | bytes 73736 | tf_op jit(solution)/shard_map/ppermute | solution.py:306
  58.0 1.3 %collective-permute-start.3 = (f32[48,128]{1,0:T(8,128)}, f32[48,128]{1,0:T(8,128)S(1)}, u32[]{:S(2)}, u32[]{:S(2)}) collective-permute-start(f32[48,128]{1,0:T(8,128)} %get-tuple-element.19), channel_id=1, source_target_pairs={{1,0},{2,1},{3,2},{5,4},{6,5},{7,6},{9,8},{10,9},{11,10},{13,12},{... | collective-permute-start | bytes 73736 | tf_op jit(solution)/shard_map/ppermute | solution.py:306
  59.3 0.0 all-to-all-done.1
  59.3 0.0 copy-start
  59.3 0.4 collective-permute-done.2.got_lo
  59.7 0.0 copy-start.3
  59.7 4.2 %collective-permute-done.3.got_hi = f32[48,128]{1,0:T(8,128)S(1)} collective-permute-done((f32[48,128]{1,0:T(8,128)}, f32[48,128]{1,0:T(8,128)S(1)}, u32[]{:S(2)}, u32[]{:S(2)}) %collective-permute-start.3) | collective-permute-done | bytes 24608 | tf_op jit(solution)/shard_map/ppermute | solution.py:306
  63.9 0.0 copy-start.4
  63.9 0.0 copy-done
  63.9 0.0 copy-done.3
  64.0 0.6 copy-done.4
  64.6 6.6 %shard_map.98 = (f32[24,16,512]{2,1,0:T(8,128)}, f32[384,128]{1,0:T(8,128)}) custom-call(f32[24,16,512]{2,1,0:T(8,128)} %get-tuple-element.17.field, f32[48,128]{1,0:T(8,128)} %copy-done.3, f32[48,128]{1,0:T(8,128)} %copy-done.4, f32[384,128]{1,0:T(8,128)} %bitcast.19, s32[128]{0:T(128)} %get-tuple-element.21.slot), custom_call_target="tpu_custom_call" | custom-call | tf_op jit(solution)/shard_map/pallas_call | solution.py:356
Async XLA Ops:
  36.2 10.2 %collective-permute-start.1 = (f32[12,16,512]{2,1,0:T(8,128)}, f32[12,16,512]{2,1,0:T(8,128)S(1)}, u32[]{:S(2)}, u32[]{:S(2)}) collective-permute-start(f32[12,16,512]{2,1,0:T(8,128)} %get-tuple-element.15.sent_lo), channel_id=1, source_target_pairs={{4,0},{8,4},{12,8},{16,12},{20,16},{24,20},{28,24},{32,28},{36,32}... | collective-permute-start | bytes 1179656 | tf_op jit(solution)/shard_map/ppermute | solution.py:306
  40.5 11.4 %collective-permute-start = (f32[12,16,512]{2,1,0:T(8,128)}, f32[12,16,512]{2,1,0:T(8,128)S(1)}, u32[]{:S(2)}, u32[]{:S(2)}) collective-permute-start(f32[12,16,512]{2,1,0:T(8,128)} %get-tuple-element.16.sent_hi), channel_id=1, source_target_pairs={{0,4},{4,8},{8,12},{12,16},{16,20},{20,24},{24,28},{28,32},{32,36}... | collective-permute-start | bytes 1179656 | tf_op jit(solution)/shard_map/ppermute | solution.py:306
  42.4 16.9 %all-to-all-start.1 = ((f32[4,96,128]{2,1,0:T(8,128)}), f32[4,96,128]{2,1,0:T(8,128)S(1)}, u32[]{:S(2)}, u32[]{:S(2)}) async-start(f32[4,96,128]{2,1,0:T(8,128)} %bitcast.24), calls=%async_computation.1 | async-start | bytes 393216 | tf_op jit(solution)/shard_map/all_to_all | solution.py:343
  46.4 5.4 %copy-start.1 = (f32[12,16,512]{2,1,0:T(8,128)}, f32[12,16,512]{2,1,0:T(8,128)S(1)}, u32[]{:S(2)}) copy-start(f32[12,16,512]{2,1,0:T(8,128)S(1)} %collective-permute-done.1.got_hi) | copy-start | bytes 1179652
  51.9 0.7 %copy-start.2 = (f32[12,16,512]{2,1,0:T(8,128)}, f32[12,16,512]{2,1,0:T(8,128)S(1)}, u32[]{:S(2)}) copy-start(f32[12,16,512]{2,1,0:T(8,128)S(1)} %collective-permute-done.got_lo) | copy-start | bytes 1179652
  55.5 4.2 %collective-permute-start.2 = (f32[48,128]{1,0:T(8,128)}, f32[48,128]{1,0:T(8,128)S(1)}, u32[]{:S(2)}, u32[]{:S(2)}) collective-permute-start(f32[48,128]{1,0:T(8,128)} %get-tuple-element.18), channel_id=1, source_target_pairs={{0,1},{1,2},{2,3},{4,5},{5,6},{6,7},{8,9},{9,10},{10,11},{12,13},{... | collective-permute-start | bytes 73736 | tf_op jit(solution)/shard_map/ppermute | solution.py:306
  58.0 5.9 %collective-permute-start.3 = (f32[48,128]{1,0:T(8,128)}, f32[48,128]{1,0:T(8,128)S(1)}, u32[]{:S(2)}, u32[]{:S(2)}) collective-permute-start(f32[48,128]{1,0:T(8,128)} %get-tuple-element.19), channel_id=1, source_target_pairs={{1,0},{2,1},{3,2},{5,4},{6,5},{7,6},{9,8},{10,9},{11,10},{13,12},{... | collective-permute-start | bytes 73736 | tf_op jit(solution)/shard_map/ppermute | solution.py:306
  59.3 4.6 %copy-start = (f32[4,96,128]{2,1,0:T(8,128)}, f32[4,96,128]{2,1,0:T(8,128)S(1)}, u32[]{:S(2)}) copy-start(f32[4,96,128]{2,1,0:T(8,128)S(1)} %all-to-all-done.1) | copy-start | bytes 589828
  59.7 4.2 %copy-start.3 = (f32[48,128]{1,0:T(8,128)}, f32[48,128]{1,0:T(8,128)S(1)}, u32[]{:S(2)}) copy-start(f32[48,128]{1,0:T(8,128)S(1)} %collective-permute-done.2.got_lo) | copy-start | bytes 73732
  63.9 0.6 copy-start.4
where the time goes:
time: 71.5 us; the launch traced here: 71.1 us
  Pallas kernels  30.9 us (43%)
  blocking collectives  14.2 us (20%)
  starting transfers between devices  13.3 us (19%)
  waiting for transfers between devices  10 us (14%)
  local copies, waits for them, and re-layouts  1.36 us (2%)
  between operations  0.72 us (1%)
    pallas_call x1, Pallas kernels, body(): call(main_kernel, (sds(384, 128), sds(24, 16, 512), sds(12, 16, 512), sds...  18.4 us
    all_to_all x1, blocking collectives, body(): lax.all_to_all(send.reshape(N_GY, ROWS, 128), 'gy', split_axis=0, concat_...  14.2 us
    ppermute x4, waiting for transfers between devices, shifted(): return lax.ppermute(shard, axis, pairs)  10 us
    ppermute x4, starting transfers between devices, shifted(): return lax.ppermute(shard, axis, pairs)  9.91 us
    pallas_call x1, Pallas kernels, body(): call(last_pass_kernel, (sds(24, 16, 512), sds(384, 128)), (whole(), whole...  6.56 us
    all_to_all x1, starting transfers between devices, body(): lax.all_to_all(drag_e.reshape(N_GY, 96, 128), 'gy', split_axis=0, concat_...  3.38 us
    pallas_call x1, Pallas kernels, body(): call(pack_kernel, (sds(N_GY * ROWS, 128), sds(128, dtype=jnp.int32)), (wh...  2.96 us
    pallas_call x1, Pallas kernels, body(): call(first_pass_kernel, (sds(24, 16, 512), sds(48, 128), sds(48, 128)), (...  2.93 us
  transfers between devices with their start and end apart: 5, of which 3 were waited for; matrix products, arithmetic and copies ran while one was open for 1% of the time, Pallas kernels for 4%

commit v1 on v0

v1 whole, which is shorter than its diff:
```python
import jax
import jax.numpy as jnp
import numpy as np
from jax import lax
from jax.experimental import pallas as pl
from jax.experimental.pallas import tpu as pltpu
from jax.sharding import PartitionSpec as P

GLL = (
    -1.0,
    -0.8717401485096066,
    -0.5917001814331423,
    -0.2092992179024789,
    0.2092992179024789,
    0.5917001814331423,
    0.8717401485096066,
    1.0,
)
SHARPNESS = 8.0
INTERPRET = False
F32 = jnp.float32
BF16 = jnp.bfloat16
VMEM = pltpu.VMEM
SMEM = pltpu.SMEM
N_GY = 4
SHARE = 32
ROWS = 264
PAIRED = (0, 2, 4, 6, 1, 3, 5, 7)


def node_table():
    q = np.array(GLL, np.float64)
    rows = []
    for order in (tuple(range(8)), PAIRED):
        for t in range(7):
            rows.append([q[[m for m in range(8) if m != i][t]] for i in order])
        rows.append([1.0 / np.prod([q[i] - q[m] for m in range(8) if m != i]) for i in order])
    rows.append([q[i] for i in range(8)])
    for shift in (-2.0, 0.0, 2.0):
        rows.append([q[i] + shift for i in PAIRED])
    table = np.array(rows, np.float32).reshape(-1, 1)
    return np.ascontiguousarray(np.broadcast_to(table, (table.shape[0], 128)))


UNROLL_A = 16
UNROLL_B = 8
OWN_FLOPS = 2_000_000_000
UNPACK_FLOPS = 1_000_000_000


def call(kernel, outs, ins, scratch=(), flops=0, aliases=None):
    args = [
        a
        if INTERPRET
        else pltpu.with_memory_space_constraint(a, VMEM if m == "vmem" else pltpu.HBM)
        if m in ("vmem", "hbm", "table")
        else a
        for a, m in ins
    ]
    shapes = [
        VMEM(shape, dtype) if m == "vmem" and not INTERPRET else jax.ShapeDtypeStruct(shape, dtype)
        for shape, dtype, m in outs
    ]
    return pl.pallas_call(
        kernel,
        out_shape=shapes,
        in_specs=[pl.BlockSpec(memory_space=SMEM if m in ("smem", "table") else VMEM) for _, m in ins],
        out_specs=[pl.BlockSpec(memory_space=SMEM if m == "smem" else VMEM) for _, _, m in outs],
        scratch_shapes=scratch,
        interpret=INTERPRET,
        input_output_aliases=aliases or {},
        compiler_params=pltpu.CompilerParams(vmem_limit_bytes=24 * 1024 * 1024),
        cost_estimate=pl.CostEstimate(flops=flops, bytes_accessed=0, transcendentals=0),
    )(*args)


def lanes(shape=(1, 128)):
    return lax.broadcasted_iota(jnp.int32, shape, len(shape) - 1)


def pack_kernel(dest, counts, elem, pos, vel, coef, send, block, own_elem):
    me = lax.axis_index("gy")
    lane = lanes()
    ids = lax.broadcasted_iota(jnp.int32, (8, 128), 0) * 128 + lanes((8, 128))

    def one(b, state):
        taken, labels = state
        d = dest[b] ^ me
        r = (taken >> (8 * d)) & 255
        block[d * SHARE + r] = b
        base = d * ROWS + r
        send[pl.ds(base, 3, stride=32), :] = pos[pl.ds(b, 3, stride=128), :]
        send[pl.ds(base + 96, 3, stride=32), :] = vel[pl.ds(b, 3, stride=128), :]
        rate = coef[pl.ds(2 * b, 1), :]
        send[pl.ds(base + 192, 1), :] = jnp.where(lane < counts[b], rate, 0.0)
        send[pl.ds(base + 224, 1), :] = coef[pl.ds(2 * b + 1, 1), :]
        own_elem[d * SHARE + r] = elem[b]
        labels = jnp.where(ids == d * 128 + r, elem[b], labels)
        return (taken + (1 << (8 * d)), labels)

    _, labels = lax.fori_loop(0, 128, one, (jnp.int32(0), jnp.zeros((8, 128), jnp.int32)), unroll=8)
    labels = labels.astype(F32)
    for d in range(N_GY):
        send[d * ROWS + 256 : d * ROWS + 264, :] = jnp.broadcast_to(labels[d : d + 1, :], (8, 128))


def split_two(x):
    high = x.astype(BF16)
    low = (x - high.astype(F32)).astype(BF16)
    return high, low


def lagrange(x, nodes, first):
    out = nodes[8 * (first + 7) : 8 * (first + 8), :]
    for t in range(7):
        out = out * (x - nodes[8 * (first + t) : 8 * (first + t + 1), :])
    return out


def gauss(x, nodes, row):
    d = nodes[8 * row : 8 * row + 8, :] - x
    return jnp.exp(d * d * (-SHARPNESS))


def outer(a, b):
    return jnp.concatenate([a[j : j + 1, :] * b for j in range(8)], axis=0)


def spread_field(vel, field):
    low_half = lanes() < 64

    def one(xy, _):
        for c in range(3):
            for h in range(4):
                t = vel[c * 8 + xy, :, 128 * h : 128 * h + 128].astype(F32)
                turned = pltpu.roll(t, 64, 1)
                at = xy * 384 + (c * 8 + h) * 16
                field[pl.ds(at, 16), :] = jnp.where(low_half, t, turned)
                field[pl.ds(at + 64, 16), :] = jnp.where(low_half, turned, t)
        return 0

    lax.fori_loop(0, 8, one, 0)


def interpolate(group, element, field, nodes, fluid):
    def one(r, _):
        e = element(r)
        basis_r = lagrange(group[pl.ds(r, 1), :], nodes, 8)
        basis_s = lagrange(group[pl.ds(r + 32, 1), :], nodes, 0)
        basis_t = lagrange(group[pl.ds(r + 64, 1), :], nodes, 0)
        high, low = split_two(outer(basis_s, basis_t))
        nodal = field[pl.ds((e >> 4) * 384 + (e & 15), 24, stride=16), :].astype(BF16)
        part = jnp.dot(nodal, jnp.concatenate([high, low], axis=0), preferred_element_type=F32)
        for c in range(3):
            fluid[pl.ds(c * 32 + r, 1), :] = jnp.sum(
                part[8 * c : 8 * c + 8, :] * basis_r, axis=0, keepdims=True
            )
        return 0

    lax.fori_loop(0, SHARE, one, 0, unroll=UNROLL_A)


def find_drag(group, fluid, drag):
    w = [
        fluid[32 * c : 32 * c + 32, :] - group[96 + 32 * c : 128 + 32 * c, :] for c in range(3)
    ]
    scale = group[224:256, :]
    square = (w[0] * w[0] + w[1] * w[1] + w[2] * w[2]) * (scale * scale)
    power = jnp.where(square > 0.0, jnp.exp(0.3435 * jnp.log(square)), 0.0)
    factor = group[192:224, :] * (1.0 + 0.15 * power)
    for c in range(3):
        drag[32 * c : 32 * c + 32, :] = factor * w[c]


def project(group, element, drag, nodes, parts):
    low_half = lanes() < 64

    def one(r, _):
        e = element(r)
        x = group[pl.ds(r, 1), :]
        weights = [gauss(x, nodes, 17 + k) for k in range(3)]
        planes = outer(
            gauss(group[pl.ds(r + 32, 1), :], nodes, 16),
            gauss(group[pl.ds(r + 64, 1), :], nodes, 16),
        )
        planes = jnp.concatenate(split_two(planes), axis=0)
        rows = []
        for c in range(3):
            force = -drag[pl.ds(c * 32 + r, 1), :]
            rows += [wr * force for wr in weights]
        rows = jnp.concatenate(split_two(jnp.concatenate(rows, axis=0)), axis=0)
        both = lax.dot_general(
            rows, planes, (((1,), (1,)), ((), ())), preferred_element_type=F32
        )
        both = both[:72, :] + both[72:, :]
        both = both + pltpu.roll(both, 64, 1)
        at = (e >> 4) * 576 + (e & 15)
        for k in range(9):
            t = both[8 * k : 8 * k + 8, :]
            t = jnp.where(low_half, t, pltpu.roll(t, 4, 0))
            parts[pl.ds(at + k * 64, 4, stride=16), :] = t[0:4, :]
        return 0

    lax.fori_loop(0, SHARE, one, 0, unroll=UNROLL_B)


def own_kernel(elem, group, vel, nodes, field, parts, drag, fluid):
    def element(r):
        return elem[r]

    spread_field(vel, field)
    interpolate(group, element, field, nodes, fluid)
    find_drag(group, fluid, drag)
    project(group, element, drag, nodes, parts)


def rest_kernel(
    g1, g2, g3, field, nodes, _, d1, d2, d3, inside, ghosts, parts, fluid, lab_v, lab_s, sem
):
    groups = (g1, g2, g3)
    drags = (d1, d2, d3)
    for k, g in enumerate(groups):
        lab_v[k : k + 1, :] = g[256:257, :].astype(jnp.int32)
    copy = pltpu.make_async_copy(lab_v, lab_s, sem)
    copy.start()
    copy.wait()
    elements = [lambda r, k=k: lab_s[k, r] for k in range(3)]
    for k in range(3):
        interpolate(groups[k], elements[k], field, nodes, fluid)
        find_drag(groups[k], fluid, drags[k])
    for k in range(3):
        project(groups[k], elements[k], drags[k], nodes, parts)
    gather_parts(parts, inside, ghosts)


def gather_parts(parts, inside, ghosts):
    low_half = lanes() < 64
    odd = lax.axis_index("gx") & 1
    to_lo = (1 - odd) * 12
    to_hi = odd * 12

    def part(x, y, c, k, h):
        return parts[pl.ds((x * 4 + y) * 576 + (c * 3 + k) * 64 + h * 16, 16), :]

    def one(y, _):
        for c in range(3):
            lower = []
            upper = []
            for h in range(4):
                lo = part(0, y, c, 1, h) + part(1, y, c, 0, h)
                hi = part(1, y, c, 1, h) + part(0, y, c, 2, h)
                inside[c * 8 + y, :, 128 * h : 128 * h + 128] = lo
                inside[c * 8 + 4 + y, :, 128 * h : 128 * h + 128] = hi
                lower.append(lo)
                upper.append(hi)
            for h in range(4):
                lo = part(0, y, c, 0, h)
                hi = part(1, y, c, 2, h)
                if h == 3:
                    lo = lo + jnp.where(low_half, 0.0, pltpu.roll(lower[0], 64, 1))
                if h == 0:
                    hi = hi + jnp.where(low_half, pltpu.roll(upper[3], 64, 1), 0.0)
                ghosts[to_lo + c * 4 + y, :, 128 * h : 128 * h + 128] = lo
                ghosts[to_hi + c * 4 + y, :, 128 * h : 128 * h + 128] = hi
        return 0

    lax.fori_loop(0, 4, one, 0)


def first_pass_kernel(last_gx, inside, sent, near, far, field, faces):
    low_half = lanes() < 64
    spot = (lanes() % 64) // 8
    gx = lax.axis_index("gx")
    odd = (gx & 1) == 1
    has_before = gx > 0
    has_after = gx < last_gx
    to_lo = (1 - (gx & 1)) * 12
    to_hi = (gx & 1) * 12
    y_odd = (lax.axis_index("gy") & 1) == 1

    def cut(ref, at, h):
        return ref[at, :, 128 * h : 128 * h + 128]

    for c in range(3):
        packed = [jnp.zeros((16, 128), F32), jnp.zeros((16, 128), F32)]
        for y in range(4):
            pair = [(cut(near, c * 4 + y, h), cut(far, c * 4 + y, h)) for h in range(4)]
            got_lo = [jnp.where(odd, n, f) for n, f in pair]
            got_hi = [jnp.where(odd, f, n) for n, f in pair]
            lower = [cut(inside, c * 8 + y, h) + got_lo[h] for h in range(4)]
            upper = [cut(inside, c * 8 + 4 + y, h) + got_hi[h] for h in range(4)]
            first = got_lo[0] + pltpu.roll(cut(sent, to_lo + c * 4 + y, 3), 64, 1)
            last = got_hi[3] + pltpu.roll(cut(sent, to_hi + c * 4 + y, 0), 64, 1)
            low3, up0 = lower[3], upper[0]
            lower[0] = jnp.where(low_half & has_before, first, lower[0])
            upper[3] = jnp.where(low_half | jnp.logical_not(has_after), upper[3], last)
            lower[3] = jnp.where(low_half, low3, low3 + pltpu.roll(up0, 64, 1))
            upper[0] = jnp.where(low_half, up0 + pltpu.roll(low3, 64, 1), up0)
            for x, layer in ((0, lower), (1, upper)):
                for h in range(4):
                    field[c * 8 + x * 4 + y, :, 128 * h : 128 * h + 128] = layer[h]
                    k = x * 4 + h
                    if y == 0:
                        moved = pltpu.roll(layer[h], 8 * k, 1) if k else layer[h]
                        packed[0] = jnp.where(spot == k, moved, packed[0])
                    if y == 3:
                        by = (8 * k - 56) % 128
                        moved = pltpu.roll(layer[h], by, 1) if by else layer[h]
                        packed[1] = jnp.where(spot == k, moved, packed[1])
        faces[16 * c : 16 * c + 16, :] = jnp.where(y_odd, packed[0], packed[1])
        faces[48 + 16 * c : 64 + 16 * c, :] = jnp.where(y_odd, packed[1], packed[0])


def last_pass_kernel(field, got1, got3, out):
    lane = lanes()
    bottom = (lane % 64) < 8
    top = (lane % 64) >= 56
    z = lax.broadcasted_iota(jnp.int32, (16, 128), 0)
    lane16 = lanes((16, 128))
    up_here = (lane16 % 8 == 7) & (z < 15)
    down_here = (lane16 % 8 == 0) & (z > 0)
    odd = (lax.axis_index("gy") & 1) == 1

    def one_comp(c, _):
        one = got1[pl.ds(16 * c, 16), :]
        three = got3[pl.ds(16 * c, 16), :]
        lo_pack = jnp.where(odd, one, three)
        hi_pack = jnp.where(odd, three, one)
        for x in range(2):
            for h in range(4):
                k = x * 4 + h
                f = [field[c * 8 + x * 4 + y, :, 128 * h : 128 * h + 128] for y in range(4)]
                down = lo_pack if k == 0 else pltpu.roll(lo_pack, (128 - 8 * k) % 128, 1)
                up = hi_pack if k == 7 else pltpu.roll(hi_pack, 56 - 8 * k, 1)
                for y in range(4):
                    above = up if y == 3 else pltpu.roll(f[y + 1], 56, 1)
                    below = down if y == 0 else pltpu.roll(f[y - 1], 72, 1)
                    g = f[y] + jnp.where(top, above, jnp.where(bottom, below, 0.0))
                    above = pltpu.roll(pltpu.roll(g, 7, 1), 15, 0)
                    below = pltpu.roll(pltpu.roll(g, 121, 1), 1, 0)
                    g = g + jnp.where(up_here, above, jnp.where(down_here, below, 0.0))
                    out[c * 8 + x * 4 + y, :, 128 * h : 128 * h + 128] = g
        return 0

    lax.fori_loop(0, 3, one_comp, 0)


def unpack_kernel(block, d0, d1, d2, d3, drag):
    for k, d in enumerate((d0, d1, d2, d3)):

        def one(r, _):
            drag[pl.ds(block[k * SHARE + r], 3, stride=128), :] = d[pl.ds(r, 3, stride=32), :]
            return 0

        lax.fori_loop(0, SHARE, one, 0, unroll=8)


def swapped(x, axis, partner):
    count = lax.axis_size(axis)
    pairs = [(i, partner(i)) for i in range(count) if 0 <= partner(i) < count]
    return lax.ppermute(x, axis, pairs)


def body(velocity, part_pos, part_vel, part_coef, counts, dest, elem):
    pos = part_pos.transpose(1, 0, 2).reshape(384, 128)
    vel = part_vel.transpose(1, 0, 2).reshape(384, 128)
    coef = part_coef.reshape(256, 128)
    nodes = jnp.asarray(node_table())
    send, block, own_elem = call(
        pack_kernel,
        [((N_GY * ROWS, 128), F32, "vmem"), ((128,), jnp.int32, "smem"), ((128,), jnp.int32, "smem")],
        [(dest, "table"), (counts, "table"), (elem, "table"), (pos, "hbm"), (vel, "hbm"), (coef, "hbm")],
    )
    own = send[:ROWS]
    groups = [
        swapped(send[k * ROWS : (k + 1) * ROWS], "gy", lambda i, k=k: i ^ k) for k in range(1, N_GY)
    ]
    field, parts, drag_own = call(
        own_kernel,
        [((8 * 384, 128), F32, "vmem"), ((8 * 576, 128), F32, "vmem"), ((96, 128), F32, "vmem")],
        [(own_elem, "smem"), (own, "vmem"), (velocity.reshape(24, 16, 512), "hbm"), (nodes, "")],
        (VMEM((96, 128), F32),),
        flops=OWN_FLOPS,
    )
    *drags, inside, ghosts, _ = call(
        rest_kernel,
        [((96, 128), F32, "vmem")] * 3
        + [((24, 16, 512), F32, "vmem")] * 2
        + [((8 * 576, 128), F32, "vmem")],
        [(g, "vmem") for g in groups] + [(field, "vmem"), (nodes, ""), (parts, "vmem")],
        (
            VMEM((96, 128), F32),
            VMEM((8, 128), jnp.int32),
            SMEM((8, 128), jnp.int32),
            pltpu.SemaphoreType.DMA,
        ),
        aliases={5: 5},
    )
    far = swapped(ghosts[12:], "gx", lambda i: i + 1 if i & 1 else i - 1)
    near = swapped(ghosts[:12], "gx", lambda i: i ^ 1)
    back = [swapped(d, "gy", lambda i, k=k: i ^ k) for k, d in enumerate(drags, 1)]
    last_gx = lax.axis_size("gx") - 1
    field, faces = call(
        lambda *refs: first_pass_kernel(last_gx, *refs),
        [((24, 16, 512), F32, "vmem"), ((96, 128), F32, "vmem")],
        [(inside, "vmem"), (ghosts, "vmem"), (near, "vmem"), (far, "vmem")],
    )
    got1 = swapped(faces[:48], "gy", lambda i: i ^ 1)
    got3 = lax.ppermute(faces[48:], "gy", [(1, 2), (2, 1)])
    (drag,) = call(
        unpack_kernel,
        [((384, 128), F32, "")],
        [(block, "smem"), (drag_own, "vmem")] + [(d, "vmem") for d in back],
        flops=UNPACK_FLOPS,
    )
    (out,) = call(
        last_pass_kernel,
        [((24, 16, 512), F32, "")],
        [(field, "vmem"), (got1, "vmem"), (got3, "vmem")],
    )
    return (
        drag.reshape(3, 128, 128).transpose(1, 0, 2),
        out.reshape(velocity.shape),
    )


def solution(mesh):
    in_specs = (
        P(None, "gx", "gy", None, None),
        P(("gx", "gy"), None, None),
        P(("gx", "gy"), None, None),
        P(("gx", "gy"), None, None),
        P(("gx", "gy")),
        P(("gx", "gy")),
        P(("gx", "gy")),
    )
    out_specs = (P(("gx", "gy"), None, None), P(None, "gx", "gy", None, None))
    return jax.shard_map(body, mesh=mesh, in_specs=in_specs, out_specs=out_specs, check_vma=False)
```

time: 71.5 us -> 46.1 us (0.64)
  the two profiles are of different devices: /device:TPU:24 before, /device:TPU:18 now
where the time goes in v1:
time: 46.1 us; the launch traced here: 45.8 us
  Pallas kernels  21.9 us (48%)
  starting transfers between devices  15.5 us (34%)
  waiting for transfers between devices  6.65 us (14%)
  local copies, waits for them, and re-layouts  0.98 us (2%)
  between operations  0.76 us (2%)
    pallas_call x6, Pallas kernels, call(): pl.pallas_call(kernel, out_shape=shapes, in_specs=[pl.BlockSpec(memory_sp...  21.9 us
    ppermute x9, starting transfers between devices, swapped(): return lax.ppermute(x, axis, pairs)  12.1 us
    ppermute x9, waiting for transfers between devices, swapped(): return lax.ppermute(x, axis, pairs)  5.96 us
    ppermute x1, starting transfers between devices, body(): got3 = lax.ppermute(faces[48:], 'gy', [(1, 2), (2, 1)])  3.4 us
  transfers between devices with their start and end apart: 10, of which 5 were waited for; matrix products, arithmetic and copies ran while one was open for 0% of the time, Pallas kernels for 13%

profile of v1, /device:TPU:18, one launch (start us, length us, event | category | flops | bytes accessed | tf_op | source)
XLA Modules:
  0.0 45.8 jit_solution(16236135303604030781)
XLA Ops:
  0.6 2.9 %shard_map.95 = (f32[1056,128]{1,0:T(8,128)S(1)}, s32[128]{0:T(128)S(1)}, s32[128]{0:T(128)S(1)}) custom-call(s32[128]{0:T(128)} %dest.1, s32[128]{0:T(128)} %counts.1, s32[128]{0:T(128)} %elem.1, f32[384,128]{1,0:T(8,128)} %bitcast.13, f32[384,128]{1,0:T(8,128)} %bitcast.14, f32[256,128]{1,0:T(8,128)} %bitcast.15), custom_call_target="tpu_custom_call" | custom-call | tf_op jit(solution)/shard_map/pallas_call | solution.py:64
  3.6 1.6 %collective-permute-start.2 = (f32[264,128]{1,0:T(8,128)S(1)}, f32[264,128]{1,0:T(8,128)S(1)}, u32[]{:S(2)}, u32[]{:S(2)}) collective-permute-start(f32[264,128]{1,0:T(8,128)S(1)} %get-tuple-element.30), channel_id=1, source_target_pairs={{0,3},{1,2},{2,1},{3,0},{4,7},{5,6},{6,5},{7,4},{8,11},{9,10},{10,... | collective-permute-start | bytes 405512 | tf_op jit(solution)/shard_map/ppermute | solution.py:361
  5.2 1.1 %collective-permute-start.1 = (f32[264,128]{1,0:T(8,128)S(1)}, f32[264,128]{1,0:T(8,128)S(1)}, u32[]{:S(2)}, u32[]{:S(2)}) collective-permute-start(f32[264,128]{1,0:T(8,128)S(1)} %get-tuple-element.31), channel_id=1, source_target_pairs={{0,2},{1,3},{2,0},{3,1},{4,6},{5,7},{6,4},{7,5},{8,10},{9,11},{10,... | collective-permute-start | bytes 405512 | tf_op jit(solution)/shard_map/ppermute | solution.py:361
  6.3 1.5 %collective-permute-start = (f32[264,128]{1,0:T(8,128)S(1)}, f32[264,128]{1,0:T(8,128)S(1)}, u32[]{:S(2)}, u32[]{:S(2)}) collective-permute-start(f32[264,128]{1,0:T(8,128)S(1)} %get-tuple-element.32), channel_id=1, source_target_pairs={{0,1},{1,0},{2,3},{3,2},{4,5},{5,4},{6,7},{7,6},{8,9},{9,8},{10,11... | collective-permute-start | bytes 405512 | tf_op jit(solution)/shard_map/ppermute | solution.py:361
  7.8 0.0 copy-start
  7.8 0.9 %copy-done = f32[160,128]{1,0:T(8,128)S(1)} copy-done((f32[160,128]{1,0:T(8,128)S(1)}, f32[160,128]{1,0:T(8,128)}, u32[]{:S(2)}) %copy-start) | copy-done | bytes 81944
  8.7 4.0 %shard_map.96 = (f32[3072,128]{1,0:T(8,128)S(1)}, f32[4608,128]{1,0:T(8,128)S(1)}, f32[96,128]{1,0:T(8,128)S(1)}) custom-call(s32[128]{0:T(128)S(1)} %get-tuple-element.16.elem, f32[264,128]{1,0:T(8,128)S(1)} %get-tuple-element.33.group, bf16[24,16,512]{2,1,0:T(8,128)(2,1)} %bitcast.16, f32[160,128]{1,0:T(8,128)S(1)} %copy-done), custom_call_target="tpu_custom_call" | custom-call | flops 2000000000 | tf_op jit(solution)/shard_map/pallas_call | solution.py:64
  12.7 0.0 collective-permute-done.2.g3
  12.7 0.4 collective-permute-done.1.g2
  13.1 0.6 %collective-permute-done.g1 = f32[264,128]{1,0:T(8,128)S(1)} collective-permute-done((f32[264,128]{1,0:T(8,128)S(1)}, f32[264,128]{1,0:T(8,128)S(1)}, u32[]{:S(2)}, u32[]{:S(2)}) %collective-permute-start) | collective-permute-done | bytes 135200 | tf_op jit(solution)/shard_map/ppermute | solution.py:361
  13.7 8.1 %shard_map.97 = (f32[96,128]{1,0:T(8,128)S(1)}, f32[96,128]{1,0:T(8,128)S(1)}, f32[96,128]{1,0:T(8,128)S(1)}, f32[24,16,512]{2,1,0:T(8,128)S(1)}, f32[24,16,512]{2,1,0:T(8,128)S(1)}, /*index=5*/f32[4608,128]{1,0:T(8,128)S(1)}) custom-call(f32[264,128]{1,0:T(8,128)S(1)} %collective-permute-done.g1, ...), custom_call_target="tpu_custom_call", output_to_operand_aliasing={{5}: (5, {})} | custom-call | tf_op jit(solution)/shard_map/pallas_call | solution.py:64
  21.8 0.1 fusion
  21.9 4.2 %collective-permute-start.7 = (f32[12,16,512]{2,1,0:T(8,128)S(1)}, f32[12,16,512]{2,1,0:T(8,128)S(1)}, u32[]{:S(2)}, u32[]{:S(2)}) collective-permute-start(f32[12,16,512]{2,1,0:T(8,128)S(1)} %get-tuple-element.28), channel_id=1, source_target_pairs={{4,8},{8,4},{12,16},{16,12},{20,24},{24,20},{28,32},{32,28},{36,40... | collective-permute-start | bytes 1179656 | tf_op jit(solution)/shard_map/ppermute | solution.py:361
  26.1 0.1 collective-permute-start.6
  26.1 1.0 %collective-permute-start.3 = (f32[96,128]{1,0:T(8,128)S(1)}, f32[96,128]{1,0:T(8,128)S(1)}, u32[]{:S(2)}, u32[]{:S(2)}) collective-permute-start(f32[96,128]{1,0:T(8,128)S(1)} %get-tuple-element.21), channel_id=1, source_target_pairs={{0,1},{1,0},{2,3},{3,2},{4,5},{5,4},{6,7},{7,6},{8,9},{9,8},{10,11... | collective-permute-start | bytes 147464 | tf_op jit(solution)/shard_map/ppermute | solution.py:361
  27.1 2.1 %collective-permute-start.4 = (f32[96,128]{1,0:T(8,128)S(1)}, f32[96,128]{1,0:T(8,128)S(1)}, u32[]{:S(2)}, u32[]{:S(2)}) collective-permute-start(f32[96,128]{1,0:T(8,128)S(1)} %get-tuple-element.22), channel_id=1, source_target_pairs={{0,2},{1,3},{2,0},{3,1},{4,6},{5,7},{6,4},{7,5},{8,10},{9,11},{10,... | collective-permute-start | bytes 147464 | tf_op jit(solution)/shard_map/ppermute | solution.py:361
  29.2 0.5 %collective-permute-start.5 = (f32[96,128]{1,0:T(8,128)S(1)}, f32[96,128]{1,0:T(8,128)S(1)}, u32[]{:S(2)}, u32[]{:S(2)}) collective-permute-start(f32[96,128]{1,0:T(8,128)S(1)} %get-tuple-element.23), channel_id=1, source_target_pairs={{0,3},{1,2},{2,1},{3,0},{4,7},{5,6},{6,5},{7,4},{8,11},{9,10},{10,... | collective-permute-start | bytes 147464 | tf_op jit(solution)/shard_map/ppermute | solution.py:361
  29.7 3.3 %collective-permute-done.7.refs_3_ = f32[12,16,512]{2,1,0:T(8,128)S(1)} collective-permute-done((f32[12,16,512]{2,1,0:T(8,128)S(1)}, f32[12,16,512]{2,1,0:T(8,128)S(1)}, u32[]{:S(2)}, u32[]{:S(2)}) %collective-permute-start.7) | collective-permute-done | bytes 393248 | tf_op jit(solution)/shard_map/ppermute | solution.py:361
  33.1 0.0 collective-permute-done.6.refs_2_
  33.1 0.4 shard_map.99
  33.5 3.4 %collective-permute-start.9 = (f32[48,128]{1,0:T(8,128)S(1)}, f32[48,128]{1,0:T(8,128)S(1)}, u32[]{:S(2)}, u32[]{:S(2)}) collective-permute-start(f32[48,128]{1,0:T(8,128)S(1)} %get-tuple-element.34), channel_id=1, source_target_pairs={{1,2},{2,1},{5,6},{6,5},{9,10},{10,9},{13,14},{14,13},{17,18},{18,... | collective-permute-start | bytes 73736 | tf_op jit(solution)/shard_map/ppermute | solution.py:409
  36.9 0.1 collective-permute-start.8
  37.0 0.0 collective-permute-done.3.d1
  37.0 0.0 collective-permute-done.4.d2
  37.0 0.0 collective-permute-done.5.d3
  37.0 1.5 %shard_map.98 = f32[384,128]{1,0:T(8,128)} custom-call(s32[128]{0:T(128)S(1)} %get-tuple-element.15.block, f32[96,128]{1,0:T(8,128)S(1)} %get-tuple-element.18.d0, f32[96,128]{1,0:T(8,128)S(1)} %collective-permute-done.3.d1, f32[96,128]{1,0:T(8,128)S(1)} %collective-permute-done.4.d2, f32[96,128]{1,0:T(8,128)S(1)} %collective-permute-done.5.d3), custom_call_target="tpu_custom_call" | custom-call | flops 1000000000 | tf_op jit(solution)/shard_map/pallas_call | solution.py:64
  38.5 0.7 %collective-permute-done.9.got3 = f32[48,128]{1,0:T(8,128)S(1)} collective-permute-done((f32[48,128]{1,0:T(8,128)S(1)}, f32[48,128]{1,0:T(8,128)S(1)}, u32[]{:S(2)}, u32[]{:S(2)}) %collective-permute-start.9) | collective-permute-done | bytes 24608 | tf_op jit(solution)/shard_map/ppermute | solution.py:409
  39.2 1.6 %collective-permute-done.8.got1 = f32[48,128]{1,0:T(8,128)S(1)} collective-permute-done((f32[48,128]{1,0:T(8,128)S(1)}, f32[48,128]{1,0:T(8,128)S(1)}, u32[]{:S(2)}, u32[]{:S(2)}) %collective-permute-start.8) | collective-permute-done | bytes 24608 | tf_op jit(solution)/shard_map/ppermute | solution.py:361
  40.8 5.0 %shard_map.100 = f32[24,16,512]{2,1,0:T(8,128)} custom-call(f32[24,16,512]{2,1,0:T(8,128)S(1)} %get-tuple-element.26.field, f32[48,128]{1,0:T(8,128)S(1)} %collective-permute-done.8.got1, f32[48,128]{1,0:T(8,128)S(1)} %collective-permute-done.9.got3), custom_call_target="tpu_custom_call" | custom-call | tf_op jit(solution)/shard_map/pallas_call | solution.py:64
  (2 shorter events, 0.0 us)
Async XLA Ops:
  3.6 9.1 %collective-permute-start.2 = (f32[264,128]{1,0:T(8,128)S(1)}, f32[264,128]{1,0:T(8,128)S(1)}, u32[]{:S(2)}, u32[]{:S(2)}) collective-permute-start(f32[264,128]{1,0:T(8,128)S(1)} %get-tuple-element.30), channel_id=1, source_target_pairs={{0,3},{1,2},{2,1},{3,0},{4,7},{5,6},{6,5},{7,4},{8,11},{9,10},{10,... | collective-permute-start | bytes 405512 | tf_op jit(solution)/shard_map/ppermute | solution.py:361
  5.2 8.0 %collective-permute-start.1 = (f32[264,128]{1,0:T(8,128)S(1)}, f32[264,128]{1,0:T(8,128)S(1)}, u32[]{:S(2)}, u32[]{:S(2)}) collective-permute-start(f32[264,128]{1,0:T(8,128)S(1)} %get-tuple-element.31), channel_id=1, source_target_pairs={{0,2},{1,3},{2,0},{3,1},{4,6},{5,7},{6,4},{7,5},{8,10},{9,11},{10,... | collective-permute-start | bytes 405512 | tf_op jit(solution)/shard_map/ppermute | solution.py:361
  6.3 7.5 %collective-permute-start = (f32[264,128]{1,0:T(8,128)S(1)}, f32[264,128]{1,0:T(8,128)S(1)}, u32[]{:S(2)}, u32[]{:S(2)}) collective-permute-start(f32[264,128]{1,0:T(8,128)S(1)} %get-tuple-element.32), channel_id=1, source_target_pairs={{0,1},{1,0},{2,3},{3,2},{4,5},{5,4},{6,7},{7,6},{8,9},{9,8},{10,11... | collective-permute-start | bytes 405512 | tf_op jit(solution)/shard_map/ppermute | solution.py:361
  7.8 0.9 %copy-start = (f32[160,128]{1,0:T(8,128)S(1)}, f32[160,128]{1,0:T(8,128)}, u32[]{:S(2)}) copy-start(f32[160,128]{1,0:T(8,128)} %constant.2.clone.nodes) | copy-start | bytes 245764
  21.9 11.2 %collective-permute-start.7 = (f32[12,16,512]{2,1,0:T(8,128)S(1)}, f32[12,16,512]{2,1,0:T(8,128)S(1)}, u32[]{:S(2)}, u32[]{:S(2)}) collective-permute-start(f32[12,16,512]{2,1,0:T(8,128)S(1)} %get-tuple-element.28), channel_id=1, source_target_pairs={{4,8},{8,4},{12,16},{16,12},{20,24},{24,20},{28,32},{32,28},{36,40... | collective-permute-start | bytes 1179656 | tf_op jit(solution)/shard_map/ppermute | solution.py:361
  26.1 7.0 %collective-permute-start.6 = (f32[12,16,512]{2,1,0:T(8,128)S(1)}, f32[12,16,512]{2,1,0:T(8,128)S(1)}, u32[]{:S(2)}, u32[]{:S(2)}) collective-permute-start(f32[12,16,512]{2,1,0:T(8,128)S(1)} %get-tuple-element.29), channel_id=1, source_target_pairs={{0,4},{4,0},{8,12},{12,8},{16,20},{20,16},{24,28},{28,24},{32,36},... | collective-permute-start | bytes 1179656 | tf_op jit(solution)/shard_map/ppermute | solution.py:361
  26.1 10.9 %collective-permute-start.3 = (f32[96,128]{1,0:T(8,128)S(1)}, f32[96,128]{1,0:T(8,128)S(1)}, u32[]{:S(2)}, u32[]{:S(2)}) collective-permute-start(f32[96,128]{1,0:T(8,128)S(1)} %get-tuple-element.21), channel_id=1, source_target_pairs={{0,1},{1,0},{2,3},{3,2},{4,5},{5,4},{6,7},{7,6},{8,9},{9,8},{10,11... | collective-permute-start | bytes 147464 | tf_op jit(solution)/shard_map/ppermute | solution.py:361
  27.1 9.9 %collective-permute-start.4 = (f32[96,128]{1,0:T(8,128)S(1)}, f32[96,128]{1,0:T(8,128)S(1)}, u32[]{:S(2)}, u32[]{:S(2)}) collective-permute-start(f32[96,128]{1,0:T(8,128)S(1)} %get-tuple-element.22), channel_id=1, source_target_pairs={{0,2},{1,3},{2,0},{3,1},{4,6},{5,7},{6,4},{7,5},{8,10},{9,11},{10,... | collective-permute-start | bytes 147464 | tf_op jit(solution)/shard_map/ppermute | solution.py:361
  29.2 7.9 %collective-permute-start.5 = (f32[96,128]{1,0:T(8,128)S(1)}, f32[96,128]{1,0:T(8,128)S(1)}, u32[]{:S(2)}, u32[]{:S(2)}) collective-permute-start(f32[96,128]{1,0:T(8,128)S(1)} %get-tuple-element.23), channel_id=1, source_target_pairs={{0,3},{1,2},{2,1},{3,0},{4,7},{5,6},{6,5},{7,4},{8,11},{9,10},{10,... | collective-permute-start | bytes 147464 | tf_op jit(solution)/shard_map/ppermute | solution.py:361
  33.5 5.7 %collective-permute-start.9 = (f32[48,128]{1,0:T(8,128)S(1)}, f32[48,128]{1,0:T(8,128)S(1)}, u32[]{:S(2)}, u32[]{:S(2)}) collective-permute-start(f32[48,128]{1,0:T(8,128)S(1)} %get-tuple-element.34), channel_id=1, source_target_pairs={{1,2},{2,1},{5,6},{6,5},{9,10},{10,9},{13,14},{14,13},{17,18},{18,... | collective-permute-start | bytes 73736 | tf_op jit(solution)/shard_map/ppermute | solution.py:409
  36.9 3.9 %collective-permute-start.8 = (f32[48,128]{1,0:T(8,128)S(1)}, f32[48,128]{1,0:T(8,128)S(1)}, u32[]{:S(2)}, u32[]{:S(2)}) collective-permute-start(f32[48,128]{1,0:T(8,128)S(1)} %get-tuple-element.35), channel_id=1, source_target_pairs={{0,1},{1,0},{2,3},{3,2},{4,5},{5,4},{6,7},{7,6},{8,9},{9,8},{10,11... | collective-permute-start | bytes 73736 | tf_op jit(solution)/shard_map/ppermute | solution.py:361

commit v2 on v1

--- a/solution.py
+++ b/solution.py
@@ -36,16 +36,21 @@
             rows.append([q[[m for m in range(8) if m != i][t]] for i in order])
         rows.append([1.0 / np.prod([q[i] - q[m] for m in range(8) if m != i]) for i in order])
     rows.append([q[i] for i in range(8)])
-    for shift in (-2.0, 0.0, 2.0):
-        rows.append([q[i] + shift for i in PAIRED])
+    for first, second in ((-2.0, 0.0), (2.0, 2.0)):
+        for half in (PAIRED[:4], PAIRED[4:]):
+            rows.append([q[i] + first for i in half] + [q[i] + second for i in half])
     table = np.array(rows, np.float32).reshape(-1, 1)
     return np.ascontiguousarray(np.broadcast_to(table, (table.shape[0], 128)))
 
 
+PITCH = 17
 UNROLL_A = 16
-UNROLL_B = 8
+UNROLL_B = 16
 OWN_FLOPS = 2_000_000_000
 UNPACK_FLOPS = 1_000_000_000
+
+
+SPACES = {"vmem": VMEM, "hbm": VMEM, "": VMEM, "smem": SMEM, "table": SMEM, "raw": pltpu.HBM}
 
 
 def call(kernel, outs, ins, scratch=(), flops=0, aliases=None):
@@ -53,7 +58,7 @@
         a
         if INTERPRET
         else pltpu.with_memory_space_constraint(a, VMEM if m == "vmem" else pltpu.HBM)
-        if m in ("vmem", "hbm", "table")
+        if m in ("vmem", "hbm", "table", "raw")
         else a
         for a, m in ins
     ]
@@ -64,8 +69,8 @@
     return pl.pallas_call(
         kernel,
         out_shape=shapes,
-        in_specs=[pl.BlockSpec(memory_space=SMEM if m in ("smem", "table") else VMEM) for _, m in ins],
-        out_specs=[pl.BlockSpec(memory_space=SMEM if m == "smem" else VMEM) for _, _, m in outs],
+        in_specs=[pl.BlockSpec(memory_space=SPACES[m]) for _, m in ins],
+        out_specs=[pl.BlockSpec(memory_space=SPACES[m]) for _, _, m in outs],
         scratch_shapes=scratch,
         interpret=INTERPRET,
         input_output_aliases=aliases or {},
@@ -134,9 +139,9 @@
             for h in range(4):
                 t = vel[c * 8 + xy, :, 128 * h : 128 * h + 128].astype(F32)
                 turned = pltpu.roll(t, 64, 1)
-                at = xy * 384 + (c * 8 + h) * 16
+                at = (xy * 24 + c * 8 + h) * PITCH
                 field[pl.ds(at, 16), :] = jnp.where(low_half, t, turned)
-                field[pl.ds(at + 64, 16), :] = jnp.where(low_half, turned, t)
+                field[pl.ds(at + 4 * PITCH, 16), :] = jnp.where(low_half, turned, t)
         return 0
 
     lax.fori_loop(0, 8, one, 0)
@@ -149,7 +154,7 @@
         basis_s = lagrange(group[pl.ds(r + 32, 1), :], nodes, 0)
         basis_t = lagrange(group[pl.ds(r + 64, 1), :], nodes, 0)
         high, low = split_two(outer(basis_s, basis_t))
-        nodal = field[pl.ds((e >> 4) * 384 + (e & 15), 24, stride=16), :].astype(BF16)
+        nodal = field[pl.ds((e >> 4) * (24 * PITCH) + (e & 15), 24, stride=PITCH), :].astype(BF16)
         part = jnp.dot(nodal, jnp.concatenate([high, low], axis=0), preferred_element_type=F32)
         for c in range(3):
             fluid[pl.ds(c * 32 + r, 1), :] = jnp.sum(
@@ -174,40 +179,46 @@
 
 def project(group, element, drag, nodes, parts):
     low_half = lanes() < 64
+    upper_rows = lax.broadcasted_iota(jnp.int32, (8, 128), 0) < 4
 
     def one(r, _):
         e = element(r)
         x = group[pl.ds(r, 1), :]
-        weights = [gauss(x, nodes, 17 + k) for k in range(3)]
+        near = [gauss(x, nodes, 17 + k) for k in range(2)]
+        after = [gauss(x, nodes, 19 + k) for k in range(2)]
         planes = outer(
             gauss(group[pl.ds(r + 32, 1), :], nodes, 16),
             gauss(group[pl.ds(r + 64, 1), :], nodes, 16),
         )
         planes = jnp.concatenate(split_two(planes), axis=0)
+        force = [-drag[pl.ds(c * 32 + r, 1), :] for c in range(3)]
+        mixed = jnp.where(upper_rows, force[0], force[1])
         rows = []
-        for c in range(3):
-            force = -drag[pl.ds(c * 32 + r, 1), :]
-            rows += [wr * force for wr in weights]
+        for k in range(2):
+            rows += [near[k] * f for f in force] + [after[k] * mixed, after[k] * force[2]]
         rows = jnp.concatenate(split_two(jnp.concatenate(rows, axis=0)), axis=0)
         both = lax.dot_general(
             rows, planes, (((1,), (1,)), ((), ())), preferred_element_type=F32
         )
-        both = both[:72, :] + both[72:, :]
-        both = both + pltpu.roll(both, 64, 1)
-        at = (e >> 4) * 576 + (e & 15)
-        for k in range(9):
-            t = both[8 * k : 8 * k + 8, :]
-            t = jnp.where(low_half, t, pltpu.roll(t, 4, 0))
-            parts[pl.ds(at + k * 64, 4, stride=16), :] = t[0:4, :]
+        both = both[:80, :] + both[80:, :]
+        at = (e >> 4) * (36 * PITCH) + (e & 15)
+        for k in range(5):
+            even = both[8 * k : 8 * k + 8, :]
+            odd = both[40 + 8 * k : 48 + 8 * k, :]
+            t = jnp.where(low_half, even, odd)
+            t = t + pltpu.roll(jnp.where(low_half, odd, even), 64, 1)
+            n = 8 if k < 4 else 4
+            parts[pl.ds(at + k * 8 * PITCH, n, stride=PITCH), :] = t[0:n, :]
         return 0
 
     lax.fori_loop(0, SHARE, one, 0, unroll=UNROLL_B)
 
 
-def own_kernel(elem, group, vel, nodes, field, parts, drag, fluid):
+def own_kernel(elem, group, vel, nodes, field, parts, drag, table, fluid):
     def element(r):
         return elem[r]
 
+    table[...] = nodes[...]
     spread_field(vel, field)
     interpolate(group, element, field, nodes, fluid)
     find_drag(group, fluid, drag)
@@ -240,7 +251,8 @@
     to_hi = odd * 12
 
     def part(x, y, c, k, h):
-        return parts[pl.ds((x * 4 + y) * 576 + (c * 3 + k) * 64 + h * 16, 16), :]
+        n = 2 * c + k if k < 2 else 6 + c
+        return parts[pl.ds(((x * 4 + y) * 36 + n * 4 + h) * PITCH, 16), :]
 
     def one(y, _):
         for c in range(3):
@@ -311,7 +323,7 @@
         faces[48 + 16 * c : 64 + 16 * c, :] = jnp.where(y_odd, packed[1], packed[0])
 
 
-def last_pass_kernel(field, got1, got3, out):
+def last_passes(field, rows, before, after, buf, start):
     lane = lanes()
     bottom = (lane % 64) < 8
     top = (lane % 64) >= 56
@@ -319,40 +331,86 @@
     lane16 = lanes((16, 128))
     up_here = (lane16 % 8 == 7) & (z < 15)
     down_here = (lane16 % 8 == 0) & (z > 0)
-    odd = (lax.axis_index("gy") & 1) == 1
 
     def one_comp(c, _):
-        one = got1[pl.ds(16 * c, 16), :]
-        three = got3[pl.ds(16 * c, 16), :]
-        lo_pack = jnp.where(odd, one, three)
-        hi_pack = jnp.where(odd, three, one)
+        lo_pack = before(c)
+        hi_pack = after(c)
         for x in range(2):
-            for h in range(4):
-                k = x * 4 + h
-                f = [field[c * 8 + x * 4 + y, :, 128 * h : 128 * h + 128] for y in range(4)]
-                down = lo_pack if k == 0 else pltpu.roll(lo_pack, (128 - 8 * k) % 128, 1)
-                up = hi_pack if k == 7 else pltpu.roll(hi_pack, 56 - 8 * k, 1)
-                for y in range(4):
-                    above = up if y == 3 else pltpu.roll(f[y + 1], 56, 1)
-                    below = down if y == 0 else pltpu.roll(f[y - 1], 72, 1)
-                    g = f[y] + jnp.where(top, above, jnp.where(bottom, below, 0.0))
+            for y in rows:
+                for h in range(4):
+                    k = x * 4 + h
+
+                    def at(row):
+                        return field[c * 8 + x * 4 + row, :, 128 * h : 128 * h + 128]
+
+                    if y == 3:
+                        above = hi_pack if k == 7 else pltpu.roll(hi_pack, 56 - 8 * k, 1)
+                    else:
+                        above = pltpu.roll(at(y + 1), 56, 1)
+                    if y == 0:
+                        below = lo_pack if k == 0 else pltpu.roll(lo_pack, 128 - 8 * k, 1)
+                    else:
+                        below = pltpu.roll(at(y - 1), 72, 1)
+                    g = at(y) + jnp.where(top, above, jnp.where(bottom, below, 0.0))
                     above = pltpu.roll(pltpu.roll(g, 7, 1), 15, 0)
                     below = pltpu.roll(pltpu.roll(g, 121, 1), 1, 0)
                     g = g + jnp.where(up_here, above, jnp.where(down_here, below, 0.0))
-                    out[c * 8 + x * 4 + y, :, 128 * h : 128 * h + 128] = g
+                    buf[c * 8 + x * 4 + y, :, 128 * h : 128 * h + 128] = g
+                start(c * 8 + x * 4 + y)
         return 0
 
     lax.fori_loop(0, 3, one_comp, 0)
 
 
-def unpack_kernel(block, d0, d1, d2, d3, drag):
+def inner_kernel(block, field, d0, d1, d2, d3, drag, out, drag_buf, buf, sem, drag_sem):
+    def copy(row):
+        return pltpu.make_async_copy(buf.at[row], out.at[row], sem.at[row])
+
+    last_passes(field, (1, 2), lambda c: None, lambda c: None, buf, lambda row: copy(row).start())
     for k, d in enumerate((d0, d1, d2, d3)):
 
         def one(r, _):
-            drag[pl.ds(block[k * SHARE + r], 3, stride=128), :] = d[pl.ds(r, 3, stride=32), :]
+            drag_buf[pl.ds(block[k * SHARE + r], 3, stride=128), :] = d[pl.ds(r, 3, stride=32), :]
             return 0
 
         lax.fori_loop(0, SHARE, one, 0, unroll=8)
+    moves = [
+        pltpu.make_async_copy(
+            drag_buf.at[pl.ds(96 * k, 96)], drag.at[pl.ds(96 * k, 96)], drag_sem.at[k]
+        )
+        for k in range(4)
+    ]
+    for move in moves:
+        move.start()
+    for row in range(24):
+        if row % 4 in (1, 2):
+            copy(row).wait()
+    for move in moves:
+        move.wait()
+
+
+def outer_kernel(field, got1, got3, _, out, buf, sem):
+    odd = (lax.axis_index("gy") & 1) == 1
+
+    def copy(row):
+        return pltpu.make_async_copy(buf.at[row], out.at[row], sem.at[row])
+
+    def face(c, first):
+        a = got1[pl.ds(16 * c, 16), :]
+        b = got3[pl.ds(16 * c, 16), :]
+        return jnp.where(odd, a, b) if first else jnp.where(odd, b, a)
+
+    last_passes(
+        field,
+        (0, 3),
+        lambda c: face(c, True),
+        lambda c: face(c, False),
+        buf,
+        lambda row: copy(row).start(),
+    )
+    for row in range(24):
+        if row % 4 in (0, 3):
+            copy(row).wait()
 
 
 def swapped(x, axis, partner):
@@ -375,10 +433,10 @@
     groups = [
         swapped(send[k * ROWS : (k + 1) * ROWS], "gy", lambda i, k=k: i ^ k) for k in range(1, N_GY)
     ]
-    field, parts, drag_own = call(
+    field, parts, drag_own, table = call(
         own_kernel,
-        [((8 * 384, 128), F32, "vmem"), ((8 * 576, 128), F32, "vmem"), ((96, 128), F32, "vmem")],
-        [(own_elem, "smem"), (own, "vmem"), (velocity.reshape(24, 16, 512), "hbm"), (nodes, "")],
+        [((8 * 24 * PITCH, 128), F32, "vmem"), ((8 * 36 * PITCH, 128), F32, "vmem"), ((96, 128), F32, "vmem"), (nodes.shape, F32, "vmem")],
+        [(own_elem, "smem"), (own, "vmem"), (velocity.reshape(24, 16, 512), "hbm"), (nodes, "hbm")],
         (VMEM((96, 128), F32),),
         flops=OWN_FLOPS,
     )
@@ -386,8 +444,8 @@
         rest_kernel,
         [((96, 128), F32, "vmem")] * 3
         + [((24, 16, 512), F32, "vmem")] * 2
-        + [((8 * 576, 128), F32, "vmem")],
-        [(g, "vmem") for g in groups] + [(field, "vmem"), (nodes, ""), (parts, "vmem")],
+        + [((8 * 36 * PITCH, 128), F32, "vmem")],
+        [(g, "vmem") for g in groups] + [(field, "vmem"), (table, "vmem"), (parts, "vmem")],
         (
             VMEM((96, 128), F32),
             VMEM((8, 128), jnp.int32),
@@ -407,16 +465,25 @@
     )
     got1 = swapped(faces[:48], "gy", lambda i: i ^ 1)
     got3 = lax.ppermute(faces[48:], "gy", [(1, 2), (2, 1)])
-    (drag,) = call(
-        unpack_kernel,
-        [((384, 128), F32, "")],
-        [(block, "smem"), (drag_own, "vmem")] + [(d, "vmem") for d in back],
+    grid = (24, 16, 512)
+    drag, out = call(
+        inner_kernel,
+        [((384, 128), F32, "raw"), (grid, F32, "raw")],
+        [(block, "smem"), (field, "vmem"), (drag_own, "vmem")] + [(d, "vmem") for d in back],
+        (
+            VMEM((384, 128), F32),
+            VMEM(grid, F32),
+            pltpu.SemaphoreType.DMA((24,)),
+            pltpu.SemaphoreType.DMA((4,)),
+        ),
         flops=UNPACK_FLOPS,
     )
     (out,) = call(
-        last_pass_kernel,
-        [((24, 16, 512), F32, "")],
-        [(field, "vmem"), (got1, "vmem"), (got3, "vmem")],
+        outer_kernel,
+        [(grid, F32, "raw")],
+        [(field, "vmem"), (got1, "vmem"), (got3, "vmem"), (out, "raw")],
+        (VMEM(grid, F32), pltpu.SemaphoreType.DMA((24,))),
+        aliases={3: 0},
     )
     return (
         drag.reshape(3, 128, 128).transpose(1, 0, 2),

time: 46.1 us -> 41.2 us (0.89)
  Pallas kernels: 21.9 us -> 17.3 us
  local copies, waits for them, and re-layouts: 0.98 us -> 0.1 us
    pallas_call x6, Pallas kernels: 21.9 us -> 17.3 us  [call(): pl.pallas_call(kernel, out_shape=shapes, in_specs=[pl.BlockSpec(memory_sp...]
    ppermute x9, waiting for transfers between devices: 5.96 us -> 7.06 us  [swapped(): return lax.ppermute(x, axis, pairs)]
    unnamed x2 -> x0, local copies, waits for them, and re-layouts: 0.89 us -> none
    ppermute x1, waiting for transfers between devices: 0.69 us -> 0.01 us  [body(): got3 = lax.ppermute(faces[48:], 'gy', [(1, 2), (2, 1)])]
  transfers between devices with their start and end apart: 10 -> 10, of which waited for: 5 -> 4; matrix products, arithmetic and copies ran while one was open for 0% -> 0% of each run, Pallas kernels for 13% -> 16%
where the time goes in v2:
time: 41.2 us; the launch traced here: 40.7 us
  Pallas kernels  17.3 us (42%)
  starting transfers between devices  15.5 us (38%)
  waiting for transfers between devices  7.06 us (17%)
  between operations  0.77 us (2%)
    pallas_call x6, Pallas kernels, call(): pl.pallas_call(kernel, out_shape=shapes, in_specs=[pl.BlockSpec(memory_sp...  17.3 us
    ppermute x9, starting transfers between devices, swapped(): return lax.ppermute(x, axis, pairs)  12.1 us
    ppermute x9, waiting for transfers between devices, swapped(): return lax.ppermute(x, axis, pairs)  7.06 us
    ppermute x1, starting transfers between devices, body(): got3 = lax.ppermute(faces[48:], 'gy', [(1, 2), (2, 1)])  3.41 us
  transfers between devices with their start and end apart: 10, of which 4 were waited for; matrix products, arithmetic and copies ran while one was open for 0% of the time, Pallas kernels for 16%

profile of v2, /device:TPU:18, one launch (start us, length us, event | category | flops | bytes accessed | tf_op | source)
XLA Modules:
  0.0 40.7 jit_solution(8792058086303530817)
XLA Ops:
  0.6 2.9 %shard_map.95 = (f32[1056,128]{1,0:T(8,128)S(1)}, s32[128]{0:T(128)S(1)}, s32[128]{0:T(128)S(1)}) custom-call(s32[128]{0:T(128)} %dest.1, s32[128]{0:T(128)} %counts.1, s32[128]{0:T(128)} %elem.1, f32[384,128]{1,0:T(8,128)} %bitcast.13, f32[384,128]{1,0:T(8,128)} %bitcast.14, f32[256,128]{1,0:T(8,128)} %bitcast.15), custom_call_target="tpu_custom_call" | custom-call | tf_op jit(solution)/shard_map/pallas_call | solution.py:69
  3.6 1.6 %collective-permute-start.2 = (f32[264,128]{1,0:T(8,128)S(1)}, f32[264,128]{1,0:T(8,128)S(1)}, u32[]{:S(2)}, u32[]{:S(2)}) collective-permute-start(f32[264,128]{1,0:T(8,128)S(1)} %get-tuple-element.37), channel_id=1, source_target_pairs={{0,3},{1,2},{2,1},{3,0},{4,7},{5,6},{6,5},{7,4},{8,11},{9,10},{10,... | collective-permute-start | bytes 405512 | tf_op jit(solution)/shard_map/ppermute | solution.py:419
  5.2 1.1 %collective-permute-start.1 = (f32[264,128]{1,0:T(8,128)S(1)}, f32[264,128]{1,0:T(8,128)S(1)}, u32[]{:S(2)}, u32[]{:S(2)}) collective-permute-start(f32[264,128]{1,0:T(8,128)S(1)} %get-tuple-element.38), channel_id=1, source_target_pairs={{0,2},{1,3},{2,0},{3,1},{4,6},{5,7},{6,4},{7,5},{8,10},{9,11},{10,... | collective-permute-start | bytes 405512 | tf_op jit(solution)/shard_map/ppermute | solution.py:419
  6.3 1.5 %collective-permute-start = (f32[264,128]{1,0:T(8,128)S(1)}, f32[264,128]{1,0:T(8,128)S(1)}, u32[]{:S(2)}, u32[]{:S(2)}) collective-permute-start(f32[264,128]{1,0:T(8,128)S(1)} %get-tuple-element.39), channel_id=1, source_target_pairs={{0,1},{1,0},{2,3},{3,2},{4,5},{5,4},{6,7},{7,6},{8,9},{9,8},{10,11... | collective-permute-start | bytes 405512 | tf_op jit(solution)/shard_map/ppermute | solution.py:419
  7.8 3.5 %shard_map.96 = (f32[3264,128]{1,0:T(8,128)S(1)}, f32[4896,128]{1,0:T(8,128)S(1)}, f32[96,128]{1,0:T(8,128)S(1)}, f32[168,128]{1,0:T(8,128)S(1)}) custom-call(s32[128]{0:T(128)S(1)} %get-tuple-element.20.elem, f32[264,128]{1,0:T(8,128)S(1)} %get-tuple-element.36.group, bf16[24,16,512]{2,1,0:T(8,128)(2,1)} %bitcast.16, f32[168,128]{1,0:T(8,128)} %constant.2.clone.nodes), custom_call_target="tpu_custom_call" | custom-call | flops 2000000000 | tf_op jit(solution)/shard_map/pallas_call | solution.py:69
  11.2 0.0 collective-permute-done.2.g3
  11.2 1.9 %collective-permute-done.1.g2 = f32[264,128]{1,0:T(8,128)S(1)} collective-permute-done((f32[264,128]{1,0:T(8,128)S(1)}, f32[264,128]{1,0:T(8,128)S(1)}, u32[]{:S(2)}, u32[]{:S(2)}) %collective-permute-start.1) | collective-permute-done | bytes 135200 | tf_op jit(solution)/shard_map/ppermute | solution.py:419
  13.1 0.6 %collective-permute-done.g1 = f32[264,128]{1,0:T(8,128)S(1)} collective-permute-done((f32[264,128]{1,0:T(8,128)S(1)}, f32[264,128]{1,0:T(8,128)S(1)}, u32[]{:S(2)}, u32[]{:S(2)}) %collective-permute-start) | collective-permute-done | bytes 135200 | tf_op jit(solution)/shard_map/ppermute | solution.py:419
  13.7 6.3 %shard_map.97 = (f32[96,128]{1,0:T(8,128)S(1)}, f32[96,128]{1,0:T(8,128)S(1)}, f32[96,128]{1,0:T(8,128)S(1)}, f32[24,16,512]{2,1,0:T(8,128)S(1)}, f32[24,16,512]{2,1,0:T(8,128)S(1)}, /*index=5*/f32[4896,128]{1,0:T(8,128)S(1)}) custom-call(f32[264,128]{1,0:T(8,128)S(1)} %collective-permute-done.g1, ...), custom_call_target="tpu_custom_call", output_to_operand_aliasing={{5}: (5, {})} | custom-call | tf_op jit(solution)/shard_map/pallas_call | solution.py:69
  20.0 0.1 fusion
  20.1 4.2 %collective-permute-start.4 = (f32[12,16,512]{2,1,0:T(8,128)S(1)}, f32[12,16,512]{2,1,0:T(8,128)S(1)}, u32[]{:S(2)}, u32[]{:S(2)}) collective-permute-start(f32[12,16,512]{2,1,0:T(8,128)S(1)} %get-tuple-element.34), channel_id=1, source_target_pairs={{4,8},{8,4},{12,16},{16,12},{20,24},{24,20},{28,32},{32,28},{36,40... | collective-permute-start | bytes 1179656 | tf_op jit(solution)/shard_map/ppermute | solution.py:419
  24.3 0.1 collective-permute-start.3
  24.4 1.0 %collective-permute-start.5 = (f32[96,128]{1,0:T(8,128)S(1)}, f32[96,128]{1,0:T(8,128)S(1)}, u32[]{:S(2)}, u32[]{:S(2)}) collective-permute-start(f32[96,128]{1,0:T(8,128)S(1)} %get-tuple-element.28), channel_id=1, source_target_pairs={{0,1},{1,0},{2,3},{3,2},{4,5},{5,4},{6,7},{7,6},{8,9},{9,8},{10,11... | collective-permute-start | bytes 147464 | tf_op jit(solution)/shard_map/ppermute | solution.py:419
  25.3 2.1 %collective-permute-start.6 = (f32[96,128]{1,0:T(8,128)S(1)}, f32[96,128]{1,0:T(8,128)S(1)}, u32[]{:S(2)}, u32[]{:S(2)}) collective-permute-start(f32[96,128]{1,0:T(8,128)S(1)} %get-tuple-element.29), channel_id=1, source_target_pairs={{0,2},{1,3},{2,0},{3,1},{4,6},{5,7},{6,4},{7,5},{8,10},{9,11},{10,... | collective-permute-start | bytes 147464 | tf_op jit(solution)/shard_map/ppermute | solution.py:419
  27.4 0.5 %collective-permute-start.7 = (f32[96,128]{1,0:T(8,128)S(1)}, f32[96,128]{1,0:T(8,128)S(1)}, u32[]{:S(2)}, u32[]{:S(2)}) collective-permute-start(f32[96,128]{1,0:T(8,128)S(1)} %get-tuple-element.30), channel_id=1, source_target_pairs={{0,3},{1,2},{2,1},{3,0},{4,7},{5,6},{6,5},{7,4},{8,11},{9,10},{10,... | collective-permute-start | bytes 147464 | tf_op jit(solution)/shard_map/ppermute | solution.py:419
  28.0 3.4 %collective-permute-done.4.refs_3_ = f32[12,16,512]{2,1,0:T(8,128)S(1)} collective-permute-done((f32[12,16,512]{2,1,0:T(8,128)S(1)}, f32[12,16,512]{2,1,0:T(8,128)S(1)}, u32[]{:S(2)}, u32[]{:S(2)}) %collective-permute-start.4) | collective-permute-done | bytes 393248 | tf_op jit(solution)/shard_map/ppermute | solution.py:419
  31.3 0.0 collective-permute-done.3.refs_2_
  31.3 0.4 %shard_map.98 = (f32[24,16,512]{2,1,0:T(8,128)S(1)}, f32[96,128]{1,0:T(8,128)S(1)}) custom-call(f32[24,16,512]{2,1,0:T(8,128)S(1)} %get-tuple-element.24.refs_0_, f32[24,16,512]{2,1,0:T(8,128)S(1)} %get-tuple-element.25.refs_1_, f32[12,16,512]{2,1,0:T(8,128)S(1)} %collective-permute-done.3.refs_2_, f32[12,16,512]{2,1,0:T(8,128)S(1)} %collective-permute-done.4.refs_3_), custom_call_target="tpu_custom_call" | custom-call | tf_op jit(solution)/shard_map/pallas_call | solution.py:69
  31.7 3.4 %collective-permute-start.9 = (f32[48,128]{1,0:T(8,128)S(1)}, f32[48,128]{1,0:T(8,128)S(1)}, u32[]{:S(2)}, u32[]{:S(2)}) collective-permute-start(f32[48,128]{1,0:T(8,128)S(1)} %get-tuple-element.40), channel_id=1, source_target_pairs={{1,2},{2,1},{5,6},{6,5},{9,10},{10,9},{13,14},{14,13},{17,18},{18,... | collective-permute-start | bytes 73736 | tf_op jit(solution)/shard_map/ppermute | solution.py:467
  35.2 0.1 collective-permute-start.8
  35.3 0.0 collective-permute-done.5.d1
  35.3 0.0 collective-permute-done.6.d2
  35.3 0.0 collective-permute-done.7.d3
  35.3 2.6 %shard_map.99 = (f32[384,128]{1,0:T(8,128)}, f32[24,16,512]{2,1,0:T(8,128)}) custom-call(s32[128]{0:T(128)S(1)} %get-tuple-element.18.block, f32[24,16,512]{2,1,0:T(8,128)S(1)} %get-tuple-element.26.field, f32[96,128]{1,0:T(8,128)S(1)} %get-tuple-element.27.d0, f32[96,128]{1,0:T(8,128)S(1)} %collective-permute-done.5.d1, ...), custom_call_target="tpu_custom_call" | custom-call | flops 1000000000 | tf_op jit(solution)/shard_map/pallas_call | solution.py:69
  37.9 0.0 collective-permute-done.9.got3
  37.9 1.2 %collective-permute-done.8.got1 = f32[48,128]{1,0:T(8,128)S(1)} collective-permute-done((f32[48,128]{1,0:T(8,128)S(1)}, f32[48,128]{1,0:T(8,128)S(1)}, u32[]{:S(2)}, u32[]{:S(2)}) %collective-permute-start.8) | collective-permute-done | bytes 24608 | tf_op jit(solution)/shard_map/ppermute | solution.py:419
  39.1 1.7 %shard_map.100 = f32[24,16,512]{2,1,0:T(8,128)} custom-call(f32[24,16,512]{2,1,0:T(8,128)S(1)} %get-tuple-element.26.field, f32[48,128]{1,0:T(8,128)S(1)} %collective-permute-done.8.got1, f32[48,128]{1,0:T(8,128)S(1)} %collective-permute-done.9.got3, f32[24,16,512]{2,1,0:T(8,128)} %get-tuple-element.33._), custom_call_target="tpu_custom_call", output_to_operand_aliasing={{}: (3, {})} | custom-call | tf_op jit(solution)/shard_map/pallas_call | solution.py:69
  (2 shorter events, 0.0 us)
Async XLA Ops:
  3.6 7.6 %collective-permute-start.2 = (f32[264,128]{1,0:T(8,128)S(1)}, f32[264,128]{1,0:T(8,128)S(1)}, u32[]{:S(2)}, u32[]{:S(2)}) collective-permute-start(f32[264,128]{1,0:T(8,128)S(1)} %get-tuple-element.37), channel_id=1, source_target_pairs={{0,3},{1,2},{2,1},{3,0},{4,7},{5,6},{6,5},{7,4},{8,11},{9,10},{10,... | collective-permute-start | bytes 405512 | tf_op jit(solution)/shard_map/ppermute | solution.py:419
  5.2 8.0 %collective-permute-start.1 = (f32[264,128]{1,0:T(8,128)S(1)}, f32[264,128]{1,0:T(8,128)S(1)}, u32[]{:S(2)}, u32[]{:S(2)}) collective-permute-start(f32[264,128]{1,0:T(8,128)S(1)} %get-tuple-element.38), channel_id=1, source_target_pairs={{0,2},{1,3},{2,0},{3,1},{4,6},{5,7},{6,4},{7,5},{8,10},{9,11},{10,... | collective-permute-start | bytes 405512 | tf_op jit(solution)/shard_map/ppermute | solution.py:419
  6.3 7.5 %collective-permute-start = (f32[264,128]{1,0:T(8,128)S(1)}, f32[264,128]{1,0:T(8,128)S(1)}, u32[]{:S(2)}, u32[]{:S(2)}) collective-permute-start(f32[264,128]{1,0:T(8,128)S(1)} %get-tuple-element.39), channel_id=1, source_target_pairs={{0,1},{1,0},{2,3},{3,2},{4,5},{5,4},{6,7},{7,6},{8,9},{9,8},{10,11... | collective-permute-start | bytes 405512 | tf_op jit(solution)/shard_map/ppermute | solution.py:419
  20.1 11.2 %collective-permute-start.4 = (f32[12,16,512]{2,1,0:T(8,128)S(1)}, f32[12,16,512]{2,1,0:T(8,128)S(1)}, u32[]{:S(2)}, u32[]{:S(2)}) collective-permute-start(f32[12,16,512]{2,1,0:T(8,128)S(1)} %get-tuple-element.34), channel_id=1, source_target_pairs={{4,8},{8,4},{12,16},{16,12},{20,24},{24,20},{28,32},{32,28},{36,40... | collective-permute-start | bytes 1179656 | tf_op jit(solution)/shard_map/ppermute | solution.py:419
  24.3 7.0 %collective-permute-start.3 = (f32[12,16,512]{2,1,0:T(8,128)S(1)}, f32[12,16,512]{2,1,0:T(8,128)S(1)}, u32[]{:S(2)}, u32[]{:S(2)}) collective-permute-start(f32[12,16,512]{2,1,0:T(8,128)S(1)} %get-tuple-element.35), channel_id=1, source_target_pairs={{0,4},{4,0},{8,12},{12,8},{16,20},{20,16},{24,28},{28,24},{32,36},... | collective-permute-start | bytes 1179656 | tf_op jit(solution)/shard_map/ppermute | solution.py:419
  24.4 10.9 %collective-permute-start.5 = (f32[96,128]{1,0:T(8,128)S(1)}, f32[96,128]{1,0:T(8,128)S(1)}, u32[]{:S(2)}, u32[]{:S(2)}) collective-permute-start(f32[96,128]{1,0:T(8,128)S(1)} %get-tuple-element.28), channel_id=1, source_target_pairs={{0,1},{1,0},{2,3},{3,2},{4,5},{5,4},{6,7},{7,6},{8,9},{9,8},{10,11... | collective-permute-start | bytes 147464 | tf_op jit(solution)/shard_map/ppermute | solution.py:419
  25.3 9.9 %collective-permute-start.6 = (f32[96,128]{1,0:T(8,128)S(1)}, f32[96,128]{1,0:T(8,128)S(1)}, u32[]{:S(2)}, u32[]{:S(2)}) collective-permute-start(f32[96,128]{1,0:T(8,128)S(1)} %get-tuple-element.29), channel_id=1, source_target_pairs={{0,2},{1,3},{2,0},{3,1},{4,6},{5,7},{6,4},{7,5},{8,10},{9,11},{10,... | collective-permute-start | bytes 147464 | tf_op jit(solution)/shard_map/ppermute | solution.py:419
  27.4 7.9 %collective-permute-start.7 = (f32[96,128]{1,0:T(8,128)S(1)}, f32[96,128]{1,0:T(8,128)S(1)}, u32[]{:S(2)}, u32[]{:S(2)}) collective-permute-start(f32[96,128]{1,0:T(8,128)S(1)} %get-tuple-element.30), channel_id=1, source_target_pairs={{0,3},{1,2},{2,1},{3,0},{4,7},{5,6},{6,5},{7,4},{8,11},{9,10},{10,... | collective-permute-start | bytes 147464 | tf_op jit(solution)/shard_map/ppermute | solution.py:419
  31.7 6.1 %collective-permute-start.9 = (f32[48,128]{1,0:T(8,128)S(1)}, f32[48,128]{1,0:T(8,128)S(1)}, u32[]{:S(2)}, u32[]{:S(2)}) collective-permute-start(f32[48,128]{1,0:T(8,128)S(1)} %get-tuple-element.40), channel_id=1, source_target_pairs={{1,2},{2,1},{5,6},{6,5},{9,10},{10,9},{13,14},{14,13},{17,18},{18,... | collective-permute-start | bytes 73736 | tf_op jit(solution)/shard_map/ppermute | solution.py:467
  35.2 3.9 %collective-permute-start.8 = (f32[48,128]{1,0:T(8,128)S(1)}, f32[48,128]{1,0:T(8,128)S(1)}, u32[]{:S(2)}, u32[]{:S(2)}) collective-permute-start(f32[48,128]{1,0:T(8,128)S(1)} %get-tuple-element.41), channel_id=1, source_target_pairs={{0,1},{1,0},{2,3},{3,2},{4,5},{5,4},{6,7},{7,6},{8,9},{9,8},{10,11... | collective-permute-start | bytes 73736 | tf_op jit(solution)/shard_map/ppermute | solution.py:419

commit v3 on v2

--- a/solution.py
+++ b/solution.py
@@ -44,6 +44,7 @@
 
 
 PITCH = 17
+ORDER = (3, 1, 2)
 UNROLL_A = 16
 UNROLL_B = 16
 OWN_FLOPS = 2_000_000_000
@@ -83,7 +84,28 @@
     return lax.broadcasted_iota(jnp.int32, shape, len(shape) - 1)
 
 
-def pack_kernel(dest, counts, elem, pos, vel, coef, send, block, own_elem):
+def pack_kernel(
+    dest_hbm, counts_hbm, elem_hbm, pos_hbm, vel_hbm, coef_hbm,
+    send, block, own_elem,
+    dest, counts, elem, pos, vel, coef, sem,
+):
+    tables = [
+        pltpu.make_async_copy(a, b, sem.at[k])
+        for k, (a, b) in enumerate(((dest_hbm, dest), (counts_hbm, counts), (elem_hbm, elem)))
+    ]
+    halves = []
+    for k in range(2):
+        cut = pl.ds(64 * k, 64)
+        pairs = (
+            (pos_hbm.at[:, cut], pos.at[:, cut]),
+            (vel_hbm.at[:, cut], vel.at[:, cut]),
+            (coef_hbm.at[pl.ds(128 * k, 128)], coef.at[pl.ds(128 * k, 128)]),
+        )
+        halves.append(
+            [pltpu.make_async_copy(a, b, sem.at[3 + 3 * k + n]) for n, (a, b) in enumerate(pairs)]
+        )
+    for copy in tables + halves[0] + halves[1]:
+        copy.start()
     me = lax.axis_index("gy")
     lane = lanes()
     ids = lax.broadcasted_iota(jnp.int32, (8, 128), 0) * 128 + lanes((8, 128))
@@ -92,19 +114,26 @@
         taken, labels = state
         d = dest[b] ^ me
         r = (taken >> (8 * d)) & 255
+        e = elem[b]
         block[d * SHARE + r] = b
+        own_elem[d * SHARE + r] = e
         base = d * ROWS + r
-        send[pl.ds(base, 3, stride=32), :] = pos[pl.ds(b, 3, stride=128), :]
-        send[pl.ds(base + 96, 3, stride=32), :] = vel[pl.ds(b, 3, stride=128), :]
+        send[pl.ds(base, 3, stride=32), :] = pos[:, b, :]
+        send[pl.ds(base + 96, 3, stride=32), :] = vel[:, b, :]
         rate = coef[pl.ds(2 * b, 1), :]
         send[pl.ds(base + 192, 1), :] = jnp.where(lane < counts[b], rate, 0.0)
         send[pl.ds(base + 224, 1), :] = coef[pl.ds(2 * b + 1, 1), :]
-        own_elem[d * SHARE + r] = elem[b]
-        labels = jnp.where(ids == d * 128 + r, elem[b], labels)
+        labels = jnp.where(ids == d * 128 + r, e, labels)
         return (taken + (1 << (8 * d)), labels)
 
-    _, labels = lax.fori_loop(0, 128, one, (jnp.int32(0), jnp.zeros((8, 128), jnp.int32)), unroll=8)
-    labels = labels.astype(F32)
+    state = (jnp.int32(0), jnp.zeros((8, 128), jnp.int32))
+    for copy in tables:
+        copy.wait()
+    for k in range(2):
+        for copy in halves[k]:
+            copy.wait()
+        state = lax.fori_loop(64 * k, 64 * k + 64, one, state, unroll=8)
+    labels = state[1].astype(F32)
     for d in range(N_GY):
         send[d * ROWS + 256 : d * ROWS + 264, :] = jnp.broadcast_to(labels[d : d + 1, :], (8, 128))
 
@@ -299,8 +328,13 @@
             pair = [(cut(near, c * 4 + y, h), cut(far, c * 4 + y, h)) for h in range(4)]
             got_lo = [jnp.where(odd, n, f) for n, f in pair]
             got_hi = [jnp.where(odd, f, n) for n, f in pair]
-            lower = [cut(inside, c * 8 + y, h) + got_lo[h] for h in range(4)]
-            upper = [cut(inside, c * 8 + 4 + y, h) + got_hi[h] for h in range(4)]
+            lower = [
+                cut(inside, c * 8 + y, h) + jnp.where(has_before, got_lo[h], 0.0) for h in range(4)
+            ]
+            upper = [
+                cut(inside, c * 8 + 4 + y, h) + jnp.where(has_after, got_hi[h], 0.0)
+                for h in range(4)
+            ]
             first = got_lo[0] + pltpu.roll(cut(sent, to_lo + c * 4 + y, 3), 64, 1)
             last = got_hi[3] + pltpu.roll(cut(sent, to_hi + c * 4 + y, 0), 64, 1)
             low3, up0 = lower[3], upper[0]
@@ -390,14 +424,16 @@
 
 
 def outer_kernel(field, got1, got3, _, out, buf, sem):
-    odd = (lax.axis_index("gy") & 1) == 1
+    gy = lax.axis_index("gy")
+    odd = (gy & 1) == 1
+    between = (gy > 0) & (gy < N_GY - 1)
 
     def copy(row):
         return pltpu.make_async_copy(buf.at[row], out.at[row], sem.at[row])
 
     def face(c, first):
         a = got1[pl.ds(16 * c, 16), :]
-        b = got3[pl.ds(16 * c, 16), :]
+        b = jnp.where(between, got3[pl.ds(16 * c, 16), :], 0.0)
         return jnp.where(odd, a, b) if first else jnp.where(odd, b, a)
 
     last_passes(
@@ -415,24 +451,26 @@
 
 def swapped(x, axis, partner):
     count = lax.axis_size(axis)
-    pairs = [(i, partner(i)) for i in range(count) if 0 <= partner(i) < count]
-    return lax.ppermute(x, axis, pairs)
+    return lax.ppermute(x, axis, [(i, partner(i) % count) for i in range(count)])
 
 
 def body(velocity, part_pos, part_vel, part_coef, counts, dest, elem):
-    pos = part_pos.transpose(1, 0, 2).reshape(384, 128)
-    vel = part_vel.transpose(1, 0, 2).reshape(384, 128)
+    pos = part_pos.transpose(1, 0, 2)
+    vel = part_vel.transpose(1, 0, 2)
     coef = part_coef.reshape(256, 128)
     nodes = jnp.asarray(node_table())
     send, block, own_elem = call(
         pack_kernel,
         [((N_GY * ROWS, 128), F32, "vmem"), ((128,), jnp.int32, "smem"), ((128,), jnp.int32, "smem")],
-        [(dest, "table"), (counts, "table"), (elem, "table"), (pos, "hbm"), (vel, "hbm"), (coef, "hbm")],
+        [(a, "raw") for a in (dest, counts, elem, pos, vel, coef)],
+        (SMEM((128,), jnp.int32),) * 3
+        + (VMEM(pos.shape, F32),) * 2
+        + (VMEM(coef.shape, F32), pltpu.SemaphoreType.DMA((9,))),
     )
     own = send[:ROWS]
-    groups = [
-        swapped(send[k * ROWS : (k + 1) * ROWS], "gy", lambda i, k=k: i ^ k) for k in range(1, N_GY)
-    ]
+    groups = {
+        k: swapped(send[k * ROWS : (k + 1) * ROWS], "gy", lambda i, k=k: i ^ k) for k in ORDER
+    }
     field, parts, drag_own, table = call(
         own_kernel,
         [((8 * 24 * PITCH, 128), F32, "vmem"), ((8 * 36 * PITCH, 128), F32, "vmem"), ((96, 128), F32, "vmem"), (nodes.shape, F32, "vmem")],
@@ -445,7 +483,7 @@
         [((96, 128), F32, "vmem")] * 3
         + [((24, 16, 512), F32, "vmem")] * 2
         + [((8 * 36 * PITCH, 128), F32, "vmem")],
-        [(g, "vmem") for g in groups] + [(field, "vmem"), (table, "vmem"), (parts, "vmem")],
+        [(groups[k], "vmem") for k in ORDER] + [(field, "vmem"), (table, "vmem"), (parts, "vmem")],
         (
             VMEM((96, 128), F32),
             VMEM((8, 128), jnp.int32),
@@ -456,7 +494,7 @@
     )
     far = swapped(ghosts[12:], "gx", lambda i: i + 1 if i & 1 else i - 1)
     near = swapped(ghosts[:12], "gx", lambda i: i ^ 1)
-    back = [swapped(d, "gy", lambda i, k=k: i ^ k) for k, d in enumerate(drags, 1)]
+    back = {k: swapped(d, "gy", lambda i, k=k: i ^ k) for k, d in zip(ORDER, drags)}
     last_gx = lax.axis_size("gx") - 1
     field, faces = call(
         lambda *refs: first_pass_kernel(last_gx, *refs),
@@ -464,12 +502,12 @@
         [(inside, "vmem"), (ghosts, "vmem"), (near, "vmem"), (far, "vmem")],
     )
     got1 = swapped(faces[:48], "gy", lambda i: i ^ 1)
-    got3 = lax.ppermute(faces[48:], "gy", [(1, 2), (2, 1)])
+    got3 = swapped(faces[48:], "gy", lambda i: i ^ 3)
     grid = (24, 16, 512)
     drag, out = call(
         inner_kernel,
         [((384, 128), F32, "raw"), (grid, F32, "raw")],
-        [(block, "smem"), (field, "vmem"), (drag_own, "vmem")] + [(d, "vmem") for d in back],
+        [(block, "smem"), (field, "vmem"), (drag_own, "vmem")] + [(back[k], "vmem") for k in range(1, N_GY)],
         (
             VMEM((384, 128), F32),
             VMEM(grid, F32),

time: 41.2 us -> 40.1 us (0.973)
  the two profiles are of different devices: /device:TPU:18 before, /device:TPU:0 now
where the time goes in v3:
time: 40.1 us; the launch traced here: 39.9 us
  starting transfers between devices  17.9 us (45%)
  Pallas kernels  17.1 us (43%)
  waiting for transfers between devices  4.11 us (10%)
  between operations  0.72 us (2%)
    ppermute x10, starting transfers between devices, swapped(): lax.ppermute(x, axis, [(i, partner(i) % count) for i in range(count)])  17.9 us
    pallas_call x6, Pallas kernels, call(): pl.pallas_call(kernel, out_shape=shapes, in_specs=[pl.BlockSpec(memory_sp...  17.1 us
    ppermute x10, waiting for transfers between devices, swapped(): lax.ppermute(x, axis, [(i, partner(i) % count) for i in range(count)])  4.11 us
  transfers between devices with their start and end apart: 10, of which 5 were waited for; matrix products, arithmetic and copies ran while one was open for 0% of the time, Pallas kernels for 16%

profile of v3, /device:TPU:0, one launch (start us, length us, event | category | flops | bytes accessed | tf_op | source)
XLA Modules:
  0.0 39.9 jit_solution(13323457861066941334)
XLA Ops:
  0.6 2.7 %shard_map.95 = (f32[1056,128]{1,0:T(8,128)S(1)}, s32[128]{0:T(128)S(1)}, s32[128]{0:T(128)S(1)}) custom-call(s32[128]{0:T(128)} %dest_hbm.1, s32[128]{0:T(128)} %counts_hbm.1, s32[128]{0:T(128)} %elem_hbm.1, f32[3,128,128]{2,1,0:T(8,128)} %bitcast.9, f32[3,128,128]{2,1,0:T(8,128)} %bitcast.10, f32[256,128]{1,0:T(8,128)} %bitcast.11), custom_call_target="tpu_custom_call" | custom-call | tf_op jit(solution)/shard_map/pallas_call | solution.py:70
  3.4 3.2 %collective-permute-start.2 = (f32[264,128]{1,0:T(8,128)S(1)}, f32[264,128]{1,0:T(8,128)S(1)}, u32[]{:S(2)}, u32[]{:S(2)}) collective-permute-start(f32[264,128]{1,0:T(8,128)S(1)} %get-tuple-element.37), channel_id=1, source_target_pairs={{0,2},{1,3},{2,0},{3,1},{4,6},{5,7},{6,4},{7,5},{8,10},{9,11},{10,... | collective-permute-start | bytes 405512 | tf_op jit(solution)/shard_map/ppermute | solution.py:454
  6.6 0.6 %collective-permute-start.1 = (f32[264,128]{1,0:T(8,128)S(1)}, f32[264,128]{1,0:T(8,128)S(1)}, u32[]{:S(2)}, u32[]{:S(2)}) collective-permute-start(f32[264,128]{1,0:T(8,128)S(1)} %get-tuple-element.38), channel_id=1, source_target_pairs={{0,1},{1,0},{2,3},{3,2},{4,5},{5,4},{6,7},{7,6},{8,9},{9,8},{10,11... | collective-permute-start | bytes 405512 | tf_op jit(solution)/shard_map/ppermute | solution.py:454
  7.2 0.6 %collective-permute-start = (f32[264,128]{1,0:T(8,128)S(1)}, f32[264,128]{1,0:T(8,128)S(1)}, u32[]{:S(2)}, u32[]{:S(2)}) collective-permute-start(f32[264,128]{1,0:T(8,128)S(1)} %get-tuple-element.39), channel_id=1, source_target_pairs={{0,3},{1,2},{2,1},{3,0},{4,7},{5,6},{6,5},{7,4},{8,11},{9,10},{10,... | collective-permute-start | bytes 405512 | tf_op jit(solution)/shard_map/ppermute | solution.py:454
  7.7 3.5 %shard_map.96 = (f32[3264,128]{1,0:T(8,128)S(1)}, f32[4896,128]{1,0:T(8,128)S(1)}, f32[96,128]{1,0:T(8,128)S(1)}, f32[168,128]{1,0:T(8,128)S(1)}) custom-call(s32[128]{0:T(128)S(1)} %get-tuple-element.20.elem, f32[264,128]{1,0:T(8,128)S(1)} %get-tuple-element.36.group, bf16[24,16,512]{2,1,0:T(8,128)(2,1)} %bitcast.12, f32[168,128]{1,0:T(8,128)} %constant.2.clone.nodes), custom_call_target="tpu_custom_call" | custom-call | flops 2000000000 | tf_op jit(solution)/shard_map/pallas_call | solution.py:70
  11.2 0.0 collective-permute-done.2.g3
  11.2 2.2 %collective-permute-done.1.g2 = f32[264,128]{1,0:T(8,128)S(1)} collective-permute-done((f32[264,128]{1,0:T(8,128)S(1)}, f32[264,128]{1,0:T(8,128)S(1)}, u32[]{:S(2)}, u32[]{:S(2)}) %collective-permute-start.1) | collective-permute-done | bytes 135200 | tf_op jit(solution)/shard_map/ppermute | solution.py:454
  13.4 0.2 collective-permute-done.g1
  13.5 6.3 %shard_map.97 = (f32[96,128]{1,0:T(8,128)S(1)}, f32[96,128]{1,0:T(8,128)S(1)}, f32[96,128]{1,0:T(8,128)S(1)}, f32[24,16,512]{2,1,0:T(8,128)S(1)}, f32[24,16,512]{2,1,0:T(8,128)S(1)}, /*index=5*/f32[4896,128]{1,0:T(8,128)S(1)}) custom-call(f32[264,128]{1,0:T(8,128)S(1)} %collective-permute-done.g1, ...), custom_call_target="tpu_custom_call", output_to_operand_aliasing={{5}: (5, {})} | custom-call | tf_op jit(solution)/shard_map/pallas_call | solution.py:70
  19.9 0.1 fusion
  19.9 5.4 %collective-permute-start.4 = (f32[12,16,512]{2,1,0:T(8,128)S(1)}, f32[12,16,512]{2,1,0:T(8,128)S(1)}, u32[]{:S(2)}, u32[]{:S(2)}) collective-permute-start(f32[12,16,512]{2,1,0:T(8,128)S(1)} %get-tuple-element.34), channel_id=1, source_target_pairs={{0,124},{4,8},{8,4},{12,16},{16,12},{20,24},{24,20},{28,32},{32,28... | collective-permute-start | bytes 1179656 | tf_op jit(solution)/shard_map/ppermute | solution.py:454
  25.3 0.0 collective-permute-start.3
  25.3 1.4 %collective-permute-start.5 = (f32[96,128]{1,0:T(8,128)S(1)}, f32[96,128]{1,0:T(8,128)S(1)}, u32[]{:S(2)}, u32[]{:S(2)}) collective-permute-start(f32[96,128]{1,0:T(8,128)S(1)} %get-tuple-element.28), channel_id=1, source_target_pairs={{0,1},{1,0},{2,3},{3,2},{4,5},{5,4},{6,7},{7,6},{8,9},{9,8},{10,11... | collective-permute-start | bytes 147464 | tf_op jit(solution)/shard_map/ppermute | solution.py:454
  26.7 3.2 %collective-permute-start.6 = (f32[96,128]{1,0:T(8,128)S(1)}, f32[96,128]{1,0:T(8,128)S(1)}, u32[]{:S(2)}, u32[]{:S(2)}) collective-permute-start(f32[96,128]{1,0:T(8,128)S(1)} %get-tuple-element.29), channel_id=1, source_target_pairs={{0,2},{1,3},{2,0},{3,1},{4,6},{5,7},{6,4},{7,5},{8,10},{9,11},{10,... | collective-permute-start | bytes 147464 | tf_op jit(solution)/shard_map/ppermute | solution.py:454
  29.9 0.1 collective-permute-start.7
  30.0 0.8 %collective-permute-done.4.refs_3_ = f32[12,16,512]{2,1,0:T(8,128)S(1)} collective-permute-done((f32[12,16,512]{2,1,0:T(8,128)S(1)}, f32[12,16,512]{2,1,0:T(8,128)S(1)}, u32[]{:S(2)}, u32[]{:S(2)}) %collective-permute-start.4) | collective-permute-done | bytes 393248 | tf_op jit(solution)/shard_map/ppermute | solution.py:454
  30.8 0.0 collective-permute-done.3.refs_2_
  30.8 0.4 %shard_map.98 = (f32[24,16,512]{2,1,0:T(8,128)S(1)}, f32[96,128]{1,0:T(8,128)S(1)}) custom-call(f32[24,16,512]{2,1,0:T(8,128)S(1)} %get-tuple-element.24.refs_0_, f32[24,16,512]{2,1,0:T(8,128)S(1)} %get-tuple-element.25.refs_1_, f32[12,16,512]{2,1,0:T(8,128)S(1)} %collective-permute-done.3.refs_2_, f32[12,16,512]{2,1,0:T(8,128)S(1)} %collective-permute-done.4.refs_3_), custom_call_target="tpu_custom_call" | custom-call | tf_op jit(solution)/shard_map/pallas_call | solution.py:70
  31.2 3.2 %collective-permute-start.9 = (f32[48,128]{1,0:T(8,128)S(1)}, f32[48,128]{1,0:T(8,128)S(1)}, u32[]{:S(2)}, u32[]{:S(2)}) collective-permute-start(f32[48,128]{1,0:T(8,128)S(1)} %get-tuple-element.40), channel_id=1, source_target_pairs={{0,3},{1,2},{2,1},{3,0},{4,7},{5,6},{6,5},{7,4},{8,11},{9,10},{10,... | collective-permute-start | bytes 73736 | tf_op jit(solution)/shard_map/ppermute | solution.py:454
  34.4 0.2 collective-permute-start.8
  34.7 0.0 collective-permute-done.5.d1
  34.7 0.0 collective-permute-done.6.d2
  34.7 0.5 %collective-permute-done.7.d3 = f32[96,128]{1,0:T(8,128)S(1)} collective-permute-done((f32[96,128]{1,0:T(8,128)S(1)}, f32[96,128]{1,0:T(8,128)S(1)}, u32[]{:S(2)}, u32[]{:S(2)}) %collective-permute-start.7) | collective-permute-done | bytes 49184 | tf_op jit(solution)/shard_map/ppermute | solution.py:454
  35.2 2.6 %shard_map.99 = (f32[384,128]{1,0:T(8,128)}, f32[24,16,512]{2,1,0:T(8,128)}) custom-call(s32[128]{0:T(128)S(1)} %get-tuple-element.18.block, f32[24,16,512]{2,1,0:T(8,128)S(1)} %get-tuple-element.26.field, f32[96,128]{1,0:T(8,128)S(1)} %get-tuple-element.27.d0, f32[96,128]{1,0:T(8,128)S(1)} %collective-permute-done.5.d1, ...), custom_call_target="tpu_custom_call" | custom-call | flops 1000000000 | tf_op jit(solution)/shard_map/pallas_call | solution.py:70
  37.8 0.0 collective-permute-done.9.got3
  37.8 0.5 %collective-permute-done.8.got1 = f32[48,128]{1,0:T(8,128)S(1)} collective-permute-done((f32[48,128]{1,0:T(8,128)S(1)}, f32[48,128]{1,0:T(8,128)S(1)}, u32[]{:S(2)}, u32[]{:S(2)}) %collective-permute-start.8) | collective-permute-done | bytes 24608 | tf_op jit(solution)/shard_map/ppermute | solution.py:454
  38.3 1.7 %shard_map.100 = f32[24,16,512]{2,1,0:T(8,128)} custom-call(f32[24,16,512]{2,1,0:T(8,128)S(1)} %get-tuple-element.26.field, f32[48,128]{1,0:T(8,128)S(1)} %collective-permute-done.8.got1, f32[48,128]{1,0:T(8,128)S(1)} %collective-permute-done.9.got3, f32[24,16,512]{2,1,0:T(8,128)} %get-tuple-element.33._), custom_call_target="tpu_custom_call", output_to_operand_aliasing={{}: (3, {})} | custom-call | tf_op jit(solution)/shard_map/pallas_call | solution.py:70
  (2 shorter events, 0.0 us)
Async XLA Ops:
  3.4 7.8 %collective-permute-start.2 = (f32[264,128]{1,0:T(8,128)S(1)}, f32[264,128]{1,0:T(8,128)S(1)}, u32[]{:S(2)}, u32[]{:S(2)}) collective-permute-start(f32[264,128]{1,0:T(8,128)S(1)} %get-tuple-element.37), channel_id=1, source_target_pairs={{0,2},{1,3},{2,0},{3,1},{4,6},{5,7},{6,4},{7,5},{8,10},{9,11},{10,... | collective-permute-start | bytes 405512 | tf_op jit(solution)/shard_map/ppermute | solution.py:454
  6.6 6.8 %collective-permute-start.1 = (f32[264,128]{1,0:T(8,128)S(1)}, f32[264,128]{1,0:T(8,128)S(1)}, u32[]{:S(2)}, u32[]{:S(2)}) collective-permute-start(f32[264,128]{1,0:T(8,128)S(1)} %get-tuple-element.38), channel_id=1, source_target_pairs={{0,1},{1,0},{2,3},{3,2},{4,5},{5,4},{6,7},{7,6},{8,9},{9,8},{10,11... | collective-permute-start | bytes 405512 | tf_op jit(solution)/shard_map/ppermute | solution.py:454
  7.2 6.4 %collective-permute-start = (f32[264,128]{1,0:T(8,128)S(1)}, f32[264,128]{1,0:T(8,128)S(1)}, u32[]{:S(2)}, u32[]{:S(2)}) collective-permute-start(f32[264,128]{1,0:T(8,128)S(1)} %get-tuple-element.39), channel_id=1, source_target_pairs={{0,3},{1,2},{2,1},{3,0},{4,7},{5,6},{6,5},{7,4},{8,11},{9,10},{10,... | collective-permute-start | bytes 405512 | tf_op jit(solution)/shard_map/ppermute | solution.py:454
  19.9 10.9 %collective-permute-start.4 = (f32[12,16,512]{2,1,0:T(8,128)S(1)}, f32[12,16,512]{2,1,0:T(8,128)S(1)}, u32[]{:S(2)}, u32[]{:S(2)}) collective-permute-start(f32[12,16,512]{2,1,0:T(8,128)S(1)} %get-tuple-element.34), channel_id=1, source_target_pairs={{0,124},{4,8},{8,4},{12,16},{16,12},{20,24},{24,20},{28,32},{32,28... | collective-permute-start | bytes 1179656 | tf_op jit(solution)/shard_map/ppermute | solution.py:454
  25.3 5.5 %collective-permute-start.3 = (f32[12,16,512]{2,1,0:T(8,128)S(1)}, f32[12,16,512]{2,1,0:T(8,128)S(1)}, u32[]{:S(2)}, u32[]{:S(2)}) collective-permute-start(f32[12,16,512]{2,1,0:T(8,128)S(1)} %get-tuple-element.35), channel_id=1, source_target_pairs={{0,4},{4,0},{8,12},{12,8},{16,20},{20,16},{24,28},{28,24},{32,36},... | collective-permute-start | bytes 1179656 | tf_op jit(solution)/shard_map/ppermute | solution.py:454
  25.3 9.4 %collective-permute-start.5 = (f32[96,128]{1,0:T(8,128)S(1)}, f32[96,128]{1,0:T(8,128)S(1)}, u32[]{:S(2)}, u32[]{:S(2)}) collective-permute-start(f32[96,128]{1,0:T(8,128)S(1)} %get-tuple-element.28), channel_id=1, source_target_pairs={{0,1},{1,0},{2,3},{3,2},{4,5},{5,4},{6,7},{7,6},{8,9},{9,8},{10,11... | collective-permute-start | bytes 147464 | tf_op jit(solution)/shard_map/ppermute | solution.py:454
  26.7 8.0 %collective-permute-start.6 = (f32[96,128]{1,0:T(8,128)S(1)}, f32[96,128]{1,0:T(8,128)S(1)}, u32[]{:S(2)}, u32[]{:S(2)}) collective-permute-start(f32[96,128]{1,0:T(8,128)S(1)} %get-tuple-element.29), channel_id=1, source_target_pairs={{0,2},{1,3},{2,0},{3,1},{4,6},{5,7},{6,4},{7,5},{8,10},{9,11},{10,... | collective-permute-start | bytes 147464 | tf_op jit(solution)/shard_map/ppermute | solution.py:454
  29.9 5.3 %collective-permute-start.7 = (f32[96,128]{1,0:T(8,128)S(1)}, f32[96,128]{1,0:T(8,128)S(1)}, u32[]{:S(2)}, u32[]{:S(2)}) collective-permute-start(f32[96,128]{1,0:T(8,128)S(1)} %get-tuple-element.30), channel_id=1, source_target_pairs={{0,3},{1,2},{2,1},{3,0},{4,7},{5,6},{6,5},{7,4},{8,11},{9,10},{10,... | collective-permute-start | bytes 147464 | tf_op jit(solution)/shard_map/ppermute | solution.py:454
  31.2 6.6 %collective-permute-start.9 = (f32[48,128]{1,0:T(8,128)S(1)}, f32[48,128]{1,0:T(8,128)S(1)}, u32[]{:S(2)}, u32[]{:S(2)}) collective-permute-start(f32[48,128]{1,0:T(8,128)S(1)} %get-tuple-element.40), channel_id=1, source_target_pairs={{0,3},{1,2},{2,1},{3,0},{4,7},{5,6},{6,5},{7,4},{8,11},{9,10},{10,... | collective-permute-start | bytes 73736 | tf_op jit(solution)/shard_map/ppermute | solution.py:454
  34.4 3.8 %collective-permute-start.8 = (f32[48,128]{1,0:T(8,128)S(1)}, f32[48,128]{1,0:T(8,128)S(1)}, u32[]{:S(2)}, u32[]{:S(2)}) collective-permute-start(f32[48,128]{1,0:T(8,128)S(1)} %get-tuple-element.41), channel_id=1, source_target_pairs={{0,1},{1,0},{2,3},{3,2},{4,5},{5,4},{6,7},{7,6},{8,9},{9,8},{10,11... | collective-permute-start | bytes 73736 | tf_op jit(solution)/shard_map/ppermute | solution.py:454

commit v4 on v3

--- a/solution.py
+++ b/solution.py
@@ -48,7 +48,7 @@
 UNROLL_A = 16
 UNROLL_B = 16
 OWN_FLOPS = 2_000_000_000
-UNPACK_FLOPS = 1_000_000_000
+INNER_FLOPS = 1_000_000_000
 
 
 SPACES = {"vmem": VMEM, "hbm": VMEM, "": VMEM, "smem": SMEM, "table": SMEM, "raw": pltpu.HBM}
@@ -255,10 +255,10 @@
 
 
 def rest_kernel(
-    g1, g2, g3, field, nodes, _, d1, d2, d3, inside, ghosts, parts, fluid, lab_v, lab_s, sem
+    g3, g1, g2, field, nodes, _, send3, send1, drag2, inside, ghosts, parts, fluid, lab_v, lab_s, sem
 ):
-    groups = (g1, g2, g3)
-    drags = (d1, d2, d3)
+    groups = (g3, g1, g2)
+    drags = (send3, send1, drag2)
     for k, g in enumerate(groups):
         lab_v[k : k + 1, :] = g[256:257, :].astype(jnp.int32)
     copy = pltpu.make_async_copy(lab_v, lab_s, sem)
@@ -270,91 +270,107 @@
         find_drag(groups[k], fluid, drags[k])
     for k in range(3):
         project(groups[k], elements[k], drags[k], nodes, parts)
-    gather_parts(parts, inside, ghosts)
-
-
-def gather_parts(parts, inside, ghosts):
+    gather_parts(parts, inside, ghosts, send1, send3)
+
+
+def slots():
+    return (lanes() % 64) // 8
+
+
+def pack_face(layers, upper):
+    spot = slots()
+    out = jnp.zeros((16, 128), F32)
+    for k, layer in enumerate(layers):
+        by = (8 * k - 56 * upper) % 128
+        out = jnp.where(spot == k, pltpu.roll(layer, by, 1) if by else layer, out)
+    return out
+
+
+def gather_parts(parts, inside, ghosts, send1, send3):
     low_half = lanes() < 64
     odd = lax.axis_index("gx") & 1
     to_lo = (1 - odd) * 12
     to_hi = odd * 12
+    y_odd = (lax.axis_index("gy") & 1) == 1
 
     def part(x, y, c, k, h):
         n = 2 * c + k if k < 2 else 6 + c
         return parts[pl.ds(((x * 4 + y) * 36 + n * 4 + h) * PITCH, 16), :]
 
-    def one(y, _):
-        for c in range(3):
-            lower = []
-            upper = []
+    for c in range(3):
+        faces = {}
+        for y in range(4):
+            lower = [part(0, y, c, 1, h) + part(1, y, c, 0, h) for h in range(4)]
+            upper = [part(1, y, c, 1, h) + part(0, y, c, 2, h) for h in range(4)]
+            lo = [part(0, y, c, 0, h) for h in range(4)]
+            hi = [part(1, y, c, 2, h) for h in range(4)]
+            lo[3] = lo[3] + jnp.where(low_half, 0.0, pltpu.roll(lower[0], 64, 1))
+            hi[0] = hi[0] + jnp.where(low_half, pltpu.roll(upper[3], 64, 1), 0.0)
             for h in range(4):
-                lo = part(0, y, c, 1, h) + part(1, y, c, 0, h)
-                hi = part(1, y, c, 1, h) + part(0, y, c, 2, h)
-                inside[c * 8 + y, :, 128 * h : 128 * h + 128] = lo
-                inside[c * 8 + 4 + y, :, 128 * h : 128 * h + 128] = hi
-                lower.append(lo)
-                upper.append(hi)
-            for h in range(4):
-                lo = part(0, y, c, 0, h)
-                hi = part(1, y, c, 2, h)
-                if h == 3:
-                    lo = lo + jnp.where(low_half, 0.0, pltpu.roll(lower[0], 64, 1))
-                if h == 0:
-                    hi = hi + jnp.where(low_half, pltpu.roll(upper[3], 64, 1), 0.0)
-                ghosts[to_lo + c * 4 + y, :, 128 * h : 128 * h + 128] = lo
-                ghosts[to_hi + c * 4 + y, :, 128 * h : 128 * h + 128] = hi
-        return 0
-
-    lax.fori_loop(0, 4, one, 0)
-
-
-def first_pass_kernel(last_gx, inside, sent, near, far, field, faces):
+                cut = slice(128 * h, 128 * h + 128)
+                inside[c * 8 + y, :, cut] = lower[h]
+                inside[c * 8 + 4 + y, :, cut] = upper[h]
+                ghosts[to_lo + c * 4 + y, :, cut] = lo[h]
+                ghosts[to_hi + c * 4 + y, :, cut] = hi[h]
+            if y in (0, 3):
+                faces[y] = (pack_face(lower + upper, y == 3), pack_face(lo + hi, y == 3))
+        for k in range(2):
+            at = slice(96 + 48 * k + 16 * c, 112 + 48 * k + 16 * c)
+            send1[at, :] = jnp.where(y_odd, faces[0][k], faces[3][k])
+            send3[at, :] = jnp.where(y_odd, faces[3][k], faces[0][k])
+
+
+def forward_kernel(got1, got3, near, far):
+    low_slots = slots() < 4
+    x_odd = (lax.axis_index("gx") & 1) == 1
+    y_odd = (lax.axis_index("gy") & 1) == 1
+    one = got1[144:192, :]
+    three = got3[144:192, :]
+    before = jnp.where(y_odd, one, three)
+    after = jnp.where(y_odd, three, one)
+    of_lo = jnp.where(low_slots, before, pltpu.roll(after, 32, 1))
+    of_hi = jnp.where(low_slots, pltpu.roll(before, 96, 1), after)
+    near[...] = jnp.where(x_odd, of_lo, of_hi)
+    far[...] = jnp.where(x_odd, of_hi, of_lo)
+
+
+def first_pass(last_gx, inside, sent, near, far, field):
     low_half = lanes() < 64
-    spot = (lanes() % 64) // 8
     gx = lax.axis_index("gx")
     odd = (gx & 1) == 1
     has_before = gx > 0
     has_after = gx < last_gx
     to_lo = (1 - (gx & 1)) * 12
     to_hi = (gx & 1) * 12
-    y_odd = (lax.axis_index("gy") & 1) == 1
-
-    def cut(ref, at, h):
-        return ref[at, :, 128 * h : 128 * h + 128]
-
-    for c in range(3):
-        packed = [jnp.zeros((16, 128), F32), jnp.zeros((16, 128), F32)]
+
+    def one_comp(c, _):
         for y in range(4):
-            pair = [(cut(near, c * 4 + y, h), cut(far, c * 4 + y, h)) for h in range(4)]
+
+            def cut(ref, at, h):
+                return ref[at + c * 4 + y, :, 128 * h : 128 * h + 128]
+
+            pair = [(cut(near, 0, h), cut(far, 0, h)) for h in range(4)]
             got_lo = [jnp.where(odd, n, f) for n, f in pair]
             got_hi = [jnp.where(odd, f, n) for n, f in pair]
             lower = [
-                cut(inside, c * 8 + y, h) + jnp.where(has_before, got_lo[h], 0.0) for h in range(4)
+                cut(inside, c * 4, h) + jnp.where(has_before, got_lo[h], 0.0) for h in range(4)
             ]
             upper = [
-                cut(inside, c * 8 + 4 + y, h) + jnp.where(has_after, got_hi[h], 0.0)
-                for h in range(4)
+                cut(inside, c * 4 + 4, h) + jnp.where(has_after, got_hi[h], 0.0) for h in range(4)
             ]
-            first = got_lo[0] + pltpu.roll(cut(sent, to_lo + c * 4 + y, 3), 64, 1)
-            last = got_hi[3] + pltpu.roll(cut(sent, to_hi + c * 4 + y, 0), 64, 1)
+            first = got_lo[0] + pltpu.roll(cut(sent, to_lo, 3), 64, 1)
+            last = got_hi[3] + pltpu.roll(cut(sent, to_hi, 0), 64, 1)
             low3, up0 = lower[3], upper[0]
             lower[0] = jnp.where(low_half & has_before, first, lower[0])
             upper[3] = jnp.where(low_half | jnp.logical_not(has_after), upper[3], last)
             lower[3] = jnp.where(low_half, low3, low3 + pltpu.roll(up0, 64, 1))
             upper[0] = jnp.where(low_half, up0 + pltpu.roll(low3, 64, 1), up0)
-            for x, layer in ((0, lower), (1, upper)):
-                for h in range(4):
-                    field[c * 8 + x * 4 + y, :, 128 * h : 128 * h + 128] = layer[h]
-                    k = x * 4 + h
-                    if y == 0:
-                        moved = pltpu.roll(layer[h], 8 * k, 1) if k else layer[h]
-                        packed[0] = jnp.where(spot == k, moved, packed[0])
-                    if y == 3:
-                        by = (8 * k - 56) % 128
-                        moved = pltpu.roll(layer[h], by, 1) if by else layer[h]
-                        packed[1] = jnp.where(spot == k, moved, packed[1])
-        faces[16 * c : 16 * c + 16, :] = jnp.where(y_odd, packed[0], packed[1])
-        faces[48 + 16 * c : 64 + 16 * c, :] = jnp.where(y_odd, packed[1], packed[0])
+            for h in range(4):
+                field[c * 8 + y, :, 128 * h : 128 * h + 128] = lower[h]
+                field[c * 8 + 4 + y, :, 128 * h : 128 * h + 128] = upper[h]
+        return 0
+
+    lax.fori_loop(0, 3, one_comp, 0)
 
 
 def last_passes(field, rows, before, after, buf, start):
@@ -396,11 +412,13 @@
     lax.fori_loop(0, 3, one_comp, 0)
 
 
-def inner_kernel(block, field, d0, d1, d2, d3, drag, out, drag_buf, buf, sem, drag_sem):
+def inner_kernel(
+    last_gx, block, inside, sent, near, far, d0, d1, d2, d3,
+    drag, out, field, drag_buf, buf, sem, drag_sem,
+):
     def copy(row):
         return pltpu.make_async_copy(buf.at[row], out.at[row], sem.at[row])
 
-    last_passes(field, (1, 2), lambda c: None, lambda c: None, buf, lambda row: copy(row).start())
     for k, d in enumerate((d0, d1, d2, d3)):
 
         def one(r, _):
@@ -408,6 +426,7 @@
             return 0
 
         lax.fori_loop(0, SHARE, one, 0, unroll=8)
+    first_pass(last_gx, inside, sent, near, far, field)
     moves = [
         pltpu.make_async_copy(
             drag_buf.at[pl.ds(96 * k, 96)], drag.at[pl.ds(96 * k, 96)], drag_sem.at[k]
@@ -416,6 +435,7 @@
     ]
     for move in moves:
         move.start()
+    last_passes(field, (1, 2), lambda c: None, lambda c: None, buf, lambda row: copy(row).start())
     for row in range(24):
         if row % 4 in (1, 2):
             copy(row).wait()
@@ -423,18 +443,39 @@
         move.wait()
 
 
-def outer_kernel(field, got1, got3, _, out, buf, sem):
+def outer_kernel(last_gx, field, got1, got3, near, far, _, out, buf, sem):
+    gx = lax.axis_index("gx")
+    x_odd = (gx & 1) == 1
     gy = lax.axis_index("gy")
-    odd = (gy & 1) == 1
-    between = (gy > 0) & (gy < N_GY - 1)
+    y_odd = (gy & 1) == 1
+    has_before = gx > 0
+    has_after = gx < last_gx
+    lane = lanes()
+    low_slots = slots() < 4
+    here = (low_slots & has_before) | (jnp.logical_not(low_slots) & has_after)
 
     def copy(row):
         return pltpu.make_async_copy(buf.at[row], out.at[row], sem.at[row])
 
     def face(c, first):
-        a = got1[pl.ds(16 * c, 16), :]
-        b = jnp.where(between, got3[pl.ds(16 * c, 16), :], 0.0)
-        return jnp.where(odd, a, b) if first else jnp.where(odd, b, a)
+        use_one = y_odd if first else jnp.logical_not(y_odd)
+        at = pl.ds(96 + 16 * c, 16)
+        own = jnp.where(use_one, got1[at, :], got3[at, :])
+        at = pl.ds(144 + 16 * c, 16)
+        sent = jnp.where(use_one, got1[at, :], got3[at, :])
+        at = pl.ds(16 * c, 16)
+        of_lo = jnp.where(x_odd, near[at, :], far[at, :])
+        of_hi = jnp.where(x_odd, far[at, :], near[at, :])
+        if first:
+            got = jnp.where(low_slots, of_lo, pltpu.roll(of_hi, 32, 1))
+        else:
+            got = jnp.where(low_slots, pltpu.roll(of_lo, 96, 1), of_hi)
+        total = own + jnp.where(here, got, 0.0)
+        new = jnp.where((lane < 8) & has_before, got + pltpu.roll(sent, 40, 1), total)
+        new = jnp.where((lane >= 120) & has_after, got + pltpu.roll(sent, 88, 1), new)
+        new = jnp.where((lane >= 88) & (lane < 96), total + pltpu.roll(total, 56, 1), new)
+        new = jnp.where((lane >= 32) & (lane < 40), total + pltpu.roll(total, 72, 1), new)
+        return jnp.where(gy > 0 if first else gy < N_GY - 1, new, 0.0)
 
     last_passes(
         field,
@@ -450,8 +491,7 @@
 
 
 def swapped(x, axis, partner):
-    count = lax.axis_size(axis)
-    return lax.ppermute(x, axis, [(i, partner(i) % count) for i in range(count)])
+    return lax.ppermute(x, axis, [(i, partner(i)) for i in range(lax.axis_size(axis))])
 
 
 def body(velocity, part_pos, part_vel, part_coef, counts, dest, elem):
@@ -478,12 +518,15 @@
         (VMEM((96, 128), F32),),
         flops=OWN_FLOPS,
     )
-    *drags, inside, ghosts, _ = call(
+    grid = (24, 16, 512)
+    send3, send1, drag2, inside, ghosts, _ = call(
         rest_kernel,
-        [((96, 128), F32, "vmem")] * 3
-        + [((24, 16, 512), F32, "vmem")] * 2
+        [((192, 128), F32, "vmem")] * 2
+        + [((96, 128), F32, "vmem")]
+        + [(grid, F32, "vmem")] * 2
         + [((8 * 36 * PITCH, 128), F32, "vmem")],
-        [(groups[k], "vmem") for k in ORDER] + [(field, "vmem"), (table, "vmem"), (parts, "vmem")],
+        [(groups[k], "vmem") for k in ORDER]
+        + [(field, "vmem"), (table, "vmem"), (parts, "vmem")],
         (
             VMEM((96, 128), F32),
             VMEM((8, 128), jnp.int32),
@@ -492,36 +535,43 @@
         ),
         aliases={5: 5},
     )
-    far = swapped(ghosts[12:], "gx", lambda i: i + 1 if i & 1 else i - 1)
+    last_gx = lax.axis_size("gx") - 1
+
+    def to_far(i):
+        other = i + 1 if i & 1 else i - 1
+        return other if 0 <= other <= last_gx else i
+
+    far = swapped(ghosts[12:], "gx", to_far)
     near = swapped(ghosts[:12], "gx", lambda i: i ^ 1)
-    back = {k: swapped(d, "gy", lambda i, k=k: i ^ k) for k, d in zip(ORDER, drags)}
-    last_gx = lax.axis_size("gx") - 1
-    field, faces = call(
-        lambda *refs: first_pass_kernel(last_gx, *refs),
-        [((24, 16, 512), F32, "vmem"), ((96, 128), F32, "vmem")],
-        [(inside, "vmem"), (ghosts, "vmem"), (near, "vmem"), (far, "vmem")],
-    )
-    got1 = swapped(faces[:48], "gy", lambda i: i ^ 1)
-    got3 = swapped(faces[48:], "gy", lambda i: i ^ 3)
-    grid = (24, 16, 512)
-    drag, out = call(
-        inner_kernel,
-        [((384, 128), F32, "raw"), (grid, F32, "raw")],
-        [(block, "smem"), (field, "vmem"), (drag_own, "vmem")] + [(back[k], "vmem") for k in range(1, N_GY)],
+    got1 = swapped(send1, "gy", lambda i: i ^ 1)
+    got3 = swapped(send3, "gy", lambda i: i ^ 3)
+    back2 = swapped(drag2, "gy", lambda i: i ^ 2)
+    forward_near, forward_far = call(
+        forward_kernel,
+        [((48, 128), F32, "vmem")] * 2,
+        [(got1, "vmem"), (got3, "vmem")],
+    )
+    got_far = swapped(forward_far, "gx", to_far)
+    got_near = swapped(forward_near, "gx", lambda i: i ^ 1)
+    drag, out, field = call(
+        lambda *refs: inner_kernel(last_gx, *refs),
+        [((384, 128), F32, "raw"), (grid, F32, "raw"), (grid, F32, "vmem")],
+        [(block, "smem")]
+        + [(a, "vmem") for a in (inside, ghosts, near, far, drag_own, got1, back2, got3)],
         (
             VMEM((384, 128), F32),
             VMEM(grid, F32),
             pltpu.SemaphoreType.DMA((24,)),
             pltpu.SemaphoreType.DMA((4,)),
         ),
-        flops=UNPACK_FLOPS,
+        flops=INNER_FLOPS,
     )
     (out,) = call(
-        outer_kernel,
+        lambda *refs: outer_kernel(last_gx, *refs),
         [(grid, F32, "raw")],
-        [(field, "vmem"), (got1, "vmem"), (got3, "vmem"), (out, "raw")],
+        [(a, "vmem") for a in (field, got1, got3, got_near, got_far)] + [(out, "raw")],
         (VMEM(grid, F32), pltpu.SemaphoreType.DMA((24,))),
-        aliases={3: 0},
+        aliases={5: 0},
     )
     return (
         drag.reshape(3, 128, 128).transpose(1, 0, 2),

time: 40.1 us -> 42.9 us (1.070)
  the two profiles are of different devices: /device:TPU:0 before, /device:TPU:30 now
where the time goes in v4:
time: 42.9 us; the launch traced here: 42.7 us
  Pallas kernels  17.4 us (41%)
  starting transfers between devices  16.6 us (39%)
  waiting for transfers between devices  7.81 us (18%)
  between operations  0.75 us (2%)
    pallas_call x6, Pallas kernels, call(): pl.pallas_call(kernel, out_shape=shapes, in_specs=[pl.BlockSpec(memory_sp...  17.4 us
    ppermute x10, starting transfers between devices, swapped(): lax.ppermute(x, axis, [(i, partner(i)) for i in range(lax.axis_size(axis))])  16.6 us
    ppermute x10, waiting for transfers between devices, swapped(): lax.ppermute(x, axis, [(i, partner(i)) for i in range(lax.axis_size(axis))])  7.81 us
  transfers between devices with their start and end apart: 10, of which 5 were waited for; matrix products, arithmetic and copies ran while one was open for 0% of the time, Pallas kernels for 15%

profile of v4, /device:TPU:30, one launch (start us, length us, event | category | flops | bytes accessed | tf_op | source)
XLA Modules:
  0.0 42.7 jit_solution(3408903367463088984)
XLA Ops:
  0.6 2.7 %shard_map.95 = (f32[1056,128]{1,0:T(8,128)S(1)}, s32[128]{0:T(128)S(1)}, s32[128]{0:T(128)S(1)}) custom-call(s32[128]{0:T(128)} %dest_hbm.1, s32[128]{0:T(128)} %counts_hbm.1, s32[128]{0:T(128)} %elem_hbm.1, f32[3,128,128]{2,1,0:T(8,128)} %bitcast.9, f32[3,128,128]{2,1,0:T(8,128)} %bitcast.10, f32[256,128]{1,0:T(8,128)} %bitcast.11), custom_call_target="tpu_custom_call" | custom-call | tf_op jit(solution)/shard_map/pallas_call | solution.py:70
  3.4 1.5 %collective-permute-start.2 = (f32[264,128]{1,0:T(8,128)S(1)}, f32[264,128]{1,0:T(8,128)S(1)}, u32[]{:S(2)}, u32[]{:S(2)}) collective-permute-start(f32[264,128]{1,0:T(8,128)S(1)} %get-tuple-element.39), channel_id=1, source_target_pairs={{0,2},{1,3},{2,0},{3,1},{4,6},{5,7},{6,4},{7,5},{8,10},{9,11},{10,... | collective-permute-start | bytes 405512 | tf_op jit(solution)/shard_map/ppermute | solution.py:494
  4.9 0.0 collective-permute-start.1
  4.9 2.7 %collective-permute-start = (f32[264,128]{1,0:T(8,128)S(1)}, f32[264,128]{1,0:T(8,128)S(1)}, u32[]{:S(2)}, u32[]{:S(2)}) collective-permute-start(f32[264,128]{1,0:T(8,128)S(1)} %get-tuple-element.41), channel_id=1, source_target_pairs={{0,3},{1,2},{2,1},{3,0},{4,7},{5,6},{6,5},{7,4},{8,11},{9,10},{10,... | collective-permute-start | bytes 405512 | tf_op jit(solution)/shard_map/ppermute | solution.py:494
  7.5 3.5 %shard_map.96 = (f32[3264,128]{1,0:T(8,128)S(1)}, f32[4896,128]{1,0:T(8,128)S(1)}, f32[96,128]{1,0:T(8,128)S(1)}, f32[168,128]{1,0:T(8,128)S(1)}) custom-call(s32[128]{0:T(128)S(1)} %get-tuple-element.21.elem, f32[264,128]{1,0:T(8,128)S(1)} %get-tuple-element.38.group, bf16[24,16,512]{2,1,0:T(8,128)(2,1)} %bitcast.12, f32[168,128]{1,0:T(8,128)} %constant.2.clone.nodes), custom_call_target="tpu_custom_call" | custom-call | flops 2000000000 | tf_op jit(solution)/shard_map/pallas_call | solution.py:70
  11.0 0.4 collective-permute-done.2.g2
  11.4 0.0 collective-permute-done.1.g1
  11.4 1.8 %collective-permute-done.g3 = f32[264,128]{1,0:T(8,128)S(1)} collective-permute-done((f32[264,128]{1,0:T(8,128)S(1)}, f32[264,128]{1,0:T(8,128)S(1)}, u32[]{:S(2)}, u32[]{:S(2)}) %collective-permute-start) | collective-permute-done | bytes 135200 | tf_op jit(solution)/shard_map/ppermute | solution.py:494
  13.2 6.4 %shard_map.97 = (f32[192,128]{1,0:T(8,128)S(1)}, f32[192,128]{1,0:T(8,128)S(1)}, f32[96,128]{1,0:T(8,128)S(1)}, f32[24,16,512]{2,1,0:T(8,128)S(1)}, f32[24,16,512]{2,1,0:T(8,128)S(1)}, /*index=5*/f32[4896,128]{1,0:T(8,128)S(1)}) custom-call(f32[264,128]{1,0:T(8,128)S(1)} %collective-permute-done.g3, ...), custom_call_target="tpu_custom_call", output_to_operand_aliasing={{5}: (5, {})} | custom-call | tf_op jit(solution)/shard_map/pallas_call | solution.py:70
  19.6 0.1 fusion
  19.6 5.6 %collective-permute-start.4 = (f32[12,16,512]{2,1,0:T(8,128)S(1)}, f32[12,16,512]{2,1,0:T(8,128)S(1)}, u32[]{:S(2)}, u32[]{:S(2)}) collective-permute-start(f32[12,16,512]{2,1,0:T(8,128)S(1)} %get-tuple-element.36), channel_id=1, source_target_pairs={{0,0},{4,8},{8,4},{12,16},{16,12},{20,24},{24,20},{28,32},{32,28},... | collective-permute-start | bytes 1179656 | tf_op jit(solution)/shard_map/ppermute | solution.py:494
  25.2 0.1 collective-permute-start.3
  25.3 0.9 %collective-permute-start.5 = (f32[192,128]{1,0:T(8,128)S(1)}, f32[192,128]{1,0:T(8,128)S(1)}, u32[]{:S(2)}, u32[]{:S(2)}) collective-permute-start(f32[192,128]{1,0:T(8,128)S(1)} %get-tuple-element.28), channel_id=1, source_target_pairs={{0,1},{1,0},{2,3},{3,2},{4,5},{5,4},{6,7},{7,6},{8,9},{9,8},{10,11... | collective-permute-start | bytes 294920 | tf_op jit(solution)/shard_map/ppermute | solution.py:494
  26.3 0.7 %collective-permute-start.7 = (f32[192,128]{1,0:T(8,128)S(1)}, f32[192,128]{1,0:T(8,128)S(1)}, u32[]{:S(2)}, u32[]{:S(2)}) collective-permute-start(f32[192,128]{1,0:T(8,128)S(1)} %get-tuple-element.30), channel_id=1, source_target_pairs={{0,3},{1,2},{2,1},{3,0},{4,7},{5,6},{6,5},{7,4},{8,11},{9,10},{10,... | collective-permute-start | bytes 294920 | tf_op jit(solution)/shard_map/ppermute | solution.py:494
  26.9 2.6 %collective-permute-start.6 = (f32[96,128]{1,0:T(8,128)S(1)}, f32[96,128]{1,0:T(8,128)S(1)}, u32[]{:S(2)}, u32[]{:S(2)}) collective-permute-start(f32[96,128]{1,0:T(8,128)S(1)} %get-tuple-element.29), channel_id=1, source_target_pairs={{0,2},{1,3},{2,0},{3,1},{4,6},{5,7},{6,4},{7,5},{8,10},{9,11},{10,... | collective-permute-start | bytes 147464 | tf_op jit(solution)/shard_map/ppermute | solution.py:494
  29.5 1.0 %collective-permute-done.5.refs_6_.got1.refs_1_ = f32[192,128]{1,0:T(8,128)S(1)} collective-permute-done((f32[192,128]{1,0:T(8,128)S(1)}, f32[192,128]{1,0:T(8,128)S(1)}, u32[]{:S(2)}, u32[]{:S(2)}) %collective-permute-start.5) | collective-permute-done | bytes 98336 | tf_op jit(solution)/shard_map/ppermute | solution.py:494
  30.5 2.8 %collective-permute-done.7.refs_8_.got3.refs_2_ = f32[192,128]{1,0:T(8,128)S(1)} collective-permute-done((f32[192,128]{1,0:T(8,128)S(1)}, f32[192,128]{1,0:T(8,128)S(1)}, u32[]{:S(2)}, u32[]{:S(2)}) %collective-permute-start.7) | collective-permute-done | bytes 98336 | tf_op jit(solution)/shard_map/ppermute | solution.py:494
  33.4 0.1 shard_map.99
  33.5 0.1 collective-permute-start.8
  33.5 2.5 %collective-permute-start.9 = (f32[48,128]{1,0:T(8,128)S(1)}, f32[48,128]{1,0:T(8,128)S(1)}, u32[]{:S(2)}, u32[]{:S(2)}) collective-permute-start(f32[48,128]{1,0:T(8,128)S(1)} %get-tuple-element.34), channel_id=1, source_target_pairs={{0,0},{4,8},{8,4},{12,16},{16,12},{20,24},{24,20},{28,32},{32,28},... | collective-permute-start | bytes 73736 | tf_op jit(solution)/shard_map/ppermute | solution.py:494
  36.1 0.0 collective-permute-done.6.refs_7_
  36.1 0.0 collective-permute-done.4.refs_4_
  36.1 0.0 collective-permute-done.3.refs_3_
  36.1 2.9 %shard_map.98 = (f32[384,128]{1,0:T(8,128)}, f32[24,16,512]{2,1,0:T(8,128)}, f32[24,16,512]{2,1,0:T(8,128)S(1)}) custom-call(s32[128]{0:T(128)S(1)} %get-tuple-element.19.refs_0_, f32[24,16,512]{2,1,0:T(8,128)S(1)} %get-tuple-element.25.refs_1_, f32[24,16,512]{2,1,0:T(8,128)S(1)} %get-tuple-element.26.refs_2_, ...), custom_call_target="tpu_custom_call" | custom-call | flops 1000000000 | tf_op jit(solution)/shard_map/pallas_call | solution.py:70
  39.0 0.0 collective-permute-done.8.refs_3_
  39.0 1.8 %collective-permute-done.9.refs_4_ = f32[48,128]{1,0:T(8,128)S(1)} collective-permute-done((f32[48,128]{1,0:T(8,128)S(1)}, f32[48,128]{1,0:T(8,128)S(1)}, u32[]{:S(2)}, u32[]{:S(2)}) %collective-permute-start.9) | collective-permute-done | bytes 24608 | tf_op jit(solution)/shard_map/ppermute | solution.py:494
  40.8 1.9 %shard_map.100 = f32[24,16,512]{2,1,0:T(8,128)} custom-call(f32[24,16,512]{2,1,0:T(8,128)S(1)} %get-tuple-element.32.refs_0_, f32[192,128]{1,0:T(8,128)S(1)} %collective-permute-done.5.refs_6_.got1.refs_1_, f32[192,128]{1,0:T(8,128)S(1)} %collective-permute-done.7.refs_8_.got3.refs_2_, ...), custom_call_target="tpu_custom_call", output_to_operand_aliasing={{}: (5, {})} | custom-call | tf_op jit(solution)/shard_map/pallas_call | solution.py:70
  (1 shorter events, 0.0 us)
Async XLA Ops:
  3.4 8.0 %collective-permute-start.2 = (f32[264,128]{1,0:T(8,128)S(1)}, f32[264,128]{1,0:T(8,128)S(1)}, u32[]{:S(2)}, u32[]{:S(2)}) collective-permute-start(f32[264,128]{1,0:T(8,128)S(1)} %get-tuple-element.39), channel_id=1, source_target_pairs={{0,2},{1,3},{2,0},{3,1},{4,6},{5,7},{6,4},{7,5},{8,10},{9,11},{10,... | collective-permute-start | bytes 405512 | tf_op jit(solution)/shard_map/ppermute | solution.py:494
  4.9 6.6 %collective-permute-start.1 = (f32[264,128]{1,0:T(8,128)S(1)}, f32[264,128]{1,0:T(8,128)S(1)}, u32[]{:S(2)}, u32[]{:S(2)}) collective-permute-start(f32[264,128]{1,0:T(8,128)S(1)} %get-tuple-element.40), channel_id=1, source_target_pairs={{0,1},{1,0},{2,3},{3,2},{4,5},{5,4},{6,7},{7,6},{8,9},{9,8},{10,11... | collective-permute-start | bytes 405512 | tf_op jit(solution)/shard_map/ppermute | solution.py:494
  4.9 8.3 %collective-permute-start = (f32[264,128]{1,0:T(8,128)S(1)}, f32[264,128]{1,0:T(8,128)S(1)}, u32[]{:S(2)}, u32[]{:S(2)}) collective-permute-start(f32[264,128]{1,0:T(8,128)S(1)} %get-tuple-element.41), channel_id=1, source_target_pairs={{0,3},{1,2},{2,1},{3,0},{4,7},{5,6},{6,5},{7,4},{8,11},{9,10},{10,... | collective-permute-start | bytes 405512 | tf_op jit(solution)/shard_map/ppermute | solution.py:494
  19.6 16.4 %collective-permute-start.4 = (f32[12,16,512]{2,1,0:T(8,128)S(1)}, f32[12,16,512]{2,1,0:T(8,128)S(1)}, u32[]{:S(2)}, u32[]{:S(2)}) collective-permute-start(f32[12,16,512]{2,1,0:T(8,128)S(1)} %get-tuple-element.36), channel_id=1, source_target_pairs={{0,0},{4,8},{8,4},{12,16},{16,12},{20,24},{24,20},{28,32},{32,28},... | collective-permute-start | bytes 1179656 | tf_op jit(solution)/shard_map/ppermute | solution.py:494
  25.2 10.9 %collective-permute-start.3 = (f32[12,16,512]{2,1,0:T(8,128)S(1)}, f32[12,16,512]{2,1,0:T(8,128)S(1)}, u32[]{:S(2)}, u32[]{:S(2)}) collective-permute-start(f32[12,16,512]{2,1,0:T(8,128)S(1)} %get-tuple-element.37), channel_id=1, source_target_pairs={{0,4},{4,0},{8,12},{12,8},{16,20},{20,16},{24,28},{28,24},{32,36},... | collective-permute-start | bytes 1179656 | tf_op jit(solution)/shard_map/ppermute | solution.py:494
  25.3 5.2 %collective-permute-start.5 = (f32[192,128]{1,0:T(8,128)S(1)}, f32[192,128]{1,0:T(8,128)S(1)}, u32[]{:S(2)}, u32[]{:S(2)}) collective-permute-start(f32[192,128]{1,0:T(8,128)S(1)} %get-tuple-element.28), channel_id=1, source_target_pairs={{0,1},{1,0},{2,3},{3,2},{4,5},{5,4},{6,7},{7,6},{8,9},{9,8},{10,11... | collective-permute-start | bytes 294920 | tf_op jit(solution)/shard_map/ppermute | solution.py:494
  26.3 7.1 %collective-permute-start.7 = (f32[192,128]{1,0:T(8,128)S(1)}, f32[192,128]{1,0:T(8,128)S(1)}, u32[]{:S(2)}, u32[]{:S(2)}) collective-permute-start(f32[192,128]{1,0:T(8,128)S(1)} %get-tuple-element.30), channel_id=1, source_target_pairs={{0,3},{1,2},{2,1},{3,0},{4,7},{5,6},{6,5},{7,4},{8,11},{9,10},{10,... | collective-permute-start | bytes 294920 | tf_op jit(solution)/shard_map/ppermute | solution.py:494
  26.9 9.2 %collective-permute-start.6 = (f32[96,128]{1,0:T(8,128)S(1)}, f32[96,128]{1,0:T(8,128)S(1)}, u32[]{:S(2)}, u32[]{:S(2)}) collective-permute-start(f32[96,128]{1,0:T(8,128)S(1)} %get-tuple-element.29), channel_id=1, source_target_pairs={{0,2},{1,3},{2,0},{3,1},{4,6},{5,7},{6,4},{7,5},{8,10},{9,11},{10,... | collective-permute-start | bytes 147464 | tf_op jit(solution)/shard_map/ppermute | solution.py:494
  33.5 5.6 %collective-permute-start.8 = (f32[48,128]{1,0:T(8,128)S(1)}, f32[48,128]{1,0:T(8,128)S(1)}, u32[]{:S(2)}, u32[]{:S(2)}) collective-permute-start(f32[48,128]{1,0:T(8,128)S(1)} %get-tuple-element.33), channel_id=1, source_target_pairs={{0,4},{4,0},{8,12},{12,8},{16,20},{20,16},{24,28},{28,24},{32,36},... | collective-permute-start | bytes 73736 | tf_op jit(solution)/shard_map/ppermute | solution.py:494
  33.5 7.3 %collective-permute-start.9 = (f32[48,128]{1,0:T(8,128)S(1)}, f32[48,128]{1,0:T(8,128)S(1)}, u32[]{:S(2)}, u32[]{:S(2)}) collective-permute-start(f32[48,128]{1,0:T(8,128)S(1)} %get-tuple-element.34), channel_id=1, source_target_pairs={{0,0},{4,8},{8,4},{12,16},{16,12},{20,24},{24,20},{28,32},{32,28},... | collective-permute-start | bytes 73736 | tf_op jit(solution)/shard_map/ppermute | solution.py:494

commit v5 on v3

--- a/solution.py
+++ b/solution.py
@@ -45,8 +45,8 @@
 
 PITCH = 17
 ORDER = (3, 1, 2)
-UNROLL_A = 16
-UNROLL_B = 16
+UNROLL_A = 32
+UNROLL_B = 32
 OWN_FLOPS = 2_000_000_000
 UNPACK_FLOPS = 1_000_000_000
 
@@ -254,21 +254,30 @@
     project(group, element, drag, nodes, parts)
 
 
-def rest_kernel(
-    g1, g2, g3, field, nodes, _, d1, d2, d3, inside, ghosts, parts, fluid, lab_v, lab_s, sem
-):
-    groups = (g1, g2, g3)
-    drags = (d1, d2, d3)
+def fetch_elements(groups, lab_v, lab_s, sem):
     for k, g in enumerate(groups):
         lab_v[k : k + 1, :] = g[256:257, :].astype(jnp.int32)
     copy = pltpu.make_async_copy(lab_v, lab_s, sem)
     copy.start()
     copy.wait()
-    elements = [lambda r, k=k: lab_s[k, r] for k in range(3)]
-    for k in range(3):
+    return [lambda r, k=k: lab_s[k, r] for k in range(len(groups))]
+
+
+def middle_kernel(group, field, nodes, _, drag, parts, fluid, lab_v, lab_s, sem):
+    (element,) = fetch_elements((group,), lab_v, lab_s, sem)
+    interpolate(group, element, field, nodes, fluid)
+    find_drag(group, fluid, drag)
+    project(group, element, drag, nodes, parts)
+
+
+def rest_kernel(ga, gb, field, nodes, _, da, db, inside, ghosts, parts, fluid, lab_v, lab_s, sem):
+    groups = (ga, gb)
+    drags = (da, db)
+    elements = fetch_elements(groups, lab_v, lab_s, sem)
+    for k in range(2):
         interpolate(groups[k], elements[k], field, nodes, fluid)
         find_drag(groups[k], fluid, drags[k])
-    for k in range(3):
+    for k in range(2):
         project(groups[k], elements[k], drags[k], nodes, parts)
     gather_parts(parts, inside, ghosts)
 
@@ -396,37 +405,33 @@
     lax.fori_loop(0, 3, one_comp, 0)
 
 
-def inner_kernel(block, field, d0, d1, d2, d3, drag, out, drag_buf, buf, sem, drag_sem):
-    def copy(row):
-        return pltpu.make_async_copy(buf.at[row], out.at[row], sem.at[row])
-
-    last_passes(field, (1, 2), lambda c: None, lambda c: None, buf, lambda row: copy(row).start())
+def inner_kernel(block, field, d0, d1, d2, d3, drag, out):
     for k, d in enumerate((d0, d1, d2, d3)):
 
         def one(r, _):
-            drag_buf[pl.ds(block[k * SHARE + r], 3, stride=128), :] = d[pl.ds(r, 3, stride=32), :]
+            drag[pl.ds(block[k * SHARE + r], 3, stride=128), :] = d[pl.ds(r, 3, stride=32), :]
             return 0
 
         lax.fori_loop(0, SHARE, one, 0, unroll=8)
+    last_passes(field, (1, 2), lambda c: None, lambda c: None, out, lambda row: None)
+
+
+def outer_kernel(field, got1, got3, done, drag_done, drag, out, buf, sem, drag_sem):
+    gy = lax.axis_index("gy")
+    odd = (gy & 1) == 1
+    between = (gy > 0) & (gy < N_GY - 1)
     moves = [
         pltpu.make_async_copy(
-            drag_buf.at[pl.ds(96 * k, 96)], drag.at[pl.ds(96 * k, 96)], drag_sem.at[k]
+            drag_done.at[pl.ds(96 * k, 96)], drag.at[pl.ds(96 * k, 96)], drag_sem.at[k]
         )
         for k in range(4)
+    ] + [
+        pltpu.make_async_copy(done.at[row], out.at[row], sem.at[row])
+        for row in range(24)
+        if row % 4 in (1, 2)
     ]
     for move in moves:
         move.start()
-    for row in range(24):
-        if row % 4 in (1, 2):
-            copy(row).wait()
-    for move in moves:
-        move.wait()
-
-
-def outer_kernel(field, got1, got3, _, out, buf, sem):
-    gy = lax.axis_index("gy")
-    odd = (gy & 1) == 1
-    between = (gy > 0) & (gy < N_GY - 1)
 
     def copy(row):
         return pltpu.make_async_copy(buf.at[row], out.at[row], sem.at[row])
@@ -444,14 +449,25 @@
         buf,
         lambda row: copy(row).start(),
     )
+    for move in moves:
+        move.wait()
     for row in range(24):
         if row % 4 in (0, 3):
             copy(row).wait()
 
 
 def swapped(x, axis, partner):
-    count = lax.axis_size(axis)
-    return lax.ppermute(x, axis, [(i, partner(i) % count) for i in range(count)])
+    return lax.ppermute(x, axis, [(i, partner(i)) for i in range(lax.axis_size(axis))])
+
+
+def swapped_all(x, partner):
+    nx, ny = lax.axis_size("gx"), lax.axis_size("gy")
+    pairs = []
+    for i in range(nx):
+        for j in range(ny):
+            a, b = partner(i, j)
+            pairs.append((i * ny + j, a * ny + b))
+    return lax.ppermute(x, ("gx", "gy"), pairs)
 
 
 def body(velocity, part_pos, part_vel, part_coef, counts, dest, elem):
@@ -478,23 +494,40 @@
         (VMEM((96, 128), F32),),
         flops=OWN_FLOPS,
     )
-    *drags, inside, ghosts, _ = call(
+    labels = (
+        VMEM((96, 128), F32),
+        VMEM((8, 128), jnp.int32),
+        SMEM((8, 128), jnp.int32),
+        pltpu.SemaphoreType.DMA,
+    )
+    first, *others = reversed(ORDER)
+    drags = {}
+    drags[first], parts = call(
+        middle_kernel,
+        [((96, 128), F32, "vmem"), ((8 * 36 * PITCH, 128), F32, "vmem")],
+        [(a, "vmem") for a in (groups[first], field, table, parts)],
+        labels,
+        flops=OWN_FLOPS,
+        aliases={3: 1},
+    )
+    drags[others[1]], drags[others[0]], inside, ghosts, _ = call(
         rest_kernel,
-        [((96, 128), F32, "vmem")] * 3
+        [((96, 128), F32, "vmem")] * 2
         + [((24, 16, 512), F32, "vmem")] * 2
         + [((8 * 36 * PITCH, 128), F32, "vmem")],
-        [(groups[k], "vmem") for k in ORDER] + [(field, "vmem"), (table, "vmem"), (parts, "vmem")],
-        (
-            VMEM((96, 128), F32),
-            VMEM((8, 128), jnp.int32),
-            SMEM((8, 128), jnp.int32),
-            pltpu.SemaphoreType.DMA,
-        ),
-        aliases={5: 5},
-    )
-    far = swapped(ghosts[12:], "gx", lambda i: i + 1 if i & 1 else i - 1)
+        [(a, "vmem") for a in (groups[others[1]], groups[others[0]], field, table, parts)],
+        labels,
+        aliases={4: 4},
+    )
+    last_gx = lax.axis_size("gx") - 1
+
+    def other_chip(i, j):
+        k = i + 1 if i & 1 else i - 1
+        return (k, j) if 0 <= k <= last_gx else (i, j ^ 1)
+
+    far = swapped_all(ghosts[12:], other_chip)
     near = swapped(ghosts[:12], "gx", lambda i: i ^ 1)
-    back = {k: swapped(d, "gy", lambda i, k=k: i ^ k) for k, d in zip(ORDER, drags)}
+    back = {k: swapped(d, "gy", lambda i, k=k: i ^ k) for k, d in drags.items()}
     last_gx = lax.axis_size("gx") - 1
     field, faces = call(
         lambda *refs: first_pass_kernel(last_gx, *refs),
@@ -502,26 +535,20 @@
         [(inside, "vmem"), (ghosts, "vmem"), (near, "vmem"), (far, "vmem")],
     )
     got1 = swapped(faces[:48], "gy", lambda i: i ^ 1)
-    got3 = swapped(faces[48:], "gy", lambda i: i ^ 3)
+    got3 = swapped_all(faces[48:], lambda i, j: (i, j ^ 3) if 0 < j < N_GY - 1 else (i ^ 1, j))
     grid = (24, 16, 512)
+    drag, inner = call(
+        inner_kernel,
+        [((384, 128), F32, "vmem"), (grid, F32, "vmem")],
+        [(block, "smem"), (field, "vmem"), (drag_own, "vmem")]
+        + [(back[k], "vmem") for k in range(1, N_GY)],
+        flops=UNPACK_FLOPS,
+    )
     drag, out = call(
-        inner_kernel,
+        outer_kernel,
         [((384, 128), F32, "raw"), (grid, F32, "raw")],
-        [(block, "smem"), (field, "vmem"), (drag_own, "vmem")] + [(back[k], "vmem") for k in range(1, N_GY)],
-        (
-            VMEM((384, 128), F32),
-            VMEM(grid, F32),
-            pltpu.SemaphoreType.DMA((24,)),
-            pltpu.SemaphoreType.DMA((4,)),
-        ),
-        flops=UNPACK_FLOPS,
-    )
-    (out,) = call(
-        outer_kernel,
-        [(grid, F32, "raw")],
-        [(field, "vmem"), (got1, "vmem"), (got3, "vmem"), (out, "raw")],
-        (VMEM(grid, F32), pltpu.SemaphoreType.DMA((24,))),
-        aliases={3: 0},
+        [(a, "vmem") for a in (field, got1, got3, inner, drag)],
+        (VMEM(grid, F32), pltpu.SemaphoreType.DMA((24,)), pltpu.SemaphoreType.DMA((4,))),
     )
     return (
         drag.reshape(3, 128, 128).transpose(1, 0, 2),

time: 40.1 us -> 34.4 us (0.86)
  the two profiles are of different devices: /device:TPU:0 before, /device:TPU:18 now
where the time goes in v5:
time: 34.4 us; the launch traced here: 34.3 us
  Pallas kernels  15.4 us (45%)
  starting transfers between devices  12.5 us (36%)
  waiting for transfers between devices  5.47 us (16%)
  between operations  0.73 us (2%)
    pallas_call x7, Pallas kernels, call(): pl.pallas_call(kernel, out_shape=shapes, in_specs=[pl.BlockSpec(memory_sp...  15.4 us
    ppermute x8, starting transfers between devices, swapped(): lax.ppermute(x, axis, [(i, partner(i)) for i in range(lax.axis_size(axis))])  8.27 us
    ppermute x2, starting transfers between devices, swapped_all(): return lax.ppermute(x, ('gx', 'gy'), pairs)  4.26 us
    ppermute x2, waiting for transfers between devices, swapped_all(): return lax.ppermute(x, ('gx', 'gy'), pairs)  3.2 us
    ppermute x8, waiting for transfers between devices, swapped(): lax.ppermute(x, axis, [(i, partner(i)) for i in range(lax.axis_size(axis))])  2.27 us
  transfers between devices with their start and end apart: 10, of which 4 were waited for; matrix products, arithmetic and copies ran while one was open for 0% of the time, Pallas kernels for 21%

profile of v5, /device:TPU:18, one launch (start us, length us, event | category | flops | bytes accessed | tf_op | source)
XLA Modules:
  0.0 34.3 jit_solution(7489341671477436197)
XLA Ops:
  0.6 2.7 %shard_map.95 = (f32[1056,128]{1,0:T(8,128)S(1)}, s32[128]{0:T(128)S(1)}, s32[128]{0:T(128)S(1)}) custom-call(s32[128]{0:T(128)} %dest_hbm.1, s32[128]{0:T(128)} %counts_hbm.1, s32[128]{0:T(128)} %elem_hbm.1, f32[3,128,128]{2,1,0:T(8,128)} %bitcast.8, f32[3,128,128]{2,1,0:T(8,128)} %bitcast.9, f32[256,128]{1,0:T(8,128)} %bitcast.10), custom_call_target="tpu_custom_call" | custom-call | tf_op jit(solution)/shard_map/pallas_call | solution.py:70
  3.4 2.2 %collective-permute-start.2 = (f32[264,128]{1,0:T(8,128)S(1)}, f32[264,128]{1,0:T(8,128)S(1)}, u32[]{:S(2)}, u32[]{:S(2)}) collective-permute-start(f32[264,128]{1,0:T(8,128)S(1)} %get-tuple-element.42), channel_id=1, source_target_pairs={{0,2},{1,3},{2,0},{3,1},{4,6},{5,7},{6,4},{7,5},{8,10},{9,11},{10,... | collective-permute-start | bytes 405512 | tf_op jit(solution)/shard_map/ppermute | solution.py:460
  5.6 1.4 %collective-permute-start.1 = (f32[264,128]{1,0:T(8,128)S(1)}, f32[264,128]{1,0:T(8,128)S(1)}, u32[]{:S(2)}, u32[]{:S(2)}) collective-permute-start(f32[264,128]{1,0:T(8,128)S(1)} %get-tuple-element.44), channel_id=1, source_target_pairs={{0,1},{1,0},{2,3},{3,2},{4,5},{5,4},{6,7},{7,6},{8,9},{9,8},{10,11... | collective-permute-start | bytes 405512 | tf_op jit(solution)/shard_map/ppermute | solution.py:460
  7.0 0.5 %collective-permute-start = (f32[264,128]{1,0:T(8,128)S(1)}, f32[264,128]{1,0:T(8,128)S(1)}, u32[]{:S(2)}, u32[]{:S(2)}) collective-permute-start(f32[264,128]{1,0:T(8,128)S(1)} %get-tuple-element.45), channel_id=1, source_target_pairs={{0,3},{1,2},{2,1},{3,0},{4,7},{5,6},{6,5},{7,4},{8,11},{9,10},{10,... | collective-permute-start | bytes 405512 | tf_op jit(solution)/shard_map/ppermute | solution.py:460
  7.5 3.1 %shard_map.96 = (f32[3264,128]{1,0:T(8,128)S(1)}, f32[4896,128]{1,0:T(8,128)S(1)}, f32[96,128]{1,0:T(8,128)S(1)}, f32[168,128]{1,0:T(8,128)S(1)}) custom-call(s32[128]{0:T(128)S(1)} %get-tuple-element.22.elem, f32[264,128]{1,0:T(8,128)S(1)} %get-tuple-element.43.group, bf16[24,16,512]{2,1,0:T(8,128)(2,1)} %bitcast.12, f32[168,128]{1,0:T(8,128)} %constant.2.clone.nodes), custom_call_target="tpu_custom_call" | custom-call | flops 2000000000 | tf_op jit(solution)/shard_map/pallas_call | solution.py:70
  10.7 0.7 %collective-permute-done.2.group = f32[264,128]{1,0:T(8,128)S(1)} collective-permute-done((f32[264,128]{1,0:T(8,128)S(1)}, f32[264,128]{1,0:T(8,128)S(1)}, u32[]{:S(2)}, u32[]{:S(2)}) %collective-permute-start.2) | collective-permute-done | bytes 135200 | tf_op jit(solution)/shard_map/ppermute | solution.py:460
  11.4 2.1 %shard_map.97 = (f32[96,128]{1,0:T(8,128)S(1)}, f32[4896,128]{1,0:T(8,128)S(1)}) custom-call(f32[264,128]{1,0:T(8,128)S(1)} %collective-permute-done.2.group, f32[3264,128]{1,0:T(8,128)S(1)} %get-tuple-element.23.field, f32[168,128]{1,0:T(8,128)S(1)} %get-tuple-element.24.nodes, f32[4896,128]{1,0:T(8,128)S(1)} %get-tuple-element.25._), custom_call_target="tpu_custom_call", output_to_operand_aliasing={{1}: (3, {})} | custom-call | flops 2000000000 | tf_op jit(solution)/shard_map/pallas_call | solution.py:70
  13.5 0.0 collective-permute-done.1.gb
  13.5 0.0 collective-permute-done.ga
  13.5 3.7 %shard_map.98 = (f32[96,128]{1,0:T(8,128)S(1)}, f32[96,128]{1,0:T(8,128)S(1)}, f32[24,16,512]{2,1,0:T(8,128)S(1)}, f32[24,16,512]{2,1,0:T(8,128)S(1)}, f32[4896,128]{1,0:T(8,128)S(1)}) custom-call(f32[264,128]{1,0:T(8,128)S(1)} %collective-permute-done.ga, f32[264,128]{1,0:T(8,128)S(1)} %collective-permute-done.1.gb, ...), custom_call_target="tpu_custom_call", output_to_operand_aliasing={{4}: (4, {})} | custom-call | tf_op jit(solution)/shard_map/pallas_call | solution.py:70
  17.2 0.1 fusion
  17.3 2.7 %collective-permute-start.4 = (f32[12,16,512]{2,1,0:T(8,128)S(1)}, f32[12,16,512]{2,1,0:T(8,128)S(1)}, u32[]{:S(2)}, u32[]{:S(2)}) collective-permute-start(f32[12,16,512]{2,1,0:T(8,128)S(1)} %get-tuple-element.40), channel_id=1, source_target_pairs={{0,1},{1,0},{2,3},{3,2},{4,8},{5,9},{6,10},{7,11},{8,4},{9,5},{10,... | collective-permute-start | bytes 1179656 | tf_op jit(solution)/shard_map/ppermute | solution.py:470
  20.0 0.0 collective-permute-start.3
  20.0 0.6 %collective-permute-start.7 = (f32[96,128]{1,0:T(8,128)S(1)}, f32[96,128]{1,0:T(8,128)S(1)}, u32[]{:S(2)}, u32[]{:S(2)}) collective-permute-start(f32[96,128]{1,0:T(8,128)S(1)} %get-tuple-element.33), channel_id=1, source_target_pairs={{0,1},{1,0},{2,3},{3,2},{4,5},{5,4},{6,7},{7,6},{8,9},{9,8},{10,11... | collective-permute-start | bytes 147464 | tf_op jit(solution)/shard_map/ppermute | solution.py:460
  20.6 2.5 %collective-permute-start.9 = (f32[96,128]{1,0:T(8,128)S(1)}, f32[96,128]{1,0:T(8,128)S(1)}, u32[]{:S(2)}, u32[]{:S(2)}) collective-permute-start(f32[96,128]{1,0:T(8,128)S(1)} %get-tuple-element.35), channel_id=1, source_target_pairs={{0,3},{1,2},{2,1},{3,0},{4,7},{5,6},{6,5},{7,4},{8,11},{9,10},{10,... | collective-permute-start | bytes 147464 | tf_op jit(solution)/shard_map/ppermute | solution.py:460
  23.1 0.9 %collective-permute-start.8 = (f32[96,128]{1,0:T(8,128)S(1)}, f32[96,128]{1,0:T(8,128)S(1)}, u32[]{:S(2)}, u32[]{:S(2)}) collective-permute-start(f32[96,128]{1,0:T(8,128)S(1)} %get-tuple-element.34), channel_id=1, source_target_pairs={{0,2},{1,3},{2,0},{3,1},{4,6},{5,7},{6,4},{7,5},{8,10},{9,11},{10,... | collective-permute-start | bytes 147464 | tf_op jit(solution)/shard_map/ppermute | solution.py:460
  24.1 2.6 %collective-permute-done.4.refs_3_ = f32[12,16,512]{2,1,0:T(8,128)S(1)} collective-permute-done((f32[12,16,512]{2,1,0:T(8,128)S(1)}, f32[12,16,512]{2,1,0:T(8,128)S(1)}, u32[]{:S(2)}, u32[]{:S(2)}) %collective-permute-start.4) | collective-permute-done | bytes 393248 | tf_op jit(solution)/shard_map/ppermute | solution.py:470
  26.7 0.0 collective-permute-done.3.refs_2_
  26.7 0.4 %shard_map.99 = (f32[24,16,512]{2,1,0:T(8,128)S(1)}, f32[96,128]{1,0:T(8,128)S(1)}) custom-call(f32[24,16,512]{2,1,0:T(8,128)S(1)} %get-tuple-element.27.refs_0_, f32[24,16,512]{2,1,0:T(8,128)S(1)} %get-tuple-element.28.refs_1_, f32[12,16,512]{2,1,0:T(8,128)S(1)} %collective-permute-done.3.refs_2_, f32[12,16,512]{2,1,0:T(8,128)S(1)} %collective-permute-done.4.refs_3_), custom_call_target="tpu_custom_call" | custom-call | tf_op jit(solution)/shard_map/pallas_call | solution.py:70
  27.1 1.6 %collective-permute-start.6 = (f32[48,128]{1,0:T(8,128)S(1)}, f32[48,128]{1,0:T(8,128)S(1)}, u32[]{:S(2)}, u32[]{:S(2)}) collective-permute-start(f32[48,128]{1,0:T(8,128)S(1)} %get-tuple-element.46), channel_id=1, source_target_pairs={{0,4},{1,2},{2,1},{3,7},{4,0},{5,6},{6,5},{7,3},{8,12},{9,10},{10,... | collective-permute-start | bytes 73736 | tf_op jit(solution)/shard_map/ppermute | solution.py:470
  28.7 0.0 collective-permute-start.5
  28.7 0.0 collective-permute-done.7.d1
  28.7 0.0 collective-permute-done.9.d3
  28.7 0.0 collective-permute-done.8.d2
  28.8 1.7 %shard_map.100 = (f32[384,128]{1,0:T(8,128)S(1)}, f32[24,16,512]{2,1,0:T(8,128)S(1)}) custom-call(s32[128]{0:T(128)S(1)} %get-tuple-element.31.block, f32[24,16,512]{2,1,0:T(8,128)S(1)} %get-tuple-element.29.field, f32[96,128]{1,0:T(8,128)S(1)} %get-tuple-element.32.d0, f32[96,128]{1,0:T(8,128)S(1)} %collective-permute-done.7.d1, ...), custom_call_target="tpu_custom_call" | custom-call | flops 1000000000 | tf_op jit(solution)/shard_map/pallas_call | solution.py:70
  30.4 0.6 %collective-permute-done.6.got3 = f32[48,128]{1,0:T(8,128)S(1)} collective-permute-done((f32[48,128]{1,0:T(8,128)S(1)}, f32[48,128]{1,0:T(8,128)S(1)}, u32[]{:S(2)}, u32[]{:S(2)}) %collective-permute-start.6) | collective-permute-done | bytes 24608 | tf_op jit(solution)/shard_map/ppermute | solution.py:470
  31.0 1.5 %collective-permute-done.5.got1 = f32[48,128]{1,0:T(8,128)S(1)} collective-permute-done((f32[48,128]{1,0:T(8,128)S(1)}, f32[48,128]{1,0:T(8,128)S(1)}, u32[]{:S(2)}, u32[]{:S(2)}) %collective-permute-start.5) | collective-permute-done | bytes 24608 | tf_op jit(solution)/shard_map/ppermute | solution.py:460
  32.5 1.7 %shard_map.101 = (f32[384,128]{1,0:T(8,128)}, f32[24,16,512]{2,1,0:T(8,128)}) custom-call(f32[24,16,512]{2,1,0:T(8,128)S(1)} %get-tuple-element.29.field, f32[48,128]{1,0:T(8,128)S(1)} %collective-permute-done.5.got1, f32[48,128]{1,0:T(8,128)S(1)} %collective-permute-done.6.got3, f32[24,16,512]{2,1,0:T(8,128)S(1)} %get-tuple-element.36.done, ...), custom_call_target="tpu_custom_call" | custom-call | tf_op jit(solution)/shard_map/pallas_call | solution.py:70
  (2 shorter events, 0.0 us)
Async XLA Ops:
  3.4 8.0 %collective-permute-start.2 = (f32[264,128]{1,0:T(8,128)S(1)}, f32[264,128]{1,0:T(8,128)S(1)}, u32[]{:S(2)}, u32[]{:S(2)}) collective-permute-start(f32[264,128]{1,0:T(8,128)S(1)} %get-tuple-element.42), channel_id=1, source_target_pairs={{0,2},{1,3},{2,0},{3,1},{4,6},{5,7},{6,4},{7,5},{8,10},{9,11},{10,... | collective-permute-start | bytes 405512 | tf_op jit(solution)/shard_map/ppermute | solution.py:460
  5.6 7.9 %collective-permute-start.1 = (f32[264,128]{1,0:T(8,128)S(1)}, f32[264,128]{1,0:T(8,128)S(1)}, u32[]{:S(2)}, u32[]{:S(2)}) collective-permute-start(f32[264,128]{1,0:T(8,128)S(1)} %get-tuple-element.44), channel_id=1, source_target_pairs={{0,1},{1,0},{2,3},{3,2},{4,5},{5,4},{6,7},{7,6},{8,9},{9,8},{10,11... | collective-permute-start | bytes 405512 | tf_op jit(solution)/shard_map/ppermute | solution.py:460
  7.0 6.5 %collective-permute-start = (f32[264,128]{1,0:T(8,128)S(1)}, f32[264,128]{1,0:T(8,128)S(1)}, u32[]{:S(2)}, u32[]{:S(2)}) collective-permute-start(f32[264,128]{1,0:T(8,128)S(1)} %get-tuple-element.45), channel_id=1, source_target_pairs={{0,3},{1,2},{2,1},{3,0},{4,7},{5,6},{6,5},{7,4},{8,11},{9,10},{10,... | collective-permute-start | bytes 405512 | tf_op jit(solution)/shard_map/ppermute | solution.py:460
  17.3 9.4 %collective-permute-start.4 = (f32[12,16,512]{2,1,0:T(8,128)S(1)}, f32[12,16,512]{2,1,0:T(8,128)S(1)}, u32[]{:S(2)}, u32[]{:S(2)}) collective-permute-start(f32[12,16,512]{2,1,0:T(8,128)S(1)} %get-tuple-element.40), channel_id=1, source_target_pairs={{0,1},{1,0},{2,3},{3,2},{4,8},{5,9},{6,10},{7,11},{8,4},{9,5},{10,... | collective-permute-start | bytes 1179656 | tf_op jit(solution)/shard_map/ppermute | solution.py:470
  20.0 6.7 %collective-permute-start.3 = (f32[12,16,512]{2,1,0:T(8,128)S(1)}, f32[12,16,512]{2,1,0:T(8,128)S(1)}, u32[]{:S(2)}, u32[]{:S(2)}) collective-permute-start(f32[12,16,512]{2,1,0:T(8,128)S(1)} %get-tuple-element.41), channel_id=1, source_target_pairs={{0,4},{4,0},{8,12},{12,8},{16,20},{20,16},{24,28},{28,24},{32,36},... | collective-permute-start | bytes 1179656 | tf_op jit(solution)/shard_map/ppermute | solution.py:460
  20.0 8.7 %collective-permute-start.7 = (f32[96,128]{1,0:T(8,128)S(1)}, f32[96,128]{1,0:T(8,128)S(1)}, u32[]{:S(2)}, u32[]{:S(2)}) collective-permute-start(f32[96,128]{1,0:T(8,128)S(1)} %get-tuple-element.33), channel_id=1, source_target_pairs={{0,1},{1,0},{2,3},{3,2},{4,5},{5,4},{6,7},{7,6},{8,9},{9,8},{10,11... | collective-permute-start | bytes 147464 | tf_op jit(solution)/shard_map/ppermute | solution.py:460
  20.6 8.1 %collective-permute-start.9 = (f32[96,128]{1,0:T(8,128)S(1)}, f32[96,128]{1,0:T(8,128)S(1)}, u32[]{:S(2)}, u32[]{:S(2)}) collective-permute-start(f32[96,128]{1,0:T(8,128)S(1)} %get-tuple-element.35), channel_id=1, source_target_pairs={{0,3},{1,2},{2,1},{3,0},{4,7},{5,6},{6,5},{7,4},{8,11},{9,10},{10,... | collective-permute-start | bytes 147464 | tf_op jit(solution)/shard_map/ppermute | solution.py:460
  23.1 5.6 %collective-permute-start.8 = (f32[96,128]{1,0:T(8,128)S(1)}, f32[96,128]{1,0:T(8,128)S(1)}, u32[]{:S(2)}, u32[]{:S(2)}) collective-permute-start(f32[96,128]{1,0:T(8,128)S(1)} %get-tuple-element.34), channel_id=1, source_target_pairs={{0,2},{1,3},{2,0},{3,1},{4,6},{5,7},{6,4},{7,5},{8,10},{9,11},{10,... | collective-permute-start | bytes 147464 | tf_op jit(solution)/shard_map/ppermute | solution.py:460
  27.1 3.9 %collective-permute-start.6 = (f32[48,128]{1,0:T(8,128)S(1)}, f32[48,128]{1,0:T(8,128)S(1)}, u32[]{:S(2)}, u32[]{:S(2)}) collective-permute-start(f32[48,128]{1,0:T(8,128)S(1)} %get-tuple-element.46), channel_id=1, source_target_pairs={{0,4},{1,2},{2,1},{3,7},{4,0},{5,6},{6,5},{7,3},{8,12},{9,10},{10,... | collective-permute-start | bytes 73736 | tf_op jit(solution)/shard_map/ppermute | solution.py:470
  28.7 3.8 %collective-permute-start.5 = (f32[48,128]{1,0:T(8,128)S(1)}, f32[48,128]{1,0:T(8,128)S(1)}, u32[]{:S(2)}, u32[]{:S(2)}) collective-permute-start(f32[48,128]{1,0:T(8,128)S(1)} %get-tuple-element.47), channel_id=1, source_target_pairs={{0,1},{1,0},{2,3},{3,2},{4,5},{5,4},{6,7},{7,6},{8,9},{9,8},{10,11... | collective-permute-start | bytes 73736 | tf_op jit(solution)/shard_map/ppermute | solution.py:460

commit v6 on v5

--- a/solution.py
+++ b/solution.py
@@ -44,9 +44,7 @@
 
 
 PITCH = 17
-ORDER = (3, 1, 2)
-UNROLL_A = 32
-UNROLL_B = 32
+ORDER = (2, 1, 3)
 OWN_FLOPS = 2_000_000_000
 UNPACK_FLOPS = 1_000_000_000
 
@@ -85,8 +83,8 @@
 
 
 def pack_kernel(
-    dest_hbm, counts_hbm, elem_hbm, pos_hbm, vel_hbm, coef_hbm,
-    send, block, own_elem,
+    dest_hbm, counts_hbm, elem_hbm, pos_hbm, vel_hbm, coef_hbm, velocity_hbm,
+    send, block, own_elem, velocity,
     dest, counts, elem, pos, vel, coef, sem,
 ):
     tables = [
@@ -104,7 +102,8 @@
         halves.append(
             [pltpu.make_async_copy(a, b, sem.at[3 + 3 * k + n]) for n, (a, b) in enumerate(pairs)]
         )
-    for copy in tables + halves[0] + halves[1]:
+    fetch = pltpu.make_async_copy(velocity_hbm, velocity, sem.at[9])
+    for copy in tables + halves[0] + halves[1] + [fetch]:
         copy.start()
     me = lax.axis_index("gy")
     lane = lanes()
@@ -133,6 +132,7 @@
         for copy in halves[k]:
             copy.wait()
         state = lax.fori_loop(64 * k, 64 * k + 64, one, state, unroll=8)
+    fetch.wait()
     labels = state[1].astype(F32)
     for d in range(N_GY):
         send[d * ROWS + 256 : d * ROWS + 264, :] = jnp.broadcast_to(labels[d : d + 1, :], (8, 128))
@@ -176,22 +176,19 @@
     lax.fori_loop(0, 8, one, 0)
 
 
-def interpolate(group, element, field, nodes, fluid):
-    def one(r, _):
-        e = element(r)
-        basis_r = lagrange(group[pl.ds(r, 1), :], nodes, 8)
-        basis_s = lagrange(group[pl.ds(r + 32, 1), :], nodes, 0)
-        basis_t = lagrange(group[pl.ds(r + 64, 1), :], nodes, 0)
+def interpolate(group, elements, field, nodes, fluid):
+    for r in range(SHARE):
+        e = elements[r]
+        basis_r = lagrange(group[r : r + 1, :], nodes, 8)
+        basis_s = lagrange(group[r + 32 : r + 33, :], nodes, 0)
+        basis_t = lagrange(group[r + 64 : r + 65, :], nodes, 0)
         high, low = split_two(outer(basis_s, basis_t))
         nodal = field[pl.ds((e >> 4) * (24 * PITCH) + (e & 15), 24, stride=PITCH), :].astype(BF16)
         part = jnp.dot(nodal, jnp.concatenate([high, low], axis=0), preferred_element_type=F32)
         for c in range(3):
-            fluid[pl.ds(c * 32 + r, 1), :] = jnp.sum(
+            fluid[c * 32 + r : c * 32 + r + 1, :] = jnp.sum(
                 part[8 * c : 8 * c + 8, :] * basis_r, axis=0, keepdims=True
             )
-        return 0
-
-    lax.fori_loop(0, SHARE, one, 0, unroll=UNROLL_A)
 
 
 def find_drag(group, fluid, drag):
@@ -206,21 +203,21 @@
         drag[32 * c : 32 * c + 32, :] = factor * w[c]
 
 
-def project(group, element, drag, nodes, parts):
+def project(group, elements, drag, nodes, parts):
     low_half = lanes() < 64
     upper_rows = lax.broadcasted_iota(jnp.int32, (8, 128), 0) < 4
 
-    def one(r, _):
-        e = element(r)
-        x = group[pl.ds(r, 1), :]
+    for r in range(SHARE):
+        e = elements[r]
+        x = group[r : r + 1, :]
         near = [gauss(x, nodes, 17 + k) for k in range(2)]
         after = [gauss(x, nodes, 19 + k) for k in range(2)]
         planes = outer(
-            gauss(group[pl.ds(r + 32, 1), :], nodes, 16),
-            gauss(group[pl.ds(r + 64, 1), :], nodes, 16),
+            gauss(group[r + 32 : r + 33, :], nodes, 16),
+            gauss(group[r + 64 : r + 65, :], nodes, 16),
         )
         planes = jnp.concatenate(split_two(planes), axis=0)
-        force = [-drag[pl.ds(c * 32 + r, 1), :] for c in range(3)]
+        force = [-drag[c * 32 + r : c * 32 + r + 1, :] for c in range(3)]
         mixed = jnp.where(upper_rows, force[0], force[1])
         rows = []
         for k in range(2):
@@ -238,47 +235,31 @@
             t = t + pltpu.roll(jnp.where(low_half, odd, even), 64, 1)
             n = 8 if k < 4 else 4
             parts[pl.ds(at + k * 8 * PITCH, n, stride=PITCH), :] = t[0:n, :]
-        return 0
-
-    lax.fori_loop(0, SHARE, one, 0, unroll=UNROLL_B)
 
 
 def own_kernel(elem, group, vel, nodes, field, parts, drag, table, fluid):
-    def element(r):
-        return elem[r]
-
     table[...] = nodes[...]
     spread_field(vel, field)
-    interpolate(group, element, field, nodes, fluid)
+    elements = [elem[r] for r in range(SHARE)]
+    interpolate(group, elements, field, nodes, fluid)
     find_drag(group, fluid, drag)
-    project(group, element, drag, nodes, parts)
-
-
-def fetch_elements(groups, lab_v, lab_s, sem):
-    for k, g in enumerate(groups):
-        lab_v[k : k + 1, :] = g[256:257, :].astype(jnp.int32)
-    copy = pltpu.make_async_copy(lab_v, lab_s, sem)
-    copy.start()
-    copy.wait()
-    return [lambda r, k=k: lab_s[k, r] for k in range(len(groups))]
-
-
-def middle_kernel(group, field, nodes, _, drag, parts, fluid, lab_v, lab_s, sem):
-    (element,) = fetch_elements((group,), lab_v, lab_s, sem)
-    interpolate(group, element, field, nodes, fluid)
+    project(group, elements, drag, nodes, parts)
+
+
+def element_list(group):
+    labels = group[256:257, :].astype(jnp.int32)
+    return [labels[0, r] for r in range(SHARE)]
+
+
+def middle_kernel(group, field, nodes, _, drag, parts, fluid):
+    elements = element_list(group)
+    interpolate(group, elements, field, nodes, fluid)
     find_drag(group, fluid, drag)
-    project(group, element, drag, nodes, parts)
-
-
-def rest_kernel(ga, gb, field, nodes, _, da, db, inside, ghosts, parts, fluid, lab_v, lab_s, sem):
-    groups = (ga, gb)
-    drags = (da, db)
-    elements = fetch_elements(groups, lab_v, lab_s, sem)
-    for k in range(2):
-        interpolate(groups[k], elements[k], field, nodes, fluid)
-        find_drag(groups[k], fluid, drags[k])
-    for k in range(2):
-        project(groups[k], elements[k], drags[k], nodes, parts)
+    project(group, elements, drag, nodes, parts)
+
+
+def rest_kernel(group, field, nodes, _, drag, inside, ghosts, parts, fluid):
+    middle_kernel(group, field, nodes, None, drag, parts, fluid)
     gather_parts(parts, inside, ghosts)
 
 
@@ -475,13 +456,13 @@
     vel = part_vel.transpose(1, 0, 2)
     coef = part_coef.reshape(256, 128)
     nodes = jnp.asarray(node_table())
-    send, block, own_elem = call(
+    send, block, own_elem, velocity_here = call(
         pack_kernel,
-        [((N_GY * ROWS, 128), F32, "vmem"), ((128,), jnp.int32, "smem"), ((128,), jnp.int32, "smem")],
-        [(a, "raw") for a in (dest, counts, elem, pos, vel, coef)],
+        [((N_GY * ROWS, 128), F32, "vmem"), ((128,), jnp.int32, "smem"), ((128,), jnp.int32, "smem"), ((24, 16, 512), BF16, "vmem")],
+        [(a, "raw") for a in (dest, counts, elem, pos, vel, coef, velocity.reshape(24, 16, 512))],
         (SMEM((128,), jnp.int32),) * 3
         + (VMEM(pos.shape, F32),) * 2
-        + (VMEM(coef.shape, F32), pltpu.SemaphoreType.DMA((9,))),
+        + (VMEM(coef.shape, F32), pltpu.SemaphoreType.DMA((10,))),
     )
     own = send[:ROWS]
     groups = {
@@ -490,34 +471,29 @@
     field, parts, drag_own, table = call(
         own_kernel,
         [((8 * 24 * PITCH, 128), F32, "vmem"), ((8 * 36 * PITCH, 128), F32, "vmem"), ((96, 128), F32, "vmem"), (nodes.shape, F32, "vmem")],
-        [(own_elem, "smem"), (own, "vmem"), (velocity.reshape(24, 16, 512), "hbm"), (nodes, "hbm")],
+        [(own_elem, "smem"), (own, "vmem"), (velocity_here, "vmem"), (nodes, "hbm")],
         (VMEM((96, 128), F32),),
         flops=OWN_FLOPS,
     )
-    labels = (
-        VMEM((96, 128), F32),
-        VMEM((8, 128), jnp.int32),
-        SMEM((8, 128), jnp.int32),
-        pltpu.SemaphoreType.DMA,
-    )
-    first, *others = reversed(ORDER)
+    fluid = (VMEM((96, 128), F32),)
     drags = {}
-    drags[first], parts = call(
-        middle_kernel,
-        [((96, 128), F32, "vmem"), ((8 * 36 * PITCH, 128), F32, "vmem")],
-        [(a, "vmem") for a in (groups[first], field, table, parts)],
-        labels,
-        flops=OWN_FLOPS,
-        aliases={3: 1},
-    )
-    drags[others[1]], drags[others[0]], inside, ghosts, _ = call(
+    for k in ORDER[:2]:
+        drags[k], parts = call(
+            middle_kernel,
+            [((96, 128), F32, "vmem"), ((8 * 36 * PITCH, 128), F32, "vmem")],
+            [(a, "vmem") for a in (groups[k], field, table, parts)],
+            fluid,
+            flops=OWN_FLOPS,
+            aliases={3: 1},
+        )
+    drags[ORDER[2]], inside, ghosts, _ = call(
         rest_kernel,
-        [((96, 128), F32, "vmem")] * 2
+        [((96, 128), F32, "vmem")]
         + [((24, 16, 512), F32, "vmem")] * 2
         + [((8 * 36 * PITCH, 128), F32, "vmem")],
-        [(a, "vmem") for a in (groups[others[1]], groups[others[0]], field, table, parts)],
-        labels,
-        aliases={4: 4},
+        [(a, "vmem") for a in (groups[ORDER[2]], field, table, parts)],
+        fluid,
+        aliases={3: 3},
     )
     last_gx = lax.axis_size("gx") - 1
 

time: 34.4 us -> 33 us (0.959)
  Pallas kernels: 15.4 us -> 13.9 us
  waiting for transfers between devices: 5.47 us -> 6.77 us
  starting transfers between devices: 12.5 us -> 11.4 us
    pallas_call x7 -> x8, Pallas kernels: 15.4 us -> 13.9 us  [call(): pl.pallas_call(kernel, out_shape=shapes, in_specs=[pl.BlockSpec(memory_sp...]
    ppermute x2, waiting for transfers between devices: 3.2 us -> 4.39 us  [swapped_all(): return lax.ppermute(x, ('gx', 'gy'), pairs)]
    ppermute x8, starting transfers between devices: 8.27 us -> 7.67 us  [swapped(): lax.ppermute(x, axis, [(i, partner(i)) for i in range(lax.axis_size(axis))])]
    ppermute x2, starting transfers between devices: 4.26 us -> 3.71 us  [swapped_all(): return lax.ppermute(x, ('gx', 'gy'), pairs)]
  transfers between devices with their start and end apart: 10 -> 10, of which waited for: 4 -> 5; matrix products, arithmetic and copies ran while one was open for 0% -> 0% of each run, Pallas kernels for 21% -> 24%
where the time goes in v6:
time: 33 us; the launch traced here: 32.9 us
  Pallas kernels  13.9 us (42%)
  starting transfers between devices  11.4 us (35%)
  waiting for transfers between devices  6.77 us (21%)
  between operations  0.71 us (2%)
    pallas_call x8, Pallas kernels, call(): pl.pallas_call(kernel, out_shape=shapes, in_specs=[pl.BlockSpec(memory_sp...  13.9 us
    ppermute x8, starting transfers between devices, swapped(): lax.ppermute(x, axis, [(i, partner(i)) for i in range(lax.axis_size(axis))])  7.67 us
    ppermute x2, waiting for transfers between devices, swapped_all(): return lax.ppermute(x, ('gx', 'gy'), pairs)  4.39 us
    ppermute x2, starting transfers between devices, swapped_all(): return lax.ppermute(x, ('gx', 'gy'), pairs)  3.71 us
    ppermute x8, waiting for transfers between devices, swapped(): lax.ppermute(x, axis, [(i, partner(i)) for i in range(lax.axis_size(axis))])  2.38 us
  transfers between devices with their start and end apart: 10, of which 5 were waited for; matrix products, arithmetic and copies ran while one was open for 0% of the time, Pallas kernels for 24%

profile of v6, /device:TPU:18, one launch (start us, length us, event | category | flops | bytes accessed | tf_op | source)
XLA Modules:
  0.0 32.9 jit_solution(782599639065574261)
XLA Ops:
  0.6 2.7 %shard_map.95 = (f32[1056,128]{1,0:T(8,128)S(1)}, s32[128]{0:T(128)S(1)}, s32[128]{0:T(128)S(1)}, bf16[24,16,512]{2,1,0:T(8,128)(2,1)S(1)}) custom-call(s32[128]{0:T(128)} %dest_hbm.1, s32[128]{0:T(128)} %counts_hbm.1, s32[128]{0:T(128)} %elem_hbm.1, f32[3,128,128]{2,1,0:T(8,128)} %bitcast.9, f32[3,128,128]{2,1,0:T(8,128)} %bitcast.10, f32[256,128]{1,0:T(8,128)} %bitcast.11, ...), custom_call_target="tpu_custom_call" | custom-call | tf_op jit(solution)/shard_map/pallas_call | solution.py:68
  3.4 2.2 %collective-permute-start.2 = (f32[264,128]{1,0:T(8,128)S(1)}, f32[264,128]{1,0:T(8,128)S(1)}, u32[]{:S(2)}, u32[]{:S(2)}) collective-permute-start(f32[264,128]{1,0:T(8,128)S(1)} %get-tuple-element.46), channel_id=1, source_target_pairs={{0,2},{1,3},{2,0},{3,1},{4,6},{5,7},{6,4},{7,5},{8,10},{9,11},{10,... | collective-permute-start | bytes 405512 | tf_op jit(solution)/shard_map/ppermute | solution.py:441
  5.6 1.4 %collective-permute-start.1 = (f32[264,128]{1,0:T(8,128)S(1)}, f32[264,128]{1,0:T(8,128)S(1)}, u32[]{:S(2)}, u32[]{:S(2)}) collective-permute-start(f32[264,128]{1,0:T(8,128)S(1)} %get-tuple-element.47), channel_id=1, source_target_pairs={{0,1},{1,0},{2,3},{3,2},{4,5},{5,4},{6,7},{7,6},{8,9},{9,8},{10,11... | collective-permute-start | bytes 405512 | tf_op jit(solution)/shard_map/ppermute | solution.py:441
  7.0 0.5 %collective-permute-start = (f32[264,128]{1,0:T(8,128)S(1)}, f32[264,128]{1,0:T(8,128)S(1)}, u32[]{:S(2)}, u32[]{:S(2)}) collective-permute-start(f32[264,128]{1,0:T(8,128)S(1)} %get-tuple-element.49), channel_id=1, source_target_pairs={{0,3},{1,2},{2,1},{3,0},{4,7},{5,6},{6,5},{7,4},{8,11},{9,10},{10,... | collective-permute-start | bytes 405512 | tf_op jit(solution)/shard_map/ppermute | solution.py:441
  7.6 3.0 %shard_map.96 = (f32[3264,128]{1,0:T(8,128)S(1)}, f32[4896,128]{1,0:T(8,128)S(1)}, f32[96,128]{1,0:T(8,128)S(1)}, f32[168,128]{1,0:T(8,128)S(1)}) custom-call(s32[128]{0:T(128)S(1)} %get-tuple-element.24.elem, f32[264,128]{1,0:T(8,128)S(1)} %get-tuple-element.48.group, bf16[24,16,512]{2,1,0:T(8,128)(2,1)S(1)} %get-tuple-element.25.vel, ...), custom_call_target="tpu_custom_call" | custom-call | flops 2000000000 | tf_op jit(solution)/shard_map/pallas_call | solution.py:68
  10.6 0.9 %collective-permute-done.2.group = f32[264,128]{1,0:T(8,128)S(1)} collective-permute-done((f32[264,128]{1,0:T(8,128)S(1)}, f32[264,128]{1,0:T(8,128)S(1)}, u32[]{:S(2)}, u32[]{:S(2)}) %collective-permute-start.2) | collective-permute-done | bytes 135200 | tf_op jit(solution)/shard_map/ppermute | solution.py:441
  11.4 1.3 %shard_map.97 = (f32[96,128]{1,0:T(8,128)S(1)}, f32[4896,128]{1,0:T(8,128)S(1)}) custom-call(f32[264,128]{1,0:T(8,128)S(1)} %collective-permute-done.2.group, f32[3264,128]{1,0:T(8,128)S(1)} %get-tuple-element.26.field, f32[168,128]{1,0:T(8,128)S(1)} %get-tuple-element.27.nodes, f32[4896,128]{1,0:T(8,128)S(1)} %get-tuple-element.28._), custom_call_target="tpu_custom_call", output_to_operand_aliasing={{1}: (3, {})} | custom-call | flops 2000000000 | tf_op jit(solution)/shard_map/pallas_call | solution.py:68
  12.8 0.5 %collective-permute-done.1.group = f32[264,128]{1,0:T(8,128)S(1)} collective-permute-done((f32[264,128]{1,0:T(8,128)S(1)}, f32[264,128]{1,0:T(8,128)S(1)}, u32[]{:S(2)}, u32[]{:S(2)}) %collective-permute-start.1) | collective-permute-done | bytes 135200 | tf_op jit(solution)/shard_map/ppermute | solution.py:441
  13.2 1.3 %shard_map.98 = (f32[96,128]{1,0:T(8,128)S(1)}, f32[4896,128]{1,0:T(8,128)S(1)}) custom-call(f32[264,128]{1,0:T(8,128)S(1)} %collective-permute-done.1.group, f32[3264,128]{1,0:T(8,128)S(1)} %get-tuple-element.26.field, f32[168,128]{1,0:T(8,128)S(1)} %get-tuple-element.27.nodes, f32[4896,128]{1,0:T(8,128)S(1)} %get-tuple-element.29._), custom_call_target="tpu_custom_call", output_to_operand_aliasing={{1}: (3, {})} | custom-call | flops 2000000000 | tf_op jit(solution)/shard_map/pallas_call | solution.py:68
  14.6 0.0 collective-permute-done.group
  14.6 1.7 %shard_map.99 = (f32[96,128]{1,0:T(8,128)S(1)}, f32[24,16,512]{2,1,0:T(8,128)S(1)}, f32[24,16,512]{2,1,0:T(8,128)S(1)}, f32[4896,128]{1,0:T(8,128)S(1)}) custom-call(f32[264,128]{1,0:T(8,128)S(1)} %collective-permute-done.group, f32[3264,128]{1,0:T(8,128)S(1)} %get-tuple-element.26.field, ...), custom_call_target="tpu_custom_call", output_to_operand_aliasing={{3}: (3, {})} | custom-call | tf_op jit(solution)/shard_map/pallas_call | solution.py:68
  16.3 0.1 fusion
  16.4 2.6 %collective-permute-start.4 = (f32[12,16,512]{2,1,0:T(8,128)S(1)}, f32[12,16,512]{2,1,0:T(8,128)S(1)}, u32[]{:S(2)}, u32[]{:S(2)}) collective-permute-start(f32[12,16,512]{2,1,0:T(8,128)S(1)} %get-tuple-element.44), channel_id=1, source_target_pairs={{0,1},{1,0},{2,3},{3,2},{4,8},{5,9},{6,10},{7,11},{8,4},{9,5},{10,... | collective-permute-start | bytes 1179656 | tf_op jit(solution)/shard_map/ppermute | solution.py:451
  19.0 0.0 collective-permute-start.3
  19.0 1.0 %collective-permute-start.9 = (f32[96,128]{1,0:T(8,128)S(1)}, f32[96,128]{1,0:T(8,128)S(1)}, u32[]{:S(2)}, u32[]{:S(2)}) collective-permute-start(f32[96,128]{1,0:T(8,128)S(1)} %get-tuple-element.39), channel_id=1, source_target_pairs={{0,3},{1,2},{2,1},{3,0},{4,7},{5,6},{6,5},{7,4},{8,11},{9,10},{10,... | collective-permute-start | bytes 147464 | tf_op jit(solution)/shard_map/ppermute | solution.py:441
  20.0 1.8 %collective-permute-start.7 = (f32[96,128]{1,0:T(8,128)S(1)}, f32[96,128]{1,0:T(8,128)S(1)}, u32[]{:S(2)}, u32[]{:S(2)}) collective-permute-start(f32[96,128]{1,0:T(8,128)S(1)} %get-tuple-element.37), channel_id=1, source_target_pairs={{0,1},{1,0},{2,3},{3,2},{4,5},{5,4},{6,7},{7,6},{8,9},{9,8},{10,11... | collective-permute-start | bytes 147464 | tf_op jit(solution)/shard_map/ppermute | solution.py:441
  21.8 0.7 %collective-permute-start.8 = (f32[96,128]{1,0:T(8,128)S(1)}, f32[96,128]{1,0:T(8,128)S(1)}, u32[]{:S(2)}, u32[]{:S(2)}) collective-permute-start(f32[96,128]{1,0:T(8,128)S(1)} %get-tuple-element.38), channel_id=1, source_target_pairs={{0,2},{1,3},{2,0},{3,1},{4,6},{5,7},{6,4},{7,5},{8,10},{9,11},{10,... | collective-permute-start | bytes 147464 | tf_op jit(solution)/shard_map/ppermute | solution.py:441
  22.5 3.3 %collective-permute-done.4.refs_3_ = f32[12,16,512]{2,1,0:T(8,128)S(1)} collective-permute-done((f32[12,16,512]{2,1,0:T(8,128)S(1)}, f32[12,16,512]{2,1,0:T(8,128)S(1)}, u32[]{:S(2)}, u32[]{:S(2)}) %collective-permute-start.4) | collective-permute-done | bytes 393248 | tf_op jit(solution)/shard_map/ppermute | solution.py:451
  25.8 0.0 collective-permute-done.3.refs_2_
  25.8 0.4 %shard_map.100 = (f32[24,16,512]{2,1,0:T(8,128)S(1)}, f32[96,128]{1,0:T(8,128)S(1)}) custom-call(f32[24,16,512]{2,1,0:T(8,128)S(1)} %get-tuple-element.31.refs_0_, f32[24,16,512]{2,1,0:T(8,128)S(1)} %get-tuple-element.32.refs_1_, f32[12,16,512]{2,1,0:T(8,128)S(1)} %collective-permute-done.3.refs_2_, f32[12,16,512]{2,1,0:T(8,128)S(1)} %collective-permute-done.4.refs_3_), custom_call_target="tpu_custom_call" | custom-call | tf_op jit(solution)/shard_map/pallas_call | solution.py:68
  26.2 1.1 %collective-permute-start.6 = (f32[48,128]{1,0:T(8,128)S(1)}, f32[48,128]{1,0:T(8,128)S(1)}, u32[]{:S(2)}, u32[]{:S(2)}) collective-permute-start(f32[48,128]{1,0:T(8,128)S(1)} %get-tuple-element.50), channel_id=1, source_target_pairs={{0,4},{1,2},{2,1},{3,7},{4,0},{5,6},{6,5},{7,3},{8,12},{9,10},{10,... | collective-permute-start | bytes 73736 | tf_op jit(solution)/shard_map/ppermute | solution.py:451
  27.3 0.0 collective-permute-start.5
  27.3 0.0 collective-permute-done.9.d3
  27.3 0.0 collective-permute-done.7.d1
  27.3 0.0 collective-permute-done.8.d2
  27.4 1.7 %shard_map.101 = (f32[384,128]{1,0:T(8,128)S(1)}, f32[24,16,512]{2,1,0:T(8,128)S(1)}) custom-call(s32[128]{0:T(128)S(1)} %get-tuple-element.35.block, f32[24,16,512]{2,1,0:T(8,128)S(1)} %get-tuple-element.33.field, f32[96,128]{1,0:T(8,128)S(1)} %get-tuple-element.36.d0, f32[96,128]{1,0:T(8,128)S(1)} %collective-permute-done.7.d1, ...), custom_call_target="tpu_custom_call" | custom-call | flops 1000000000 | tf_op jit(solution)/shard_map/pallas_call | solution.py:68
  29.0 1.1 %collective-permute-done.6.got3 = f32[48,128]{1,0:T(8,128)S(1)} collective-permute-done((f32[48,128]{1,0:T(8,128)S(1)}, f32[48,128]{1,0:T(8,128)S(1)}, u32[]{:S(2)}, u32[]{:S(2)}) %collective-permute-start.6) | collective-permute-done | bytes 24608 | tf_op jit(solution)/shard_map/ppermute | solution.py:451
  30.1 1.0 %collective-permute-done.5.got1 = f32[48,128]{1,0:T(8,128)S(1)} collective-permute-done((f32[48,128]{1,0:T(8,128)S(1)}, f32[48,128]{1,0:T(8,128)S(1)}, u32[]{:S(2)}, u32[]{:S(2)}) %collective-permute-start.5) | collective-permute-done | bytes 24608 | tf_op jit(solution)/shard_map/ppermute | solution.py:441
  31.2 1.7 %shard_map.102 = (f32[384,128]{1,0:T(8,128)}, f32[24,16,512]{2,1,0:T(8,128)}) custom-call(f32[24,16,512]{2,1,0:T(8,128)S(1)} %get-tuple-element.33.field, f32[48,128]{1,0:T(8,128)S(1)} %collective-permute-done.5.got1, f32[48,128]{1,0:T(8,128)S(1)} %collective-permute-done.6.got3, f32[24,16,512]{2,1,0:T(8,128)S(1)} %get-tuple-element.40.done, ...), custom_call_target="tpu_custom_call" | custom-call | tf_op jit(solution)/shard_map/pallas_call | solution.py:68
  (2 shorter events, 0.0 us)
Async XLA Ops:
  3.4 8.0 %collective-permute-start.2 = (f32[264,128]{1,0:T(8,128)S(1)}, f32[264,128]{1,0:T(8,128)S(1)}, u32[]{:S(2)}, u32[]{:S(2)}) collective-permute-start(f32[264,128]{1,0:T(8,128)S(1)} %get-tuple-element.46), channel_id=1, source_target_pairs={{0,2},{1,3},{2,0},{3,1},{4,6},{5,7},{6,4},{7,5},{8,10},{9,11},{10,... | collective-permute-start | bytes 405512 | tf_op jit(solution)/shard_map/ppermute | solution.py:441
  5.6 7.6 %collective-permute-start.1 = (f32[264,128]{1,0:T(8,128)S(1)}, f32[264,128]{1,0:T(8,128)S(1)}, u32[]{:S(2)}, u32[]{:S(2)}) collective-permute-start(f32[264,128]{1,0:T(8,128)S(1)} %get-tuple-element.47), channel_id=1, source_target_pairs={{0,1},{1,0},{2,3},{3,2},{4,5},{5,4},{6,7},{7,6},{8,9},{9,8},{10,11... | collective-permute-start | bytes 405512 | tf_op jit(solution)/shard_map/ppermute | solution.py:441
  7.0 7.5 %collective-permute-start = (f32[264,128]{1,0:T(8,128)S(1)}, f32[264,128]{1,0:T(8,128)S(1)}, u32[]{:S(2)}, u32[]{:S(2)}) collective-permute-start(f32[264,128]{1,0:T(8,128)S(1)} %get-tuple-element.49), channel_id=1, source_target_pairs={{0,3},{1,2},{2,1},{3,0},{4,7},{5,6},{6,5},{7,4},{8,11},{9,10},{10,... | collective-permute-start | bytes 405512 | tf_op jit(solution)/shard_map/ppermute | solution.py:441
  16.4 9.4 %collective-permute-start.4 = (f32[12,16,512]{2,1,0:T(8,128)S(1)}, f32[12,16,512]{2,1,0:T(8,128)S(1)}, u32[]{:S(2)}, u32[]{:S(2)}) collective-permute-start(f32[12,16,512]{2,1,0:T(8,128)S(1)} %get-tuple-element.44), channel_id=1, source_target_pairs={{0,1},{1,0},{2,3},{3,2},{4,8},{5,9},{6,10},{7,11},{8,4},{9,5},{10,... | collective-permute-start | bytes 1179656 | tf_op jit(solution)/shard_map/ppermute | solution.py:451
  19.0 6.8 %collective-permute-start.3 = (f32[12,16,512]{2,1,0:T(8,128)S(1)}, f32[12,16,512]{2,1,0:T(8,128)S(1)}, u32[]{:S(2)}, u32[]{:S(2)}) collective-permute-start(f32[12,16,512]{2,1,0:T(8,128)S(1)} %get-tuple-element.45), channel_id=1, source_target_pairs={{0,4},{4,0},{8,12},{12,8},{16,20},{20,16},{24,28},{28,24},{32,36},... | collective-permute-start | bytes 1179656 | tf_op jit(solution)/shard_map/ppermute | solution.py:441
  19.0 8.4 %collective-permute-start.9 = (f32[96,128]{1,0:T(8,128)S(1)}, f32[96,128]{1,0:T(8,128)S(1)}, u32[]{:S(2)}, u32[]{:S(2)}) collective-permute-start(f32[96,128]{1,0:T(8,128)S(1)} %get-tuple-element.39), channel_id=1, source_target_pairs={{0,3},{1,2},{2,1},{3,0},{4,7},{5,6},{6,5},{7,4},{8,11},{9,10},{10,... | collective-permute-start | bytes 147464 | tf_op jit(solution)/shard_map/ppermute | solution.py:441
  20.0 7.4 %collective-permute-start.7 = (f32[96,128]{1,0:T(8,128)S(1)}, f32[96,128]{1,0:T(8,128)S(1)}, u32[]{:S(2)}, u32[]{:S(2)}) collective-permute-start(f32[96,128]{1,0:T(8,128)S(1)} %get-tuple-element.37), channel_id=1, source_target_pairs={{0,1},{1,0},{2,3},{3,2},{4,5},{5,4},{6,7},{7,6},{8,9},{9,8},{10,11... | collective-permute-start | bytes 147464 | tf_op jit(solution)/shard_map/ppermute | solution.py:441
  21.8 5.6 %collective-permute-start.8 = (f32[96,128]{1,0:T(8,128)S(1)}, f32[96,128]{1,0:T(8,128)S(1)}, u32[]{:S(2)}, u32[]{:S(2)}) collective-permute-start(f32[96,128]{1,0:T(8,128)S(1)} %get-tuple-element.38), channel_id=1, source_target_pairs={{0,2},{1,3},{2,0},{3,1},{4,6},{5,7},{6,4},{7,5},{8,10},{9,11},{10,... | collective-permute-start | bytes 147464 | tf_op jit(solution)/shard_map/ppermute | solution.py:441
  26.2 3.9 %collective-permute-start.6 = (f32[48,128]{1,0:T(8,128)S(1)}, f32[48,128]{1,0:T(8,128)S(1)}, u32[]{:S(2)}, u32[]{:S(2)}) collective-permute-start(f32[48,128]{1,0:T(8,128)S(1)} %get-tuple-element.50), channel_id=1, source_target_pairs={{0,4},{1,2},{2,1},{3,7},{4,0},{5,6},{6,5},{7,3},{8,12},{9,10},{10,... | collective-permute-start | bytes 73736 | tf_op jit(solution)/shard_map/ppermute | solution.py:451
  27.3 3.8 %collective-permute-start.5 = (f32[48,128]{1,0:T(8,128)S(1)}, f32[48,128]{1,0:T(8,128)S(1)}, u32[]{:S(2)}, u32[]{:S(2)}) collective-permute-start(f32[48,128]{1,0:T(8,128)S(1)} %get-tuple-element.51), channel_id=1, source_target_pairs={{0,1},{1,0},{2,3},{3,2},{4,5},{5,4},{6,7},{7,6},{8,9},{9,8},{10,11... | collective-permute-start | bytes 73736 | tf_op jit(solution)/shard_map/ppermute | solution.py:441

commit v7 on v6

--- a/solution.py
+++ b/solution.py
@@ -44,7 +44,7 @@
 
 
 PITCH = 17
-ORDER = (2, 1, 3)
+ORDER = (1, 3, 2)
 OWN_FLOPS = 2_000_000_000
 UNPACK_FLOPS = 1_000_000_000
 

time: 33 us -> 33 us (level)
  waiting for transfers between devices: 6.77 us -> 3.59 us
  starting transfers between devices: 11.4 us -> 14.4 us
    ppermute x2, waiting for transfers between devices: 4.39 us -> 2.08 us  [swapped_all(): return lax.ppermute(x, ('gx', 'gy'), pairs)]
    ppermute x8, starting transfers between devices: 7.67 us -> 9.52 us  [swapped(): lax.ppermute(x, axis, [(i, partner(i)) for i in range(lax.axis_size(axis))])]
    ppermute x2, starting transfers between devices: 3.71 us -> 4.85 us  [swapped_all(): return lax.ppermute(x, ('gx', 'gy'), pairs)]
    ppermute x8, waiting for transfers between devices: 2.38 us -> 1.5 us  [swapped(): lax.ppermute(x, axis, [(i, partner(i)) for i in range(lax.axis_size(axis))])]
  transfers between devices with their start and end apart: 10 -> 10, of which waited for: 5 -> 2; matrix products, arithmetic and copies ran while one was open for 0% -> 0% of each run, Pallas kernels for 24% -> 24%
where the time goes in v7:
time: 33 us; the launch traced here: 32.7 us
  starting transfers between devices  14.4 us (44%)
  Pallas kernels  13.9 us (42%)
  waiting for transfers between devices  3.59 us (11%)
  between operations  0.73 us (2%)
    pallas_call x8, Pallas kernels, call(): pl.pallas_call(kernel, out_shape=shapes, in_specs=[pl.BlockSpec(memory_sp...  13.9 us
    ppermute x8, starting transfers between devices, swapped(): lax.ppermute(x, axis, [(i, partner(i)) for i in range(lax.axis_size(axis))])  9.52 us
    ppermute x2, starting transfers between devices, swapped_all(): return lax.ppermute(x, ('gx', 'gy'), pairs)  4.85 us
    ppermute x2, waiting for transfers between devices, swapped_all(): return lax.ppermute(x, ('gx', 'gy'), pairs)  2.08 us
    ppermute x8, waiting for transfers between devices, swapped(): lax.ppermute(x, axis, [(i, partner(i)) for i in range(lax.axis_size(axis))])  1.5 us
  transfers between devices with their start and end apart: 10, of which 2 were waited for; matrix products, arithmetic and copies ran while one was open for 0% of the time, Pallas kernels for 24%

profile of v7, /device:TPU:18, one launch (start us, length us, event | category | flops | bytes accessed | tf_op | source)
XLA Modules:
  0.0 32.7 jit_solution(8638998191487960816)
XLA Ops:
  0.6 2.7 %shard_map.95 = (f32[1056,128]{1,0:T(8,128)S(1)}, s32[128]{0:T(128)S(1)}, s32[128]{0:T(128)S(1)}, bf16[24,16,512]{2,1,0:T(8,128)(2,1)S(1)}) custom-call(s32[128]{0:T(128)} %dest_hbm.1, s32[128]{0:T(128)} %counts_hbm.1, s32[128]{0:T(128)} %elem_hbm.1, f32[3,128,128]{2,1,0:T(8,128)} %bitcast.9, f32[3,128,128]{2,1,0:T(8,128)} %bitcast.10, f32[256,128]{1,0:T(8,128)} %bitcast.11, ...), custom_call_target="tpu_custom_call" | custom-call | tf_op jit(solution)/shard_map/pallas_call | solution.py:68
  3.4 0.6 %collective-permute-start.2 = (f32[264,128]{1,0:T(8,128)S(1)}, f32[264,128]{1,0:T(8,128)S(1)}, u32[]{:S(2)}, u32[]{:S(2)}) collective-permute-start(f32[264,128]{1,0:T(8,128)S(1)} %get-tuple-element.46), channel_id=1, source_target_pairs={{0,1},{1,0},{2,3},{3,2},{4,5},{5,4},{6,7},{7,6},{8,9},{9,8},{10,11... | collective-permute-start | bytes 405512 | tf_op jit(solution)/shard_map/ppermute | solution.py:441
  4.0 2.2 %collective-permute-start.1 = (f32[264,128]{1,0:T(8,128)S(1)}, f32[264,128]{1,0:T(8,128)S(1)}, u32[]{:S(2)}, u32[]{:S(2)}) collective-permute-start(f32[264,128]{1,0:T(8,128)S(1)} %get-tuple-element.47), channel_id=1, source_target_pairs={{0,3},{1,2},{2,1},{3,0},{4,7},{5,6},{6,5},{7,4},{8,11},{9,10},{10,... | collective-permute-start | bytes 405512 | tf_op jit(solution)/shard_map/ppermute | solution.py:441
  6.2 1.4 %collective-permute-start = (f32[264,128]{1,0:T(8,128)S(1)}, f32[264,128]{1,0:T(8,128)S(1)}, u32[]{:S(2)}, u32[]{:S(2)}) collective-permute-start(f32[264,128]{1,0:T(8,128)S(1)} %get-tuple-element.49), channel_id=1, source_target_pairs={{0,2},{1,3},{2,0},{3,1},{4,6},{5,7},{6,4},{7,5},{8,10},{9,11},{10,... | collective-permute-start | bytes 405512 | tf_op jit(solution)/shard_map/ppermute | solution.py:441
  7.6 3.0 %shard_map.96 = (f32[3264,128]{1,0:T(8,128)S(1)}, f32[4896,128]{1,0:T(8,128)S(1)}, f32[96,128]{1,0:T(8,128)S(1)}, f32[168,128]{1,0:T(8,128)S(1)}) custom-call(s32[128]{0:T(128)S(1)} %get-tuple-element.24.elem, f32[264,128]{1,0:T(8,128)S(1)} %get-tuple-element.48.group, bf16[24,16,512]{2,1,0:T(8,128)(2,1)S(1)} %get-tuple-element.25.vel, ...), custom_call_target="tpu_custom_call" | custom-call | flops 2000000000 | tf_op jit(solution)/shard_map/pallas_call | solution.py:68
  10.6 0.0 collective-permute-done.2.group
  10.6 1.3 %shard_map.97 = (f32[96,128]{1,0:T(8,128)S(1)}, f32[4896,128]{1,0:T(8,128)S(1)}) custom-call(f32[264,128]{1,0:T(8,128)S(1)} %collective-permute-done.2.group, f32[3264,128]{1,0:T(8,128)S(1)} %get-tuple-element.26.field, f32[168,128]{1,0:T(8,128)S(1)} %get-tuple-element.27.nodes, f32[4896,128]{1,0:T(8,128)S(1)} %get-tuple-element.28._), custom_call_target="tpu_custom_call", output_to_operand_aliasing={{1}: (3, {})} | custom-call | flops 2000000000 | tf_op jit(solution)/shard_map/pallas_call | solution.py:68
  11.9 0.0 collective-permute-done.1.group
  11.9 1.3 %shard_map.98 = (f32[96,128]{1,0:T(8,128)S(1)}, f32[4896,128]{1,0:T(8,128)S(1)}) custom-call(f32[264,128]{1,0:T(8,128)S(1)} %collective-permute-done.1.group, f32[3264,128]{1,0:T(8,128)S(1)} %get-tuple-element.26.field, f32[168,128]{1,0:T(8,128)S(1)} %get-tuple-element.27.nodes, f32[4896,128]{1,0:T(8,128)S(1)} %get-tuple-element.29._), custom_call_target="tpu_custom_call", output_to_operand_aliasing={{1}: (3, {})} | custom-call | flops 2000000000 | tf_op jit(solution)/shard_map/pallas_call | solution.py:68
  13.3 0.0 collective-permute-done.group
  13.3 1.7 %shard_map.99 = (f32[96,128]{1,0:T(8,128)S(1)}, f32[24,16,512]{2,1,0:T(8,128)S(1)}, f32[24,16,512]{2,1,0:T(8,128)S(1)}, f32[4896,128]{1,0:T(8,128)S(1)}) custom-call(f32[264,128]{1,0:T(8,128)S(1)} %collective-permute-done.group, f32[3264,128]{1,0:T(8,128)S(1)} %get-tuple-element.26.field, ...), custom_call_target="tpu_custom_call", output_to_operand_aliasing={{3}: (3, {})} | custom-call | tf_op jit(solution)/shard_map/pallas_call | solution.py:68
  15.0 0.1 fusion
  15.1 2.6 %collective-permute-start.4 = (f32[12,16,512]{2,1,0:T(8,128)S(1)}, f32[12,16,512]{2,1,0:T(8,128)S(1)}, u32[]{:S(2)}, u32[]{:S(2)}) collective-permute-start(f32[12,16,512]{2,1,0:T(8,128)S(1)} %get-tuple-element.44), channel_id=1, source_target_pairs={{0,1},{1,0},{2,3},{3,2},{4,8},{5,9},{6,10},{7,11},{8,4},{9,5},{10,... | collective-permute-start | bytes 1179656 | tf_op jit(solution)/shard_map/ppermute | solution.py:451
  17.7 0.0 collective-permute-start.3
  17.7 3.5 %collective-permute-start.8 = (f32[96,128]{1,0:T(8,128)S(1)}, f32[96,128]{1,0:T(8,128)S(1)}, u32[]{:S(2)}, u32[]{:S(2)}) collective-permute-start(f32[96,128]{1,0:T(8,128)S(1)} %get-tuple-element.38), channel_id=1, source_target_pairs={{0,2},{1,3},{2,0},{3,1},{4,6},{5,7},{6,4},{7,5},{8,10},{9,11},{10,... | collective-permute-start | bytes 147464 | tf_op jit(solution)/shard_map/ppermute | solution.py:441
  21.2 0.2 collective-permute-start.9
  21.4 1.0 %collective-permute-start.7 = (f32[96,128]{1,0:T(8,128)S(1)}, f32[96,128]{1,0:T(8,128)S(1)}, u32[]{:S(2)}, u32[]{:S(2)}) collective-permute-start(f32[96,128]{1,0:T(8,128)S(1)} %get-tuple-element.37), channel_id=1, source_target_pairs={{0,1},{1,0},{2,3},{3,2},{4,5},{5,4},{6,7},{7,6},{8,9},{9,8},{10,11... | collective-permute-start | bytes 147464 | tf_op jit(solution)/shard_map/ppermute | solution.py:441
  22.4 2.1 %collective-permute-done.4.refs_3_ = f32[12,16,512]{2,1,0:T(8,128)S(1)} collective-permute-done((f32[12,16,512]{2,1,0:T(8,128)S(1)}, f32[12,16,512]{2,1,0:T(8,128)S(1)}, u32[]{:S(2)}, u32[]{:S(2)}) %collective-permute-start.4) | collective-permute-done | bytes 393248 | tf_op jit(solution)/shard_map/ppermute | solution.py:451
  24.5 0.0 collective-permute-done.3.refs_2_
  24.5 0.4 %shard_map.100 = (f32[24,16,512]{2,1,0:T(8,128)S(1)}, f32[96,128]{1,0:T(8,128)S(1)}) custom-call(f32[24,16,512]{2,1,0:T(8,128)S(1)} %get-tuple-element.31.refs_0_, f32[24,16,512]{2,1,0:T(8,128)S(1)} %get-tuple-element.32.refs_1_, f32[12,16,512]{2,1,0:T(8,128)S(1)} %collective-permute-done.3.refs_2_, f32[12,16,512]{2,1,0:T(8,128)S(1)} %collective-permute-done.4.refs_3_), custom_call_target="tpu_custom_call" | custom-call | tf_op jit(solution)/shard_map/pallas_call | solution.py:68
  24.9 2.2 %collective-permute-start.6 = (f32[48,128]{1,0:T(8,128)S(1)}, f32[48,128]{1,0:T(8,128)S(1)}, u32[]{:S(2)}, u32[]{:S(2)}) collective-permute-start(f32[48,128]{1,0:T(8,128)S(1)} %get-tuple-element.50), channel_id=1, source_target_pairs={{0,4},{1,2},{2,1},{3,7},{4,0},{5,6},{6,5},{7,3},{8,12},{9,10},{10,... | collective-permute-start | bytes 73736 | tf_op jit(solution)/shard_map/ppermute | solution.py:451
  27.2 0.6 %collective-permute-start.5 = (f32[48,128]{1,0:T(8,128)S(1)}, f32[48,128]{1,0:T(8,128)S(1)}, u32[]{:S(2)}, u32[]{:S(2)}) collective-permute-start(f32[48,128]{1,0:T(8,128)S(1)} %get-tuple-element.51), channel_id=1, source_target_pairs={{0,1},{1,0},{2,3},{3,2},{4,5},{5,4},{6,7},{7,6},{8,9},{9,8},{10,11... | collective-permute-start | bytes 73736 | tf_op jit(solution)/shard_map/ppermute | solution.py:441
  27.8 0.0 collective-permute-done.8.d2
  27.8 0.0 collective-permute-done.9.d3
  27.8 0.0 collective-permute-done.7.d1
  27.8 1.7 %shard_map.101 = (f32[384,128]{1,0:T(8,128)S(1)}, f32[24,16,512]{2,1,0:T(8,128)S(1)}) custom-call(s32[128]{0:T(128)S(1)} %get-tuple-element.35.block, f32[24,16,512]{2,1,0:T(8,128)S(1)} %get-tuple-element.33.field, f32[96,128]{1,0:T(8,128)S(1)} %get-tuple-element.36.d0, f32[96,128]{1,0:T(8,128)S(1)} %collective-permute-done.7.d1, ...), custom_call_target="tpu_custom_call" | custom-call | flops 1000000000 | tf_op jit(solution)/shard_map/pallas_call | solution.py:68
  29.5 0.0 collective-permute-done.6.got3
  29.5 1.5 %collective-permute-done.5.got1 = f32[48,128]{1,0:T(8,128)S(1)} collective-permute-done((f32[48,128]{1,0:T(8,128)S(1)}, f32[48,128]{1,0:T(8,128)S(1)}, u32[]{:S(2)}, u32[]{:S(2)}) %collective-permute-start.5) | collective-permute-done | bytes 24608 | tf_op jit(solution)/shard_map/ppermute | solution.py:441
  31.0 1.7 %shard_map.102 = (f32[384,128]{1,0:T(8,128)}, f32[24,16,512]{2,1,0:T(8,128)}) custom-call(f32[24,16,512]{2,1,0:T(8,128)S(1)} %get-tuple-element.33.field, f32[48,128]{1,0:T(8,128)S(1)} %collective-permute-done.5.got1, f32[48,128]{1,0:T(8,128)S(1)} %collective-permute-done.6.got3, f32[24,16,512]{2,1,0:T(8,128)S(1)} %get-tuple-element.40.done, ...), custom_call_target="tpu_custom_call" | custom-call | tf_op jit(solution)/shard_map/pallas_call | solution.py:68
  (2 shorter events, 0.0 us)
Async XLA Ops:
  3.4 7.2 %collective-permute-start.2 = (f32[264,128]{1,0:T(8,128)S(1)}, f32[264,128]{1,0:T(8,128)S(1)}, u32[]{:S(2)}, u32[]{:S(2)}) collective-permute-start(f32[264,128]{1,0:T(8,128)S(1)} %get-tuple-element.46), channel_id=1, source_target_pairs={{0,1},{1,0},{2,3},{3,2},{4,5},{5,4},{6,7},{7,6},{8,9},{9,8},{10,11... | collective-permute-start | bytes 405512 | tf_op jit(solution)/shard_map/ppermute | solution.py:441
  4.0 7.9 %collective-permute-start.1 = (f32[264,128]{1,0:T(8,128)S(1)}, f32[264,128]{1,0:T(8,128)S(1)}, u32[]{:S(2)}, u32[]{:S(2)}) collective-permute-start(f32[264,128]{1,0:T(8,128)S(1)} %get-tuple-element.47), channel_id=1, source_target_pairs={{0,3},{1,2},{2,1},{3,0},{4,7},{5,6},{6,5},{7,4},{8,11},{9,10},{10,... | collective-permute-start | bytes 405512 | tf_op jit(solution)/shard_map/ppermute | solution.py:441
  6.2 7.1 %collective-permute-start = (f32[264,128]{1,0:T(8,128)S(1)}, f32[264,128]{1,0:T(8,128)S(1)}, u32[]{:S(2)}, u32[]{:S(2)}) collective-permute-start(f32[264,128]{1,0:T(8,128)S(1)} %get-tuple-element.49), channel_id=1, source_target_pairs={{0,2},{1,3},{2,0},{3,1},{4,6},{5,7},{6,4},{7,5},{8,10},{9,11},{10,... | collective-permute-start | bytes 405512 | tf_op jit(solution)/shard_map/ppermute | solution.py:441
  15.1 9.4 %collective-permute-start.4 = (f32[12,16,512]{2,1,0:T(8,128)S(1)}, f32[12,16,512]{2,1,0:T(8,128)S(1)}, u32[]{:S(2)}, u32[]{:S(2)}) collective-permute-start(f32[12,16,512]{2,1,0:T(8,128)S(1)} %get-tuple-element.44), channel_id=1, source_target_pairs={{0,1},{1,0},{2,3},{3,2},{4,8},{5,9},{6,10},{7,11},{8,4},{9,5},{10,... | collective-permute-start | bytes 1179656 | tf_op jit(solution)/shard_map/ppermute | solution.py:451
  17.7 6.8 %collective-permute-start.3 = (f32[12,16,512]{2,1,0:T(8,128)S(1)}, f32[12,16,512]{2,1,0:T(8,128)S(1)}, u32[]{:S(2)}, u32[]{:S(2)}) collective-permute-start(f32[12,16,512]{2,1,0:T(8,128)S(1)} %get-tuple-element.45), channel_id=1, source_target_pairs={{0,4},{4,0},{8,12},{12,8},{16,20},{20,16},{24,28},{28,24},{32,36},... | collective-permute-start | bytes 1179656 | tf_op jit(solution)/shard_map/ppermute | solution.py:441
  17.7 10.1 %collective-permute-start.8 = (f32[96,128]{1,0:T(8,128)S(1)}, f32[96,128]{1,0:T(8,128)S(1)}, u32[]{:S(2)}, u32[]{:S(2)}) collective-permute-start(f32[96,128]{1,0:T(8,128)S(1)} %get-tuple-element.38), channel_id=1, source_target_pairs={{0,2},{1,3},{2,0},{3,1},{4,6},{5,7},{6,4},{7,5},{8,10},{9,11},{10,... | collective-permute-start | bytes 147464 | tf_op jit(solution)/shard_map/ppermute | solution.py:441
  21.2 6.6 %collective-permute-start.9 = (f32[96,128]{1,0:T(8,128)S(1)}, f32[96,128]{1,0:T(8,128)S(1)}, u32[]{:S(2)}, u32[]{:S(2)}) collective-permute-start(f32[96,128]{1,0:T(8,128)S(1)} %get-tuple-element.39), channel_id=1, source_target_pairs={{0,3},{1,2},{2,1},{3,0},{4,7},{5,6},{6,5},{7,4},{8,11},{9,10},{10,... | collective-permute-start | bytes 147464 | tf_op jit(solution)/shard_map/ppermute | solution.py:441
  21.4 6.4 %collective-permute-start.7 = (f32[96,128]{1,0:T(8,128)S(1)}, f32[96,128]{1,0:T(8,128)S(1)}, u32[]{:S(2)}, u32[]{:S(2)}) collective-permute-start(f32[96,128]{1,0:T(8,128)S(1)} %get-tuple-element.37), channel_id=1, source_target_pairs={{0,1},{1,0},{2,3},{3,2},{4,5},{5,4},{6,7},{7,6},{8,9},{9,8},{10,11... | collective-permute-start | bytes 147464 | tf_op jit(solution)/shard_map/ppermute | solution.py:441
  24.9 4.6 %collective-permute-start.6 = (f32[48,128]{1,0:T(8,128)S(1)}, f32[48,128]{1,0:T(8,128)S(1)}, u32[]{:S(2)}, u32[]{:S(2)}) collective-permute-start(f32[48,128]{1,0:T(8,128)S(1)} %get-tuple-element.50), channel_id=1, source_target_pairs={{0,4},{1,2},{2,1},{3,7},{4,0},{5,6},{6,5},{7,3},{8,12},{9,10},{10,... | collective-permute-start | bytes 73736 | tf_op jit(solution)/shard_map/ppermute | solution.py:451
  27.2 3.8 %collective-permute-start.5 = (f32[48,128]{1,0:T(8,128)S(1)}, f32[48,128]{1,0:T(8,128)S(1)}, u32[]{:S(2)}, u32[]{:S(2)}) collective-permute-start(f32[48,128]{1,0:T(8,128)S(1)} %get-tuple-element.51), channel_id=1, source_target_pairs={{0,1},{1,0},{2,3},{3,2},{4,5},{5,4},{6,7},{7,6},{8,9},{9,8},{10,11... | collective-permute-start | bytes 73736 | tf_op jit(solution)/shard_map/ppermute | solution.py:441
